TPU v7x, 256 devices: a whole 4x4x8 slice. The times are simulated.
256 devices in a mesh: dp: 2 (over y_lo), seq: 32 (over z, y_hi, core), chan: 4 (over x).
Axes of the slice: x: 4, y: 4 (y_hi: 2, y_lo: 2; y = y_hi * 2 + y_lo), z: 8, core: 2. Of those that a mesh axis runs over, the one named last changes fastest.
Arguments:
- layer_input: bfloat16 [2, 4096, 2560], P('dp', ('seq', 'chan')), may hold values from -24 to 24
- inner_weight: bfloat16 [2560, 2560], P(None, 'chan'), may hold values from -0.125 to 0.125
- mixer_weight: bfloat16 [2560, 256], replicated, may hold values from -0.01171875 to 0.01171875
- step_weight: bfloat16 [2560, 40], P(None, 'chan'), may hold values from -0.125 to 0.125
- conv_inner: float32 [4, 2560], P(None, 'chan'), may hold values from -3 to 3
- conv_mixer: float32 [4, 256], replicated, may hold values from -3 to 3
- step_bias: float32 [40], P('chan'), may hold values from -2 to 1
- decay_log: float32 [40], P('chan'), as said below
- skip_gain: float32 [40], P('chan'), may hold values from 0.5 to 1.5
- output_grad: bfloat16 [2, 4096, 2560], P('dp', 'seq', 'chan'), may hold values from -6 to 6
Outputs:
- input_grad: bfloat16 [2, 4096, 2560], P('dp', ('seq', 'chan'))
- inner_weight_grad: float32 [2560, 2560], P(('dp', 'seq'), 'chan')
- mixer_weight_grad: float32 [2560, 256], P(('dp', 'seq', 'chan'))
- step_weight_grad: float32 [2560, 40], P(('dp', 'seq'), 'chan')
Inputs may be any that keep to these rules, and one draw needn't show every extreme that they name: exp(decay_log) is at least 0.2 / 4096.
All inputs are finite; a program needn't handle non-finite values.
Results may differ from a plain program's by a relative error of at most 0.014.
Values may be sent and summed in bfloat16 or wider, within the bound.
No kernel may reach another device: no remote copies, remote signals or barrier semaphores. Data moves between devices by JAX's collectives and lax.ppermute only.
A program may use at most 128 MiB of HBM per device.

v0:
```python
import math

import jax
import jax.numpy as jnp
from jax import lax
from jax.sharding import Mesh
from jax.sharding import PartitionSpec as P

HDIM = 64
SEQ = ("seq_0", "seq_1", "seq_2")
DP_SEQ = ("dp", "seq_0", "seq_1", "seq_2")
SEQ_CHAN = ("seq_0", "seq_1", "seq_2", "chan")
DP_SEQ_CHAN = ("dp", "seq_0", "seq_1", "seq_2", "chan")


block_tokens = 256


def in_order(parts, dim):
    dims = list(parts.shape[1:])
    dims[dim] *= parts.shape[0]
    return jnp.moveaxis(parts, 0, dim).reshape(dims)


def from_everyone(value, axis):
    copies = jnp.broadcast_to(value, (lax.axis_size(axis), *value.shape))
    return lax.all_to_all(copies, axis, split_axis=0, concat_axis=0, tiled=True)


def collect(value, axis, dim):
    return in_order(from_everyone(value, axis), dim)


def from_behind(value, axis, steps):
    count = lax.axis_size(axis)
    first, last = (max(0, -steps), min(count, count - steps))
    return lax.ppermute(value, axis, [(source, source + steps) for source in range(first, last)])


def neutral_like(value, identity):
    return jax.tree.map(
        lambda part, zero: jnp.zeros_like(part) + jnp.asarray(zero, part.dtype), value, identity
    )


def entering(value, axes, combine, identity):
    before = start = neutral_like(value, identity)
    total = value
    for axis in reversed(axes):
        size, index = (lax.axis_size(axis), lax.axis_index(axis))
        pieces = jax.tree.map(
            lambda part, kind: lax.all_gather(part.astype(kind), axis),
            total,
            (jnp.bfloat16, jnp.bfloat16),
        )
        inside, total = (start, start)
        for k in range(size):
            passed = k < index
            total = combine(
                total, jax.tree.map(lambda part, own: part[k].astype(own.dtype), pieces, value)
            )
            inside = jax.tree.map(lambda new, old: jnp.where(passed, new, old), total, inside)
        before = combine(inside, before)
    return before


def entering_2(value, axes, combine, identity):
    before = start = neutral_like(value, identity)
    total = value
    for axis in reversed(axes):
        size, index = (lax.axis_size(axis), lax.axis_index(axis))
        pieces = jax.tree.map(lambda part: lax.all_gather(part, axis), total)
        inside, total = (start, start)
        for k in reversed(range(size)):
            passed = k > index
            total = combine(total, jax.tree.map(lambda part: part[k], pieces))
            inside = jax.tree.map(lambda new, old: jnp.where(passed, new, old), total, inside)
        before = combine(inside, before)
    return before


def cut_along(value, dim, size):
    before, after = (value.shape[:dim], value.shape[dim + 1 :])
    return jnp.moveaxis(value.reshape(*before, size, -1, *after), dim, 0)


def sent_and_summed(value, axis, dim):
    parts = cut_along(value, dim, lax.axis_size(axis))
    arrived = lax.all_to_all(parts, axis, split_axis=0, concat_axis=0, tiled=True)
    return arrived.astype(jnp.float32).sum(axis=0)


def over_copies(value, axis):
    return from_everyone(value, axis).astype(jnp.float32).sum(axis=0)


def side_by_side(arrays, axis, dim, along):
    widths = [a.shape[along] for a in arrays]
    both = jnp.concatenate(arrays, axis=along)
    result = sent_and_summed(both, axis, dim)
    return tuple(jnp.split(result, [sum(widths[:k]) for k in range(1, len(widths))], axis=along))


def conv_silu(inputs, history, kernel):
    length = inputs.shape[0]
    padded = jnp.concatenate([history, inputs], axis=0)
    summed = kernel[0][None, :] * padded[0:length]
    for offset in range(1, kernel.shape[0]):
        summed = summed + kernel[offset][None, :] * padded[offset : offset + length]
    return jax.nn.silu(summed)


def activations(
    inner_proj,
    mixer_proj,
    step_raw,
    inner_hist,
    mixer_hist,
    conv_inner,
    conv_mixer,
    step_bias,
    decay_log,
):
    length = inner_proj.shape[0]
    head_count = step_bias.shape[0]
    state_width = mixer_proj.shape[1] // 2
    inner_act = conv_silu(inner_proj, inner_hist, conv_inner).reshape(length, head_count, -1)
    mixer_act = conv_silu(mixer_proj, mixer_hist, conv_mixer)
    step_size = jax.nn.softplus(step_raw + step_bias[None, :])
    log_decay = -step_size * jnp.exp(decay_log)[None, :]
    return (inner_act, mixer_act[:, :state_width], mixer_act[:, state_width:], step_size, log_decay)


def spanned_scan(inner_act, input_mix, output_mix, step_size, log_decay, skip_gain, initial):
    length, head_count, head_dim = inner_act.shape
    block_len = min(block_tokens, length)
    blocks = length // block_len
    highest = lax.Precision.HIGHEST

    def to_blocks(values):
        return values.reshape((blocks, block_len) + values.shape[1:])

    def advance(carry_state, pieces):
        part_inner, part_input, part_output, part_step, part_decay = pieces
        cumulative = jnp.cumsum(part_decay, axis=0)
        scores = jnp.dot(part_output, part_input.T, precision=highest)
        causal = (jnp.arange(block_len)[:, None] >= jnp.arange(block_len)[None, :])[:, :, None]
        spread = cumulative[:, None, :] - cumulative[None, :, :]
        weights = jnp.where(causal, jnp.exp(jnp.where(causal, spread, 0.0)), 0.0)
        weights = weights * scores[:, :, None] * part_step[None, :, :]
        within = jnp.einsum("ijh,jhp->ihp", weights, part_inner, precision=highest)
        carried = jnp.exp(cumulative)[:, :, None] * jnp.einsum(
            "in,hpn->ihp", part_output, carry_state, precision=highest
        )
        result = within + carried + skip_gain[None, :, None] * part_inner
        tail_weight = jnp.exp(cumulative[-1][None, :] - cumulative) * part_step
        update_term = jnp.einsum(
            "jh,jhp,jn->hpn", tail_weight, part_inner, part_input, precision=highest
        )
        carry_state = jnp.exp(cumulative[-1])[:, None, None] * carry_state + update_term
        return (carry_state, result)

    final, results = lax.scan(
        advance,
        initial,
        (
            to_blocks(inner_act),
            to_blocks(input_mix),
            to_blocks(output_mix),
            to_blocks(step_size),
            to_blocks(log_decay),
        ),
    )
    return (results.reshape(length, head_count, head_dim), final)


def combine_carry(earlier, latter):
    return (earlier[0] + latter[0], jnp.exp(latter[0])[:, None, None] * earlier[1] + latter[1])


def contract_rows(left_rows, right_rows):
    return lax.dot_general(
        left_rows, right_rows, (((0,), (0,)), ((), ())), preferred_element_type=jnp.float32
    )


def project_back(gradient, weight):
    return lax.dot_general(
        gradient, weight, (((1,), (1,)), ((), ())), preferred_element_type=jnp.float32
    )


def split_pair(values):
    leading = values.astype(jnp.bfloat16)
    residue = (values - leading.astype(jnp.float32)).astype(jnp.bfloat16)
    return (leading, residue)


def body(
    layer_input,
    inner_weight,
    mixer_weight,
    step_weight,
    conv_inner,
    conv_mixer,
    step_bias,
    decay_log,
    skip_gain,
    output_grad,
):
    gathered = collect(layer_input[0], "chan", 0)
    seg_len = gathered.shape[0]
    chan_count = lax.axis_size("chan")
    history_len = conv_inner.shape[0] - 1
    highest = lax.Precision.HIGHEST
    inner_proj = jnp.dot(gathered, inner_weight, preferred_element_type=jnp.float32).astype(
        jnp.bfloat16
    )
    mixer_proj = jnp.dot(gathered, mixer_weight, preferred_element_type=jnp.float32).astype(
        jnp.bfloat16
    )
    step_raw = jnp.dot(gathered, step_weight, preferred_element_type=jnp.float32)
    last_rows = from_behind(gathered[seg_len - history_len :], SEQ, 1)
    inner_hist = jnp.dot(last_rows, inner_weight, preferred_element_type=jnp.float32).astype(
        jnp.bfloat16
    )
    mixer_hist = jnp.dot(last_rows, mixer_weight, preferred_element_type=jnp.float32).astype(
        jnp.bfloat16
    )
    inner_wide = lax.optimization_barrier(inner_proj).astype(jnp.float32)
    mixer_wide = lax.optimization_barrier(mixer_proj).astype(jnp.float32)
    inner_prev = lax.optimization_barrier(inner_hist).astype(jnp.float32)
    mixer_prev = lax.optimization_barrier(mixer_hist).astype(jnp.float32)

    def local_acts(inner_in, mixer_in, step_in, inner_before, mixer_before):
        return activations(
            inner_in,
            mixer_in,
            step_in,
            inner_before,
            mixer_before,
            conv_inner,
            conv_mixer,
            step_bias,
            decay_log,
        )

    acts, pull_acts = jax.vjp(local_acts, inner_wide, mixer_wide, step_raw, inner_prev, mixer_prev)
    inner_act, input_mix, output_mix, step_size, log_decay = acts
    head_count = step_bias.shape[0]
    upstream = output_grad[0].astype(jnp.float32).reshape(seg_len, head_count, HDIM)
    cumulative = jnp.cumsum(log_decay, axis=0)
    segment_decay = cumulative[-1]
    local_state = jnp.einsum(
        "th,thp,tn->hpn",
        jnp.exp(segment_decay[None, :] - cumulative) * step_size,
        inner_act,
        input_mix,
        precision=highest,
    )
    local_grad = jnp.einsum(
        "th,thp,tn->hpn", jnp.exp(cumulative), upstream, output_mix, precision=highest
    )
    neutral = (jnp.zeros_like(segment_decay), jnp.zeros_like(local_state))
    start_state = entering((segment_decay, local_state), SEQ, combine_carry, neutral)[1]
    end_grad = entering_2((segment_decay, local_grad), SEQ, combine_carry, neutral)[1]

    def scan_local(inner_in, input_in, output_in, step_in, decay_in):
        return spanned_scan(
            inner_in, input_in, output_in, step_in, decay_in, skip_gain, start_state
        )

    unused, pull_scan = jax.vjp(scan_local, inner_act, input_mix, output_mix, step_size, log_decay)
    act_grads = pull_scan((upstream, end_grad))
    inner_local, mixer_local, step_local, inner_back, mixer_back = pull_acts(act_grads)
    inner_next, mixer_next = from_behind((inner_back, mixer_back), SEQ, -1)
    keep_rows = seg_len - history_len
    inner_total = jnp.concatenate(
        [inner_local[:keep_rows], inner_local[keep_rows:] + inner_next], axis=0
    )
    grad_mixer = jnp.concatenate(
        [mixer_local[:keep_rows], mixer_local[keep_rows:] + mixer_next], axis=0
    )
    grad_inner = inner_total.astype(jnp.bfloat16)
    grad_step = step_local.astype(jnp.bfloat16)
    mixer_lead, mixer_rest = split_pair(grad_mixer)
    summed = project_back(grad_inner, inner_weight) + project_back(grad_step, step_weight)
    input_grad = sent_and_summed(
        (
            summed + project_back(mixer_lead, mixer_weight) + project_back(mixer_rest, mixer_weight)
        ).astype(jnp.bfloat16),
        "chan",
        0,
    ).astype(jnp.bfloat16)
    token_count = seg_len * lax.axis_size(SEQ) * lax.axis_size("dp")
    norm_factor = 1.0 / math.sqrt(token_count)
    inner_term = contract_rows(gathered, grad_inner) * norm_factor
    step_term = contract_rows(gathered, grad_step) * norm_factor
    mixer_total = over_copies(grad_mixer.astype(jnp.bfloat16), "chan").astype(jnp.float32)
    group_count = lax.axis_size("dp") * lax.axis_size(SEQ)
    row_share = gathered.shape[1] // (group_count * chan_count)
    grouped = gathered.reshape(seg_len, group_count, chan_count, row_share)
    picked = lax.dynamic_index_in_dim(grouped, lax.axis_index("chan"), 2, keepdims=False).reshape(
        seg_len, group_count * row_share
    )
    total_lead, total_rest = split_pair(mixer_total)
    mixer_term = (
        contract_rows(picked, total_lead) + contract_rows(picked, total_rest)
    ) * norm_factor
    inner_weight_grad, step_weight_grad, mixer_weight_grad = (
        *side_by_side(
            (inner_term.astype(jnp.bfloat16), step_term.astype(jnp.bfloat16)), DP_SEQ, 0, 1
        ),
        sent_and_summed(mixer_term.astype(jnp.bfloat16), DP_SEQ, 0),
    )
    return (input_grad[None], inner_weight_grad, mixer_weight_grad, step_weight_grad)


def solution(mesh):
    split = Mesh(
        mesh.devices.reshape(mesh.shape["dp"], 8, 2, 2, mesh.shape["chan"]),
        ("dp", "seq_0", "seq_1", "seq_2", "chan"),
    )
    placed = (
        P("dp", SEQ_CHAN, None),
        P(None, "chan"),
        P(),
        P(None, "chan"),
        P(None, "chan"),
        P(),
        P("chan"),
        P("chan"),
        P("chan"),
        P("dp", SEQ, "chan"),
    )
    return jax.shard_map(
        body,
        mesh=split,
        in_specs=placed,
        out_specs=(
            P("dp", SEQ_CHAN, None),
            P(DP_SEQ, "chan"),
            P(DP_SEQ_CHAN, None),
            P(DP_SEQ, "chan"),
        ),
        check_vma=False,
    )
```

profile of v0, /device:TPU:4, one launch (start us, length us, event | category | flops | bytes accessed | tf_op | source)
XLA Modules:
  0.0 371.9 jit_solution(11411503904716051082)
XLA Ops:
  9.2 6.4 %all-to-all-start = ((bf16[4,32,2560]{2,1,0:T(8,128)(2,1)}), bf16[4,32,2560]{2,1,0:T(8,128)(2,1)}, u32[]{:S(2)}, u32[]{:S(2)}) async-start(bf16[4,32,2560]{2,1,0:T(8,128)(2,1)} %broadcast_in_dim.167), calls=%async_computation | async-start | bytes 1310720 | tf_op jit(solution)/shard_map/all_to_all | solution.py:27
  26.1 5.5 %all-gather.2 = f32[2,1,10]{2,1,0:T(1,128)S(1)} all-gather(f32[1,1,10]{2,1,0:T(1,128)S(1)} %bitcast.380), channel_id=1, replica_groups=mesh['dp'=2,'seq_0'=8,'seq_1'=2,'seq_2'=2,'chan'=4] {'seq_2'}, dimensions={0}, use_global_device_ids=true | all-gather | bytes 120 | tf_op jit(solution)/shard_map/all_gather | solution.py:72
  32.2 5.7 %all-gather.3 = f32[2,1,10]{2,1,0:T(1,128)S(1)} all-gather(f32[1,1,10]{2,1,0:T(1,128)S(1)} %get-tuple-element.429), channel_id=1, replica_groups=mesh['dp'=2,'seq_0'=8,'seq_1'=2,'seq_2'=2,'chan'=4] {'seq_1'}, dimensions={0}, use_global_device_ids=true | all-gather | bytes 120 | tf_op jit(solution)/shard_map/all_gather | solution.py:72
  46.1 11.9 %all_gather.56 = f32[2,10,64,128]{3,2,1,0:T(8,128)S(1)} all-gather(f32[1,10,64,128]{3,2,1,0:T(8,128)S(1)} %bitcast_add_fusion.10), channel_id=1, replica_groups=mesh['dp'=2,'seq_0'=8,'seq_1'=2,'seq_2'=2,'chan'=4] {'seq_1'}, dimensions={0}, use_global_device_ids=true | all-gather | bytes 983040 | tf_op jit(solution)/shard_map/all_gather | solution.py:72
  64.5 5.8 %all-gather.6 = bf16[2,1,10]{2,1,0:T(2,128)(2,1)} all-gather(bf16[1,1,10]{2,1,0:T(2,128)(2,1)S(1)} %get-tuple-element.424), channel_id=1, replica_groups=mesh['dp'=2,'seq_0'=8,'seq_1'=2,'seq_2'=2,'chan'=4] {'seq_1'}, dimensions={0}, use_global_device_ids=true | all-gather | bytes 60 | tf_op jit(solution)/shard_map/all_gather | solution.py:52
  74.6 4.2 %copy.101 = bf16[4,32,2560]{1,0,2:T(4,128)(2,1)} copy(bf16[4,32,2560]{2,1,0:T(8,128)(2,1)} %all-to-all-done) | data formatting | bytes 1310720 | tf_op jit(solution)/shard_map/all_to_all | solution.py:27
  78.7 4.5 %reshape_reshape.4 = bf16[128,64,4,10]{0,3,2,1:T(8,128)(2,1)} reshape(bf16[4,32,2560]{1,0,2:T(4,128)(2,1)} %copy.101) | data formatting | bytes 1310720 | tf_op jit(solution)/shard_map/reshape;reshape | solution.py:302
  87.7 19.7 %all-gather.7 = bf16[8,1,10]{2,1,0:T(2,128)(2,1)} all-gather(bf16[1,1,10]{2,1,0:T(2,128)(2,1)S(1)} %get-tuple-element.421), channel_id=1, replica_groups=mesh['dp'=2,'seq_0'=8,'seq_1'=2,'seq_2'=2,'chan'=4] {'seq_0'}, dimensions={0}, use_global_device_ids=true | all-gather | bytes 180 | tf_op jit(solution)/shard_map/all_gather | solution.py:52
  108.7 13.3 %all-gather.4 = f32[8,1,10]{2,1,0:T(1,128)S(1)} all-gather(f32[1,1,10]{2,1,0:T(1,128)S(1)} %get-tuple-element.386), channel_id=1, replica_groups=mesh['dp'=2,'seq_0'=8,'seq_1'=2,'seq_2'=2,'chan'=4] {'seq_0'}, dimensions={0}, use_global_device_ids=true | all-gather | bytes 360 | tf_op jit(solution)/shard_map/all_gather | solution.py:72
  145.4 8.4 %all_gather.63 = bf16[2,10,64,128]{3,2,1,0:T(8,128)(2,1)S(1)} all-gather(bf16[1,10,64,128]{3,2,1,0:T(8,128)(2,1)S(1)} %fusion.108), channel_id=1, replica_groups=mesh['dp'=2,'seq_0'=8,'seq_1'=2,'seq_2'=2,'chan'=4] {'seq_1'}, dimensions={0}, use_global_device_ids=true | all-gather | bytes 491520 | tf_op jit(solution)/shard_map/all_gather | solution.py:52
  170.7 3.8 %fusion = bf16[2560,640]{0,1:T(8,128)(2,1)} fusion(bf16[128,2560]{1,0:T(8,128)(2,1)} %bitcast.2, bf16[3,640]{1,0:T(4,128)(2,1)S(1)} %fusion.180, bf16[125,640]{1,0:T(8,128)(2,1)S(1)} %slice.667), kind=kOutput, calls=%fused_computation.2 | convolution fusion | flops 423034880 | bytes 4096000 | tf_op jit(solution)/shard_map/dot_general | solution.py:182
  174.5 19.3 %all-gather.13.cloned.1.call-done = bf16[8,10,64,128]{3,2,1,0:T(8,128)(2,1)} async-done(((bf16[1,10,64,128]{3,2,1,0:T(8,128)(2,1)}), bf16[8,10,64,128]{3,2,1,0:T(8,128)(2,1)}) %all-gather.13.cloned.1.call-update) | async-done | bytes 1310736 | tf_op jit(solution)/shard_map/all_gather | solution.py:52
  194.2 3.2 convolution_bitcast_fusion.3
  198.5 3.5 fusion.86
  211.0 3.2 convolution_add_fusion.2
  215.6 4.8 %all-to-all-start.3 = ((bf16[4,128,256]{2,1,0:T(8,128)(2,1)}), bf16[4,128,256]{2,1,0:T(8,128)(2,1)}, u32[]{:S(2)}, u32[]{:S(2)}) async-start(bf16[4,128,256]{2,1,0:T(8,128)(2,1)} %broadcast_in_dim.171), calls=%async_computation.3 | async-start | bytes 524288 | tf_op jit(solution)/shard_map/all_to_all | solution.py:27
  225.5 7.1 %all-to-all-start.1 = ((bf16[4,32,2560]{2,1,0:T(8,128)(2,1)}), bf16[4,32,2560]{2,1,0:T(8,128)(2,1)}, u32[]{:S(2)}, u32[]{:S(2)}) async-start(bf16[4,32,2560]{2,1,0:T(8,128)(2,1)} %bitcast.370), calls=%async_computation.1 | async-start | bytes 1310720 | tf_op jit(solution)/shard_map/all_to_all | solution.py:89
  236.7 4.4 %all-to-all-done.1 = bf16[4,32,2560]{2,1,0:T(8,128)(2,1)} async-done(((bf16[4,32,2560]{2,1,0:T(8,128)(2,1)}), bf16[4,32,2560]{2,1,0:T(8,128)(2,1)}, u32[]{:S(2)}, u32[]{:S(2)}) %all-to-all-start.1) | async-done | bytes 655392 | tf_op jit(solution)/shard_map/all_to_all | solution.py:89
  241.1 7.6 %all-to-all-start.4 = ((bf16[64,10,256]{2,1,0:T(8,128)(2,1)}), bf16[64,10,256]{2,1,0:T(8,128)(2,1)}, u32[]{:S(2)}, u32[]{:S(2)}) async-start(bf16[64,10,256]{2,1,0:T(8,128)(2,1)} %reshape.626), calls=%async_computation.4 | async-start | bytes 1048576 | tf_op jit(solution)/shard_map/all_to_all | solution.py:89
  250.0 3.9 %pad_maximum_fusion = bf16[2560,650]{0,1:T(8,128)(2,1)} fusion(bf16[2560,10]{0,1:T(8,128)(2,1)S(1)} %fusion.3, bf16[2560,640]{0,1:T(8,128)(2,1)} %fusion), kind=kLoop, calls=%fused_computation.8 | loop fusion | flops 6656000 | bytes 6656000 | tf_op jit(solution)/shard_map/concatenate | solution.py:99
  253.9 5.9 %copy.100 = bf16[2560,650]{1,0:T(8,128)(2,1)} copy(bf16[2560,650]{0,1:T(8,128)(2,1)} %pad_maximum_fusion) | data formatting | bytes 6656000 | tf_op jit(solution)/shard_map/concatenate | solution.py:99
  259.8 6.1 %all-to-all-done.4 = bf16[64,10,256]{2,1,0:T(8,128)(2,1)} async-done(((bf16[64,10,256]{2,1,0:T(8,128)(2,1)}), bf16[64,10,256]{2,1,0:T(8,128)(2,1)}, u32[]{:S(2)}, u32[]{:S(2)}) %all-to-all-start.4) | async-done | bytes 327712 | tf_op jit(solution)/shard_map/all_to_all | solution.py:89
  265.9 6.5 %all-to-all-start.2 = ((bf16[64,40,650]{2,1,0:T(8,128)(2,1)}), bf16[64,40,650]{2,1,0:T(8,128)(2,1)}, u32[]{:S(2)}, u32[]{:S(2)}) async-start(bf16[64,40,650]{2,1,0:T(8,128)(2,1)} %bitcast.365), calls=%async_computation.2 | async-start | bytes 7864320 | tf_op jit(solution)/shard_map/all_to_all | solution.py:89
  276.1 84.9 %all-to-all-done.2 = bf16[64,40,650]{2,1,0:T(8,128)(2,1)} async-done(((bf16[64,40,650]{2,1,0:T(8,128)(2,1)}), bf16[64,40,650]{2,1,0:T(8,128)(2,1)}, u32[]{:S(2)}, u32[]{:S(2)}) %all-to-all-start.2) | async-done | bytes 3328032 | tf_op jit(solution)/shard_map/all_to_all | solution.py:89
  (282 shorter events, 106.9 us)
Async XLA Ops:
  7.2 64.9 %copy-start = (bf16[2560,640]{1,0:T(8,128)(2,1)S(1)}, bf16[2560,640]{1,0:T(8,128)(2,1)}, u32[]{:S(2)}) copy-start(bf16[2560,640]{1,0:T(8,128)(2,1)} %param.11) | copy-start | bytes 9830404
  9.2 12.8 %all-to-all-start = ((bf16[4,32,2560]{2,1,0:T(8,128)(2,1)}), bf16[4,32,2560]{2,1,0:T(8,128)(2,1)}, u32[]{:S(2)}, u32[]{:S(2)}) async-start(bf16[4,32,2560]{2,1,0:T(8,128)(2,1)} %broadcast_in_dim.167), calls=%async_computation | async-start | bytes 1310720 | tf_op jit(solution)/shard_map/all_to_all | solution.py:27
  15.5 111.7 %all-gather.11.cloned.1.call-start = ((), (), s32[]{:S(2)}) async-start(), calls=%async_computation.5 | async-start | bytes 2949120 | tf_op jit(solution)/shard_map/all_gather | solution.py:72
  16.2 9.3 %copy-start.84 = (f32[10]{0:T(128)}, f32[10]{0:T(128)S(1)}, u32[]{:S(2)}) copy-start(f32[10]{0:T(128)S(1)} %exp.409) | copy-start | bytes 124
  22.8 17.8 %collective-permute-start = (bf16[3,2560]{1,0:T(4,128)(2,1)S(1)}, bf16[3,2560]{1,0:T(4,128)(2,1)S(1)}, u32[]{:S(2)}, u32[]{:S(2)}) collective-permute-start(bf16[3,2560]{1,0:T(4,128)(2,1)S(1)} %slice.320), channel_id=1, source_target_pairs={{0,4},{4,8},{8,12},{12,16},{16,20},{20,24},{24,28},{28,32},{32,36}... | collective-permute-start | bytes 46088 | tf_op jit(solution)/shard_map/ppermute | solution.py:37
  25.9 16.4 %copy-start.43 = (f32[1,256]{1,0:T(1,128)S(1)}, f32[1,256]{1,0:T(1,128)}, u32[]{:S(2)}) copy-start(f32[1,256]{1,0:T(1,128)} %get-tuple-element.417) | copy-start | bytes 3076
  25.9 16.4 %copy-start.44 = (f32[1,256]{1,0:T(1,128)S(1)}, f32[1,256]{1,0:T(1,128)}, u32[]{:S(2)}) copy-start(f32[1,256]{1,0:T(1,128)} %get-tuple-element.418) | copy-start | bytes 3076
  25.9 16.4 %copy-start.45 = (f32[1,256]{1,0:T(1,128)S(1)}, f32[1,256]{1,0:T(1,128)}, u32[]{:S(2)}) copy-start(f32[1,256]{1,0:T(1,128)} %get-tuple-element.420) | copy-start | bytes 3076
  25.9 16.4 %copy-start.46 = (f32[1,256]{1,0:T(1,128)S(1)}, f32[1,256]{1,0:T(1,128)}, u32[]{:S(2)}) copy-start(f32[1,256]{1,0:T(1,128)} %get-tuple-element.419) | copy-start | bytes 3076
  25.9 16.5 %copy-start.18 = (bf16[1,128,640]{1,2,0:T(8,128)(2,1)S(1)}, bf16[1,128,640]{1,2,0:T(8,128)(2,1)}, u32[]{:S(2)}) copy-start(bf16[1,128,640]{1,2,0:T(8,128)(2,1)} %copy.88) | copy-start | bytes 491524
  26.1 16.1 %copy-start.41 = (f32[10]{0:T(128)}, f32[10]{0:T(128)S(1)}, u32[]{:S(2)}) copy-start(f32[10]{0:T(128)S(1)} %slice_reduce_fusion) | copy-start | bytes 124
  32.2 10.0 %copy-start.83 = (f32[1,1,10]{2,1,0:T(1,128)}, f32[1,1,10]{2,1,0:T(1,128)S(1)}, u32[]{:S(2)}) copy-start(f32[1,1,10]{2,1,0:T(1,128)S(1)} %get-tuple-element.429) | copy-start | bytes 124
  32.2 12.9 %copy-start.47 = (f32[10]{0:T(128)}, f32[10]{0:T(128)S(1)}, u32[]{:S(2)}) copy-start(f32[10]{0:T(128)S(1)} %get-tuple-element.430) | copy-start | bytes 124
  32.2 12.9 %copy-start.49 = (f32[10]{0:T(128)}, f32[10]{0:T(128)S(1)}, u32[]{:S(2)}) copy-start(f32[10]{0:T(128)S(1)} %get-tuple-element.431) | copy-start | bytes 124
  40.5 17.5 %copy-start.51 = (f32[10]{0:T(128)}, f32[10]{0:T(128)S(1)}, u32[]{:S(2)}) copy-start(f32[10]{0:T(128)S(1)} %get-tuple-element.427) | copy-start | bytes 124
  40.5 17.4 %copy-start.53 = (f32[10]{0:T(128)}, f32[10]{0:T(128)S(1)}, u32[]{:S(2)}) copy-start(f32[10]{0:T(128)S(1)} %get-tuple-element.428) | copy-start | bytes 124
  59.7 134.1 %all-gather.13.cloned.1.call-start = ((), (), s32[]{:S(2)}) async-start(), calls=%async_computation.6 | async-start | bytes 1474560 | tf_op jit(solution)/shard_map/all_gather | solution.py:52
  160.6 8.7 %collective-permute-start.1 = (f32[3,640]{1,0:T(4,128)}, f32[3,640]{1,0:T(4,128)}, u32[]{:S(2)}, u32[]{:S(2)}) collective-permute-start(f32[3,640]{1,0:T(4,128)} %pad_add_fusion.2), channel_id=1, source_target_pairs={{4,0},{8,4},{12,8},{16,12},{20,16},{24,20},{28,24},{32,28},{36,32}... | collective-permute-start | bytes 23048 | tf_op jit(solution)/shard_map/ppermute | solution.py:37
  207.6 6.6 %collective-permute-start.2 = (f32[3,256]{1,0:T(4,128)S(1)}, f32[3,256]{1,0:T(4,128)S(1)}, u32[]{:S(2)}, u32[]{:S(2)}) collective-permute-start(f32[3,256]{1,0:T(4,128)S(1)} %pad_add_fusion.3), channel_id=1, source_target_pairs={{4,0},{8,4},{12,8},{16,12},{20,16},{24,20},{28,24},{32,28},{36,32}... | collective-permute-start | bytes 9224 | tf_op jit(solution)/shard_map/ppermute | solution.py:37
  215.6 9.9 %all-to-all-start.3 = ((bf16[4,128,256]{2,1,0:T(8,128)(2,1)}), bf16[4,128,256]{2,1,0:T(8,128)(2,1)}, u32[]{:S(2)}, u32[]{:S(2)}) async-start(bf16[4,128,256]{2,1,0:T(8,128)(2,1)} %broadcast_in_dim.171), calls=%async_computation.3 | async-start | bytes 524288 | tf_op jit(solution)/shard_map/all_to_all | solution.py:27
  222.8 10.8 %copy-start.23 = (bf16[128,640]{0,1:T(8,128)(2,1)S(1)}, bf16[128,640]{0,1:T(8,128)(2,1)}, u32[]{:S(2)}) copy-start(bf16[128,640]{0,1:T(8,128)(2,1)} %reshape.625) | copy-start | bytes 491524
  225.5 15.6 %all-to-all-start.1 = ((bf16[4,32,2560]{2,1,0:T(8,128)(2,1)}), bf16[4,32,2560]{2,1,0:T(8,128)(2,1)}, u32[]{:S(2)}, u32[]{:S(2)}) async-start(bf16[4,32,2560]{2,1,0:T(8,128)(2,1)} %bitcast.370), calls=%async_computation.1 | async-start | bytes 1310720 | tf_op jit(solution)/shard_map/all_to_all | solution.py:89
  241.1 24.8 %all-to-all-start.4 = ((bf16[64,10,256]{2,1,0:T(8,128)(2,1)}), bf16[64,10,256]{2,1,0:T(8,128)(2,1)}, u32[]{:S(2)}, u32[]{:S(2)}) async-start(bf16[64,10,256]{2,1,0:T(8,128)(2,1)} %reshape.626), calls=%async_computation.4 | async-start | bytes 1048576 | tf_op jit(solution)/shard_map/all_to_all | solution.py:89
  265.9 95.1 %all-to-all-start.2 = ((bf16[64,40,650]{2,1,0:T(8,128)(2,1)}), bf16[64,40,650]{2,1,0:T(8,128)(2,1)}, u32[]{:S(2)}, u32[]{:S(2)}) async-start(bf16[64,40,650]{2,1,0:T(8,128)(2,1)} %bitcast.365), calls=%async_computation.2 | async-start | bytes 7864320 | tf_op jit(solution)/shard_map/all_to_all | solution.py:89
  (73 other events, 286.7 us)
Sparse Core Ops, SparseCore 0:
  59.9 44.0 all-gather.10
  156.2 37.6 all-gather.12
where the time goes:
time: 377 us; the launch traced here: 372 us
  waiting for transfers between devices  119 us (32%)
  blocking collectives  76.6 us (20%)
  local copies, waits for them, and re-layouts  45.2 us (12%)
  other arithmetic  44.3 us (12%)
  starting transfers between devices  36.5 us (10%)
  matrix products  35.2 us (9%)
  between operations  15.3 us (4%)
    all_to_all x3, waiting for transfers between devices, sent_and_summed(): lax.all_to_all(parts, axis, split_axis=0, concat_axis=0, tiled=True)  95.5 us
    all_gather x5, blocking collectives, entering_2(): pieces = jax.tree.map(lambda part: lax.all_gather(part, axis), total)  38.7 us
    all_gather x5, blocking collectives, entering(): lax.all_gather(part.astype(kind), axis)  37.8 us
    all_to_all x3, starting transfers between devices, sent_and_summed(): lax.all_to_all(parts, axis, split_axis=0, concat_axis=0, tiled=True)  21.2 us
    all_gather x1, waiting for transfers between devices, entering(): lax.all_gather(part.astype(kind), axis)  19.3 us
    all_to_all x2, starting transfers between devices, from_everyone(): return lax.all_to_all(copies, axis, split_axis=0, concat_axis=0, tiled=True)  11.2 us
    unnamed x176, local copies, waits for them, and re-layouts  8.45 us
    dot_general x4, matrix products, project_back(): lax.dot_general(gradient, weight, (((1,), (1,)), ((), ())), preferred_ele...  8.19 us
  transfers between devices with their start and end apart: 10, of which 6 were waited for; matrix products, arithmetic and copies ran while one was open for 21% of the time, Pallas kernels for 0%

commit v1 on v0

v1 whole, which is shorter than its diff:
```python
import math

import jax
import jax.numpy as jnp
from jax import lax
from jax.experimental import pallas as pl
from jax.experimental.pallas import tpu as pltpu
from jax.sharding import Mesh
from jax.sharding import PartitionSpec as P

HDIM = 64
SEQ = ("seq_0", "seq_1", "seq_2")
PAIRS = ("seq_0", "seq_1")
ROW4 = ("dp", "seq_1")
ROW8 = ("dp", "seq_1", "seq_2")
DP_SEQ = ("dp", "seq_0", "seq_1", "seq_2")
SEQ_CHAN = ("seq_0", "seq_1", "seq_2", "chan")
DP_SEQ_CHAN = ("dp", "seq_0", "seq_1", "seq_2", "chan")

F32 = jnp.float32
BF16 = jnp.bfloat16
HIGHEST = lax.Precision.HIGHEST
HALO = 16


def dot(a, b, ca=1, cb=0, precision=None):
    return lax.dot_general(
        a, b, (((ca,), (cb,)), ((), ())), precision=precision, preferred_element_type=F32
    )


def vmem(count):
    return [pl.BlockSpec(memory_space=pltpu.VMEM) for _ in range(count)]


def smem():
    return pl.BlockSpec(memory_space=pltpu.SMEM)


def call(kernel, outs, ins, scratch=(), flops=0, name=None):
    specs = [
        smem() if (a.dtype == jnp.int32) else pl.BlockSpec(memory_space=pltpu.VMEM) for a in ins
    ]
    return pl.pallas_call(
        kernel,
        out_shape=[jax.ShapeDtypeStruct(s, d) for s, d in outs],
        in_specs=specs,
        out_specs=vmem(len(outs)),
        scratch_shapes=list(scratch),
        compiler_params=pltpu.CompilerParams(vmem_limit_bytes=48 << 20),
        cost_estimate=pl.CostEstimate(flops=flops, transcendentals=0, bytes_accessed=1 << 20),
        name=name,
    )(*ins)


def heads_to_lanes(heads, width):
    head = lax.broadcasted_iota(jnp.int32, (heads, width), 0)
    lane = lax.broadcasted_iota(jnp.int32, (heads, width), 1)
    return (lane // HDIM == head).astype(F32)


def lanes_to_heads(width, heads):
    lane = lax.broadcasted_iota(jnp.int32, (width, heads), 0)
    head = lax.broadcasted_iota(jnp.int32, (width, heads), 1)
    return (lane // HDIM == head).astype(F32)


def lower(size):
    row = lax.broadcasted_iota(jnp.int32, (size, size), 0)
    col = lax.broadcasted_iota(jnp.int32, (size, size), 1)
    return row >= col


def silu_and_slope(v):
    gate = 1.0 / (1.0 + jnp.exp(-v))
    return v * gate, gate * (1.0 + v * (1.0 - gate))


def project_kernel(
    who, x0, x1, x2, x3, h0, h1, h2, h3, w_in, w_mix, w_step, k_in, k_mix, bias, decay_log, g,
    x_out, act, slope, mix, mix_slope, small, gate_out, rows, zs_out, zg_out, keep, send,
    xs, pi, pm,
):
    chan, core = who[0], who[1]
    part = x0.shape[0]
    tokens = 4 * part
    width = act.shape[1]
    heads = bias.shape[1]
    for k, x in enumerate((x0, x1, x2, x3)):
        slot = lax.rem(chan + 4 - k, 4)
        xs[pl.ds(pl.multiple_of(HALO + slot * part, 16), part), :] = x[...]
    xs[0:HALO, :] = h0[...] + h1[...] + h2[...] + h3[...]
    everything = xs[...]
    x_out[...] = xs[HALO:, :]
    pi[...] = dot(everything, w_in[...]).astype(BF16).astype(F32)
    pm[...] = dot(everything, w_mix[...]).astype(BF16).astype(F32)
    raw = dot(xs[HALO:, :], w_step[...]) + bias[...]

    def convolved(source, kernel):
        total = kernel[3:4, :] * source[HALO:, :]
        for k in range(3):
            start = HALO - 3 + k
            total = total + kernel[k : k + 1, :] * source[start : start + tokens, :]
        return total

    inner_act, inner_slope = silu_and_slope(convolved(pi, k_in))
    act[...] = inner_act
    slope[...] = inner_slope
    mix_act, mixer_slope = silu_and_slope(convolved(pm, k_mix))
    mix[...] = mix_act
    mix_slope[...] = mixer_slope

    step = jnp.maximum(raw, 0.0) + jnp.log1p(jnp.exp(-jnp.abs(raw)))
    gate_out[...] = 1.0 / (1.0 + jnp.exp(-raw))
    decay = -step * jnp.exp(decay_log[...])
    low = lower(tokens).astype(F32)
    total = dot(low, decay, precision=HIGHEST)
    rows[0] = dot(decay, low, 0, 1, precision=HIGHEST)
    row = lax.broadcasted_iota(jnp.int32, (tokens, tokens), 0)
    col = lax.broadcasted_iota(jnp.int32, (tokens, tokens), 1)
    rows[1] = dot(step, (row == col).astype(F32), 0, 0, precision=HIGHEST)
    last = total[tokens - 1 : tokens, :]
    ea = jnp.exp(total)
    tail = jnp.exp(last - total)
    small[0] = step
    small[1] = total
    small[2] = ea
    small[3] = tail
    spread = heads_to_lanes(heads, width)
    wide = dot(jnp.concatenate([tail * step, ea], axis=0), spread, precision=HIGHEST)
    zs = (wide[:tokens] * inner_act).astype(BF16)
    zg = (wide[tokens:] * g[...].astype(F32)).astype(BF16)
    zs_out[...] = zs
    zg_out[...] = zg
    state_width = mix_act.shape[1] // 2
    into = mix_act[:, :state_width].astype(BF16)
    out_of = mix_act[:, state_width:].astype(BF16)
    state = dot(into, zs, 0, 0)
    grad = dot(out_of, zg, 0, 0)
    lead = last.astype(BF16).astype(F32)
    rest = (last - lead).astype(BF16).astype(F32)
    pad = jnp.zeros((14, heads), F32)
    marks = dot(jnp.concatenate([lead, rest, pad], axis=0), spread, precision=HIGHEST).astype(BF16)
    keep[state_width:, :] = marks.astype(F32)
    send[state_width:, :] = marks

    @pl.when(core == 0)
    def _():
        keep[:state_width, :] = state
        send[:state_width, :] = grad.astype(BF16)

    @pl.when(core != 0)
    def _():
        keep[:state_width, :] = grad
        send[:state_width, :] = state.astype(BF16)


def pair_kernel(keep, recv, out):
    n = keep.shape[0] - 16
    width = keep.shape[1]
    own = keep[n : n + 1, :] + keep[n + 1 : n + 2, :]
    other = recv[n:, :].astype(F32)
    theirs = other[0:1, :] + other[1:2, :]
    pair = jnp.exp(theirs) * keep[:n, :] + recv[:n, :].astype(F32)
    total = own + theirs
    lead = total.astype(BF16)
    rest = (total - lead.astype(F32)).astype(BF16)
    groups = out.shape[0]
    per = n // groups
    for k in range(groups):
        out[k, :per, :] = pair[k * per : (k + 1) * per, :].astype(BF16)
        out[k, per : per + 1, :] = lead
        out[k, per + 1 : per + 2, :] = rest


def chain_kernel(who, recv, out):
    forward = who[1] == 0
    groups = recv.shape[0]
    per = out.shape[1]

    def step(k, state):
        slot = jnp.where(forward, k, groups - 1 - k)
        piece = recv[slot].astype(F32)
        out[slot] = state.astype(BF16)
        factor = jnp.exp(piece[per : per + 1, :] + piece[per + 1 : per + 2, :])
        return factor * state + piece[:per, :]

    lax.fori_loop(0, groups, step, jnp.zeros(out.shape[1:], F32), unroll=True)


def back_kernel(keep, before, own, send):
    n = keep.shape[0] - 16
    factor = jnp.exp(keep[n : n + 1, :] + keep[n + 1 : n + 2, :])
    groups, per = before.shape[0], before.shape[1]
    for k in range(groups):
        piece = before[k].astype(F32)
        rows = slice(k * per, (k + 1) * per)
        own[rows, :] = before[k]
        send[rows, :] = (factor * piece + keep[rows, :]).astype(BF16)


def within_kernel(act, mix, g, small, rows, u_out, row_out, col_out, mix_out):
    tokens, width = act.shape
    heads = small.shape[2]
    state_width = mix.shape[1] // 2
    into = mix[:, :state_width].astype(BF16)
    out_of = mix[:, state_width:].astype(BF16)
    scores = dot(out_of, into, 1, 1)
    causal = lower(tokens)
    lane = lax.broadcasted_iota(jnp.int32, (tokens, 128), 1)
    pull = jnp.zeros((tokens, tokens), F32)
    for pair in range(width // 128):
        lanes = slice(pair * 128, (pair + 1) * 128)
        x_pair = act[:, lanes].astype(BF16)
        g_pair = g[:, lanes]
        u_pair = jnp.zeros((tokens, 128), F32)
        for half in range(2):
            h = 2 * pair + half
            g_head = jnp.where(lane // HDIM == half, g_pair, jnp.zeros_like(g_pair))
            inner = dot(g_head, x_pair, 1, 1)
            spread = small[1, :, h : h + 1] - rows[0, h : h + 1, :]
            decay = jnp.where(causal, jnp.exp(jnp.where(causal, spread, 0.0)), 0.0)
            weights = decay * scores
            u_pair = u_pair + dot(weights.astype(BF16), g_head, 0, 0)
            step_row = rows[1, h : h + 1, :]
            both = weights * inner
            col_out[h : h + 1, :] = jnp.sum(both, axis=0, keepdims=True)
            row_out[:, h : h + 1] = jnp.sum(both * step_row, axis=1, keepdims=True)
            pull = pull + decay * inner * step_row
        u_out[:, lanes] = u_pair
    pull = pull.astype(BF16)
    mix_out[:, :state_width] = dot(pull, out_of, 0, 0)
    mix_out[:, state_width:] = dot(pull, into)


def back_through_kernel(
    who, own, other, act, slope, mix, mix_slope, g, small, gate, zs, zg, u, row_in, col_in, mix_in,
    decay_log, skip, pre_out, head_out, step_out, s0, gt,
):
    tokens, width = act.shape
    heads = small.shape[2]
    state_width = mix.shape[1] // 2

    @pl.when(who[1] == 0)
    def _():
        s0[...] = own[...]
        gt[...] = other[...]

    @pl.when(who[1] != 0)
    def _():
        s0[...] = other[...]
        gt[...] = own[...]

    into = mix[:, :state_width].astype(BF16)
    out_of = mix[:, state_width:].astype(BF16)
    gb = dot(into, gt[...])
    sc = dot(out_of, s0[...])
    step = small[0]
    spread = heads_to_lanes(heads, width)
    gather = lanes_to_heads(width, heads)
    skip_rows = jnp.broadcast_to(skip[...], (8, heads))
    wide = dot(
        jnp.concatenate([step, small[3], skip_rows], axis=0), spread, precision=HIGHEST
    )
    tail_gb = wide[tokens : 2 * tokens] * gb
    x = act[...]
    upstream = g[...].astype(F32)
    d_act = wide[:tokens] * (u[...] + tail_gb) + wide[2 * tokens : 2 * tokens + 1] * upstream
    d_pre = d_act * slope[...]
    pre_out[:, :width] = d_pre
    cross = jnp.sum(gt[...].astype(F32) * s0[...].astype(F32), axis=0, keepdims=True)
    sums = dot(
        jnp.concatenate(
            [x * tail_gb, zg[...].astype(F32) * sc, jnp.broadcast_to(cross, (8, width))], axis=0
        ),
        gather,
        precision=HIGHEST,
    )
    e_part = sums[:tokens]
    c_part = sums[tokens : 2 * tokens]
    f_part = sums[2 * tokens : 2 * tokens + 1]
    row = lax.broadcasted_iota(jnp.int32, (tokens, tokens), 0)
    col = lax.broadcasted_iota(jnp.int32, (tokens, tokens), 1)
    col_part = dot((row == col).astype(F32), col_in[...], 1, 1, precision=HIGHEST)
    e_step = step * e_part
    d_total = row_in[...] + c_part - step * col_part - e_step
    at_end = jnp.sum(e_step, axis=0, keepdims=True) + small[2, tokens - 1 : tokens, :] * f_part
    d_decay = dot((row <= col).astype(F32), d_total, precision=HIGHEST) + at_end
    d_step = col_part + e_part - d_decay * jnp.exp(decay_log[...])
    step_out[...] = jnp.zeros_like(step_out)
    step_out[:, :heads] = (d_step * gate[...]).astype(BF16)
    d_into = mix_in[:, :state_width] + dot(zs[...], gt[...], 1, 1)
    d_out_of = mix_in[:, state_width:] + dot(zg[...], s0[...], 1, 1)
    pre_out[:, width : width + state_width] = d_into * mix_slope[:, :state_width]
    pre_out[:, width + state_width :] = d_out_of * mix_slope[:, state_width:]
    head_out[...] = pre_out[0:8, :]


def conv_back_kernel(pre, ahead, step, k_in, k_mix, out, padded):
    tokens = pre.shape[0]
    width = k_in.shape[1]
    padded[:tokens, :] = pre[...]
    padded[tokens:, :] = ahead[...]

    def convolved(lanes, kernel):
        total = kernel[3:4, :] * padded[:tokens, lanes]
        for k in range(3):
            total = total + kernel[k : k + 1, :] * padded[3 - k : 3 - k + tokens, lanes]
        return total

    edge = pre.shape[1]
    out[:, :width] = convolved(slice(0, width), k_in).astype(BF16)
    out[:, width:edge] = convolved(slice(width, edge), k_mix).astype(BF16)
    out[:, edge:] = step[...]


def input_grad_kernel(grads, w_in, w_mix, w_step, out):
    width = w_in.shape[1]
    edge = width + w_mix.shape[1]
    heads = w_step.shape[1]
    total = dot(grads[:, :width], w_in[...], 1, 1)
    total = total + dot(grads[:, width:edge], w_mix[...], 1, 1)
    total = total + dot(grads[:, edge : edge + heads], w_step[...], 1, 1)
    out[...] = total.astype(BF16).reshape(out.shape)


def weight_grad_kernel(who, xt, g0, g1, g2, g3, s0, s1, s2, s3, inner_out, mix_out):
    core, place = who[1], who[2]
    total = None
    for k, (same, swapped) in enumerate(((g0, s0), (g1, s1), (g2, s2), (g3, s3))):
        source = 2 * lax.rem(place + 4 - k, 4)
        total_k = dot(xt[source + core], same[...]) + dot(xt[source + 1 - core], swapped[...])
        total = total_k if total is None else total + total_k
    width = 640
    rows = inner_out.shape[1]
    for k in range(inner_out.shape[0]):
        part = slice(k * rows, (k + 1) * rows)
        inner_out[k, :, :width] = total[part, :width].astype(BF16)
        inner_out[k, :, width:] = total[part, width + 256 :].astype(BF16)
    mix_out[...] = total[:, width : width + 256].astype(BF16)


def a2a(value, axis):
    return lax.all_to_all(value, axis, split_axis=0, concat_axis=0, tiled=True)


def turned(value, axis, steps):
    count = lax.axis_size(axis)
    return lax.ppermute(value, axis, [(k, (k + steps) % count) for k in range(count)])


def body(
    layer_input,
    inner_weight,
    mixer_weight,
    step_weight,
    conv_inner,
    conv_mixer,
    step_bias,
    decay_log,
    skip_gain,
    output_grad,
):
    own = layer_input[0]
    part, model = own.shape
    chans = lax.axis_size("chan")
    tokens = part * chans
    width = inner_weight.shape[1]
    heads = step_bias.shape[0]
    mixed = mixer_weight.shape[1]
    state_width = mixed // 2
    g = output_grad[0]
    who = jnp.stack(
        [lax.axis_index("chan"), lax.axis_index("seq_2"), lax.axis_index(ROW4)]
    ).astype(jnp.int32)
    bias = step_bias[None]
    rate = decay_log[None]
    skip = skip_gain[None]

    arrived = [own] + [turned(own, "chan", k) for k in (1, 2, 3)]
    tail_rows = own[part - HALO :]
    seq_count = lax.axis_size(SEQ)
    halos = [
        lax.ppermute(
            tail_rows,
            SEQ_CHAN,
            [(s * chans + chans - 1, (s + 1) * chans + c) for s in range(seq_count - 1)],
        )
        for c in range(chans)
    ]
    t, c = tokens, width
    x, act, slope, mix, mix_slope, small, gate, rows, zs, zg, keep, send = call(
        project_kernel,
        [
            ((t, model), BF16),
            ((t, c), F32),
            ((t, c), F32),
            ((t, mixed), F32),
            ((t, mixed), F32),
            ((4, t, heads), F32),
            ((t, heads), F32),
            ((2, heads, t), F32),
            ((t, c), BF16),
            ((t, c), BF16),
            ((state_width + 16, c), F32),
            ((state_width + 16, c), BF16),
        ],
        [
            who, *arrived, *halos, inner_weight, mixer_weight, step_weight, conv_inner,
            conv_mixer, bias, rate, g,
        ],
        [
            pltpu.VMEM((t + HALO, model), BF16),
            pltpu.VMEM((t + HALO, c), F32),
            pltpu.VMEM((t + HALO, mixed), F32),
        ],
        flops=700_000_000,
        name="project",
    )
    got = turned(send, "seq_2", 1)
    groups = lax.axis_size(PAIRS)
    per = state_width // groups
    (pairs,) = call(pair_kernel, [((groups, 2 * per, c), BF16)], [keep, got], name="pair")
    pairs = a2a(pairs, PAIRS)

    u, row_part, col_part, mix_part = call(
        within_kernel,
        [((t, c), F32), ((t, heads), F32), ((heads, t), F32), ((t, mixed), F32)],
        [act, mix, g, small, rows],
        flops=700_000_000,
        name="within",
    )
    group8 = lax.axis_size(ROW8)
    share = model // (lax.axis_size(DP_SEQ))
    lines = lax.axis_size("seq_0")
    xt = x.T.reshape(lax.axis_size("dp"), lines, group8 // 2, share, t)
    xt = jnp.swapaxes(xt, 1, 2).reshape(group8, lines * share, t)
    xt = a2a(xt, ROW8)

    (befores,) = call(chain_kernel, [((groups, per, c), BF16)], [who, pairs], name="chain")
    befores = a2a(befores, PAIRS)
    mine, others = call(
        back_kernel, [((state_width, c), BF16)] * 2, [keep, befores], name="back"
    )
    others = turned(others, "seq_2", 1)
    pre, head, step_grad = call(
        back_through_kernel,
        [((t, c + mixed), F32), ((8, c + mixed), F32), ((t, 128), BF16)],
        [
            who, mine, others, act, slope, mix, mix_slope, g, small, gate, zs, zg, u, row_part,
            col_part, mix_part, rate, skip,
        ],
        [pltpu.VMEM((state_width, c), BF16), pltpu.VMEM((state_width, c), BF16)],
        flops=500_000_000,
        name="through",
    )
    ahead = lax.ppermute(head, SEQ, [(k + 1, k) for k in range(seq_count - 1)])
    (grads,) = call(
        conv_back_kernel,
        [((t, c + mixed + 128), BF16)],
        [pre, ahead, step_grad, conv_inner, conv_mixer],
        [pltpu.VMEM((t + 8, c + mixed), F32)],
        name="conv_back",
    )
    same = [grads] + [turned(grads, ROW4, k) for k in (1, 2, 3)]
    swapped = [turned(v, "seq_2", 1) for v in same]
    (partial,) = call(
        input_grad_kernel,
        [((chans, part, model), BF16)],
        [grads, inner_weight, mixer_weight, step_weight],
        flops=500_000_000,
        name="input_grad",
    )
    input_grad = a2a(partial, "chan").astype(F32).sum(axis=0).astype(BF16)
    inner_terms, mixer_terms = call(
        weight_grad_kernel,
        [((lines, share, c + 128), BF16), ((lines * share, mixed), BF16)],
        [who, xt, *same, *swapped],
        flops=700_000_000,
        name="weight_grad",
    )
    norm = 1.0 / math.sqrt(tokens * seq_count * lax.axis_size("dp"))
    mixer_terms = a2a(mixer_terms.reshape(lines * chans, share // chans, mixed), ("seq_0", "chan"))
    inner_terms = a2a(inner_terms, "seq_0")
    summed = inner_terms.astype(F32).sum(axis=0) * norm
    mixer_weight_grad = mixer_terms.astype(F32).sum(axis=0) * norm
    return (
        input_grad[None],
        summed[:, :c],
        mixer_weight_grad,
        summed[:, c : c + heads],
    )


def solution(mesh):
    split = Mesh(
        mesh.devices.reshape(mesh.shape["dp"], 8, 2, 2, mesh.shape["chan"]),
        ("dp", "seq_0", "seq_1", "seq_2", "chan"),
    )
    placed = (
        P("dp", SEQ_CHAN, None),
        P(None, "chan"),
        P(),
        P(None, "chan"),
        P(None, "chan"),
        P(),
        P("chan"),
        P("chan"),
        P("chan"),
        P("dp", SEQ, "chan"),
    )
    return jax.shard_map(
        body,
        mesh=split,
        in_specs=placed,
        out_specs=(
            P("dp", SEQ_CHAN, None),
            P(DP_SEQ, "chan"),
            P(DP_SEQ_CHAN, None),
            P(DP_SEQ, "chan"),
        ),
        check_vma=False,
    )
```

time: 377 us -> 161 us (0.43)
  waiting for transfers between devices: 119 us -> 34.4 us
  other arithmetic: 44.3 us -> 1.61 us
  matrix products: 35.2 us -> 0 us
  blocking collectives: 76.6 us -> 47.5 us
  local copies, waits for them, and re-layouts: 45.2 us -> 18 us
  Pallas kernels: 0 us -> 16 us
  between operations: 15.3 us -> 0.92 us
  starting transfers between devices: 36.5 us -> 41.1 us
    all_gather x10 -> x0, blocking collectives: 76.6 us -> none  [the longest x5 38.7 us: entering_2(): pieces = jax.tree.map(lambda part: lax.all_gather(part, axis), total)]
    all_to_all x5 -> x4, waiting for transfers between devices: 99.5 us -> 24.8 us  [a2a(): return lax.all_to_all(value, axis, split_axis=0, concat_axis=0, tiled=True)]
    all_to_all x0 -> x2, blocking collectives: none -> 47.5 us  [a2a(): return lax.all_to_all(value, axis, split_axis=0, concat_axis=0, tiled=True)]
    dot_general x24 -> x0, matrix products: 35.2 us -> none  [the longest x4 8.19 us: project_back(): lax.dot_general(gradient, weight, (((1,), (1,)), ((), ())), preferred_ele...]
    all_gather x2 -> x0, waiting for transfers between devices: 19.3 us -> none  [the longest x1 19.3 us: entering(): lax.all_gather(part.astype(kind), axis)]
    pallas_call x0 -> x9, Pallas kernels: none -> 16 us  [call(): pl.pallas_call(kernel, out_shape=[jax.ShapeDtypeStruct(s, d) for s, d in...]
    ppermute x3 -> x17, starting transfers between devices: 4.04 us -> 20 us  [the longest x12 16 us: turned(): lax.ppermute(value, axis, [(k, (k + steps) % count) for k in range(count)])]
    all_to_all x5 -> x4, starting transfers between devices: 32.4 us -> 21.2 us  [a2a(): return lax.all_to_all(value, axis, split_axis=0, concat_axis=0, tiled=True)]
  transfers between devices with their start and end apart: 10 -> 21, of which waited for: 6 -> 10; matrix products, arithmetic and copies ran while one was open for 21% -> 3% of each run, Pallas kernels for 0% -> 6%
where the time goes in v1:
time: 161 us; the launch traced here: 160 us
  blocking collectives  47.5 us (30%)
  starting transfers between devices  41.1 us (26%)
  waiting for transfers between devices  34.4 us (21%)
  local copies, waits for them, and re-layouts  18 us (11%)
  Pallas kernels  16 us (10%)
  other arithmetic  1.61 us (1%)
    all_to_all x2, blocking collectives, a2a(): return lax.all_to_all(value, axis, split_axis=0, concat_axis=0, tiled=True)  47.5 us
    all_to_all x4, waiting for transfers between devices, a2a(): return lax.all_to_all(value, axis, split_axis=0, concat_axis=0, tiled=True)  24.8 us
    all_to_all x4, starting transfers between devices, a2a(): return lax.all_to_all(value, axis, split_axis=0, concat_axis=0, tiled=True)  21.2 us
    ppermute x12, starting transfers between devices, turned(): lax.ppermute(value, axis, [(k, (k + steps) % count) for k in range(count)])  16 us
    pallas_call x9, Pallas kernels, call(): pl.pallas_call(kernel, out_shape=[jax.ShapeDtypeStruct(s, d) for s, d in...  16 us
    unnamed x54, local copies, waits for them, and re-layouts  15.1 us
    ppermute x12, waiting for transfers between devices, turned(): lax.ppermute(value, axis, [(k, (k + steps) % count) for k in range(count)])  7.83 us
  transfers between devices with their start and end apart: 21, of which 10 were waited for; matrix products, arithmetic and copies ran while one was open for 3% of the time, Pallas kernels for 6%

profile of v1, /device:TPU:4, one launch (start us, length us, event | category | flops | bytes accessed | tf_op | source)
XLA Modules:
  0.0 159.5 jit_solution(3161368656750434841)
XLA Ops:
  3.5 4.4 %collective-permute-start.1 = (bf16[32,2560]{1,0:T(8,128)(2,1)}, bf16[32,2560]{1,0:T(8,128)(2,1)S(1)}, u32[]{:S(2)}, u32[]{:S(2)}) collective-permute-start(bf16[32,2560]{1,0:T(8,128)(2,1)} %bitcast.21), channel_id=1, source_target_pairs={{0,2},{1,3},{2,0},{3,1},{4,6},{5,7},{6,4},{7,5},{8,10},{9,11},{10,... | collective-permute-start | bytes 491528 | tf_op jit(solution)/shard_map/ppermute | solution.py:349
  7.9 1.2 copy.23.w_step
  11.4 4.3 %collective-permute-done.x1 = bf16[32,2560]{1,0:T(8,128)(2,1)S(1)} collective-permute-done((bf16[32,2560]{1,0:T(8,128)(2,1)}, bf16[32,2560]{1,0:T(8,128)(2,1)S(1)}, u32[]{:S(2)}, u32[]{:S(2)}) %collective-permute-start) | collective-permute-done | bytes 163872 | tf_op jit(solution)/shard_map/ppermute | solution.py:349
  15.7 1.3 copy-done.1
  21.6 4.5 %project.1 = (bf16[128,2560]{1,0:T(8,128)(2,1)S(1)}, f32[128,640]{1,0:T(8,128)S(1)}, f32[128,640]{1,0:T(8,128)S(1)}, f32[128,256]{1,0:T(8,128)S(1)}, f32[128,256...) custom-call(s32[3]{0:T(128)S(1)} %pad_add_fusion.who, ...), custom_call_target="tpu_custom_call" | custom-call | flops 700000000 | bytes 1048576 | tf_op jit(solution)/shard_map/project/pallas_call | solution.py:44
  26.8 1.1 collective-permute-start.7
  29.1 26.4 %all_to_all.30.recv = bf16[16,16,640]{2,1,0:T(8,128)(2,1)S(1)} all-to-all(bf16[16,16,640]{2,1,0:T(8,128)(2,1)S(1)} %pair.1), channel_id=1, replica_groups=mesh['dp'=2,'seq_0'=8,'seq_1'=2,'seq_2'=2,'chan'=4] {'seq_0','seq_1'}, dimensions={0} | all-to-all | bytes 655360 | tf_op jit(solution)/shard_map/all_to_all | solution.py:344
  55.5 1.3 chain.1
  56.9 3.5 %all-to-all-start.1 = ((bf16[16,8,640]{2,1,0:T(8,128)(2,1)}), bf16[16,8,640]{2,1,0:T(8,128)(2,1)S(1)}, u32[]{:S(2)}, u32[]{:S(2)}) async-start(bf16[16,8,640]{2,1,0:T(8,128)(2,1)} %chain.1), calls=%async_computation.1 | async-start | bytes 327680 | tf_op jit(solution)/shard_map/all_to_all | solution.py:344
  61.6 10.3 %all-to-all-done.1.before = bf16[16,8,640]{2,1,0:T(8,128)(2,1)S(1)} async-done(((bf16[16,8,640]{2,1,0:T(8,128)(2,1)}), bf16[16,8,640]{2,1,0:T(8,128)(2,1)S(1)}, u32[]{:S(2)}, u32[]{:S(2)}) %all-to-all-start.1) | async-done | bytes 163872 | tf_op jit(solution)/shard_map/all_to_all | solution.py:344
  72.0 3.7 %all-to-all-start.3 = ((bf16[8,320,128]{2,1,0:T(8,128)(2,1)}), bf16[8,320,128]{2,1,0:T(8,128)(2,1)S(1)}, u32[]{:S(2)}, u32[]{:S(2)}) async-start(bf16[8,320,128]{2,1,0:T(8,128)(2,1)} %bitcast.28), calls=%async_computation.3 | async-start | bytes 1310720 | tf_op jit(solution)/shard_map/all_to_all | solution.py:344
  76.2 1.2 copy-done.7
  83.3 3.1 %through.1 = (f32[128,896]{1,0:T(8,128)S(1)}, f32[8,896]{1,0:T(8,128)S(1)}, bf16[128,128]{1,0:T(8,128)(2,1)S(1)}) custom-call(s32[3]{0:T(128)S(1)} %pad_add_fusion.who, bf16[128,640]{1,0:T(8,128)(2,1)S(1)} %get-tuple-element.29.own, bf16[128,640]{1,0:T(8,128)(2,1)S(1)} %collective-permute-done.8.other, f32[128,640]{1,0:T(8,128)S(1)} %get-tuple-element.31.act, ...), custom_call_target="tpu_custom_call" | custom-call | flops 500000000 | bytes 1048576 | tf_op jit(solution)/shard_map/through/pallas_call | solution.py:44
  86.4 1.3 collective-permute-start.9
  87.7 1.8 %collective-permute-done.9.ahead = f32[8,896]{1,0:T(8,128)S(1)} collective-permute-done((f32[8,896]{1,0:T(8,128)S(1)}, f32[8,896]{1,0:T(8,128)S(1)}, u32[]{:S(2)}, u32[]{:S(2)}) %collective-permute-start.9) | collective-permute-done | bytes 28704 | tf_op jit(solution)/shard_map/ppermute | solution.py:457
  90.5 4.8 %collective-permute-start.12 = (bf16[128,1024]{1,0:T(8,128)(2,1)S(1)}, bf16[128,1024]{1,0:T(8,128)(2,1)S(1)}, u32[]{:S(2)}, u32[]{:S(2)}) collective-permute-start(bf16[128,1024]{1,0:T(8,128)(2,1)S(1)} %conv_back.1.grads.g0), channel_id=1, source_target_pairs={{0,136},{8,0},{128,8},{136,128},{1,137},{9,1},{129,9},{137,129},{2... | collective-permute-start | bytes 786440 | tf_op jit(solution)/shard_map/ppermute | solution.py:349
  95.3 1.7 %collective-permute-start.10 = (bf16[128,1024]{1,0:T(8,128)(2,1)S(1)}, bf16[128,1024]{1,0:T(8,128)(2,1)S(1)}, u32[]{:S(2)}, u32[]{:S(2)}) collective-permute-start(bf16[128,1024]{1,0:T(8,128)(2,1)S(1)} %conv_back.1.grads.g0), channel_id=1, source_target_pairs={{0,8},{8,128},{128,136},{136,0},{1,9},{9,129},{129,137},{137,1},{2... | collective-permute-start | bytes 786440 | tf_op jit(solution)/shard_map/ppermute | solution.py:349
  97.0 2.6 %input_grad.1 = bf16[4,32,2560]{2,1,0:T(8,128)(2,1)} custom-call(bf16[128,1024]{1,0:T(8,128)(2,1)S(1)} %conv_back.1.grads.g0, bf16[2560,640]{1,0:T(8,128)(2,1)S(1)} %copy-done, bf16[2560,256]{1,0:T(8,128)(2,1)S(1)} %copy-done.2, bf16[2560,10]{1,0:T(8,128)(2,1)S(1)} %copy.23.w_step), custom_call_target="tpu_custom_call" | custom-call | flops 500000000 | bytes 1048576 | tf_op jit(solution)/shard_map/input_grad/pallas_call | solution.py:44
  99.6 10.5 %all-to-all-start.2 = ((bf16[4,32,2560]{2,1,0:T(8,128)(2,1)}), bf16[4,32,2560]{2,1,0:T(8,128)(2,1)S(1)}, u32[]{:S(2)}, u32[]{:S(2)}) async-start(bf16[4,32,2560]{2,1,0:T(8,128)(2,1)} %input_grad.1), calls=%async_computation.2 | async-start | bytes 1310720 | tf_op jit(solution)/shard_map/all_to_all | solution.py:344
  110.1 2.3 %collective-permute-start.13 = (bf16[128,1024]{1,0:T(8,128)(2,1)S(1)}, bf16[128,1024]{1,0:T(8,128)(2,1)S(1)}, u32[]{:S(2)}, u32[]{:S(2)}) collective-permute-start(bf16[128,1024]{1,0:T(8,128)(2,1)S(1)} %conv_back.1.grads.g0), channel_id=1, source_target_pairs={{0,4},{4,0},{1,5},{5,1},{2,6},{6,2},{3,7},{7,3},{8,12},{12,8},{9,1... | collective-permute-start | bytes 786440 | tf_op jit(solution)/shard_map/ppermute | solution.py:349
  114.7 2.8 %weight_grad.1 = (bf16[8,40,768]{2,1,0:T(8,128)(2,1)}, bf16[320,256]{1,0:T(8,128)(2,1)S(1)}) custom-call(s32[3]{0:T(128)S(1)} %pad_add_fusion.who, bf16[8,320,128]{2,1,0:T(8,128)(2,1)S(1)} %all-to-all-done.3.xt, bf16[128,1024]{1,0:T(8,128)(2,1)S(1)} %conv_back.1.grads.g0, bf16[128,1024]{1,0:T(8,128)(2,1)S(1)} %collective-permute-done.10.g1, ...), custom_call_target="tpu_custom_call" | custom-call | flops 700000000 | bytes 1048576 | tf_op jit(solution)/shard_map/weight_grad/pallas_call | solution.py:44
  117.6 21.1 %all_to_all.31 = bf16[32,10,256]{2,1,0:T(8,128)(2,1)S(1)} all-to-all(bf16[32,10,256]{2,1,0:T(8,128)(2,1)S(1)} %reshape.20), channel_id=1, replica_groups=mesh['dp'=2,'seq_0'=8,'seq_1'=2,'seq_2'=2,'chan'=4] {'seq_0','chan'}, dimensions={0} | all-to-all | bytes 327680 | tf_op jit(solution)/shard_map/all_to_all | solution.py:344
  138.6 3.5 %all-to-all-start.4 = ((bf16[8,40,768]{2,1,0:T(8,128)(2,1)}), bf16[8,40,768]{2,1,0:T(8,128)(2,1)S(1)}, u32[]{:S(2)}, u32[]{:S(2)}) async-start(bf16[8,40,768]{2,1,0:T(8,128)(2,1)} %get-tuple-element.48), calls=%async_computation.4 | async-start | bytes 983040 | tf_op jit(solution)/shard_map/all_to_all | solution.py:344
  143.6 14.5 %all-to-all-done.4 = bf16[8,40,768]{2,1,0:T(8,128)(2,1)S(1)} async-done(((bf16[8,40,768]{2,1,0:T(8,128)(2,1)}), bf16[8,40,768]{2,1,0:T(8,128)(2,1)S(1)}, u32[]{:S(2)}, u32[]{:S(2)}) %all-to-all-start.4) | async-done | bytes 491552 | tf_op jit(solution)/shard_map/all_to_all | solution.py:344
  (95 shorter events, 25.3 us)
Async XLA Ops:
  1.5 7.6 %collective-permute-start.6 = (bf16[16,2560]{1,0:T(8,128)(2,1)S(1)}, bf16[16,2560]{1,0:T(8,128)(2,1)S(1)}, u32[]{:S(2)}, u32[]{:S(2)}) collective-permute-start(bf16[16,2560]{1,0:T(8,128)(2,1)S(1)} %slice_bitcast_fusion), channel_id=1, source_target_pairs={{3,7},{7,11},{11,15},{15,19},{19,23},{23,27},{27,31},{31,35},{35,3... | collective-permute-start | bytes 245768 | tf_op jit(solution)/shard_map/ppermute | solution.py:384
  2.2 7.7 %collective-permute-start.5 = (bf16[16,2560]{1,0:T(8,128)(2,1)S(1)}, bf16[16,2560]{1,0:T(8,128)(2,1)S(1)}, u32[]{:S(2)}, u32[]{:S(2)}) collective-permute-start(bf16[16,2560]{1,0:T(8,128)(2,1)S(1)} %slice_bitcast_fusion), channel_id=1, source_target_pairs={{3,6},{7,10},{11,14},{15,18},{19,22},{23,26},{27,30},{31,34},{35,3... | collective-permute-start | bytes 245768 | tf_op jit(solution)/shard_map/ppermute | solution.py:384
  2.9 7.8 %collective-permute-start.2 = (bf16[32,2560]{1,0:T(8,128)(2,1)}, bf16[32,2560]{1,0:T(8,128)(2,1)S(1)}, u32[]{:S(2)}, u32[]{:S(2)}) collective-permute-start(bf16[32,2560]{1,0:T(8,128)(2,1)} %bitcast.20), channel_id=1, source_target_pairs={{0,3},{1,0},{2,1},{3,2},{4,7},{5,4},{6,5},{7,6},{8,11},{9,8},{10,9... | collective-permute-start | bytes 491528 | tf_op jit(solution)/shard_map/ppermute | solution.py:349
  3.5 8.0 %collective-permute-start.1 = (bf16[32,2560]{1,0:T(8,128)(2,1)}, bf16[32,2560]{1,0:T(8,128)(2,1)S(1)}, u32[]{:S(2)}, u32[]{:S(2)}) collective-permute-start(bf16[32,2560]{1,0:T(8,128)(2,1)} %bitcast.21), channel_id=1, source_target_pairs={{0,2},{1,3},{2,0},{3,1},{4,6},{5,7},{6,4},{7,5},{8,10},{9,11},{10,... | collective-permute-start | bytes 491528 | tf_op jit(solution)/shard_map/ppermute | solution.py:349
  7.9 7.8 %collective-permute-start = (bf16[32,2560]{1,0:T(8,128)(2,1)}, bf16[32,2560]{1,0:T(8,128)(2,1)S(1)}, u32[]{:S(2)}, u32[]{:S(2)}) collective-permute-start(bf16[32,2560]{1,0:T(8,128)(2,1)} %bitcast.22), channel_id=1, source_target_pairs={{0,1},{1,2},{2,3},{3,0},{4,5},{5,6},{6,7},{7,4},{8,9},{9,10},{10,1... | collective-permute-start | bytes 491528 | tf_op jit(solution)/shard_map/ppermute | solution.py:349
  9.2 1.4 collective-permute-start.4
  9.9 0.8 collective-permute-start.3
  26.8 28.8 %copy-start.6 = (f32[4,128,10]{2,1,0:T(8,128)}, f32[4,128,10]{2,1,0:T(8,128)S(1)}, u32[]{:S(2)}) copy-start(f32[4,128,10]{2,1,0:T(8,128)S(1)} %get-tuple-element.35.small) | copy-start | bytes 61444
  26.8 28.8 %copy-start.24 = (f32[2,10,128]{2,1,0:T(8,128)}, f32[2,10,128]{2,1,0:T(8,128)S(1)}, u32[]{:S(2)}) copy-start(f32[2,10,128]{2,1,0:T(8,128)S(1)} %get-tuple-element.39.rows) | copy-start | bytes 30724
  26.8 2.2 %collective-permute-start.7 = (bf16[144,640]{1,0:T(8,128)(2,1)S(1)}, bf16[144,640]{1,0:T(8,128)(2,1)S(1)}, u32[]{:S(2)}, u32[]{:S(2)}) collective-permute-start(bf16[144,640]{1,0:T(8,128)(2,1)S(1)} %get-tuple-element.28), channel_id=1, source_target_pairs={{0,4},{4,0},{1,5},{5,1},{2,6},{6,2},{3,7},{7,3},{8,12},{12,8},{9,1... | collective-permute-start | bytes 552968 | tf_op jit(solution)/shard_map/ppermute | solution.py:349
  29.0 47.2 %copy-start.4 = (bf16[1,128,640]{2,1,0:T(8,128)(2,1)S(1)}, bf16[1,128,640]{2,1,0:T(8,128)(2,1)}, u32[]{:S(2)}) copy-start(bf16[1,128,640]{2,1,0:T(8,128)(2,1)} %param.19) | copy-start | bytes 491524
  56.9 15.1 %all-to-all-start.1 = ((bf16[16,8,640]{2,1,0:T(8,128)(2,1)}), bf16[16,8,640]{2,1,0:T(8,128)(2,1)S(1)}, u32[]{:S(2)}, u32[]{:S(2)}) async-start(bf16[16,8,640]{2,1,0:T(8,128)(2,1)} %chain.1), calls=%async_computation.1 | async-start | bytes 327680 | tf_op jit(solution)/shard_map/all_to_all | solution.py:344
  72.0 27.7 %all-to-all-start.3 = ((bf16[8,320,128]{2,1,0:T(8,128)(2,1)}), bf16[8,320,128]{2,1,0:T(8,128)(2,1)S(1)}, u32[]{:S(2)}, u32[]{:S(2)}) async-start(bf16[8,320,128]{2,1,0:T(8,128)(2,1)} %bitcast.28), calls=%async_computation.3 | async-start | bytes 1310720 | tf_op jit(solution)/shard_map/all_to_all | solution.py:344
  75.7 4.4 %collective-permute-start.8 = (bf16[128,640]{1,0:T(8,128)(2,1)S(1)}, bf16[128,640]{1,0:T(8,128)(2,1)S(1)}, u32[]{:S(2)}, u32[]{:S(2)}) collective-permute-start(bf16[128,640]{1,0:T(8,128)(2,1)S(1)} %get-tuple-element.30), channel_id=1, source_target_pairs={{0,4},{4,0},{1,5},{5,1},{2,6},{6,2},{3,7},{7,3},{8,12},{12,8},{9,1... | collective-permute-start | bytes 491528 | tf_op jit(solution)/shard_map/ppermute | solution.py:349
  86.4 3.1 %collective-permute-start.9 = (f32[8,896]{1,0:T(8,128)S(1)}, f32[8,896]{1,0:T(8,128)S(1)}, u32[]{:S(2)}, u32[]{:S(2)}) collective-permute-start(f32[8,896]{1,0:T(8,128)S(1)} %get-tuple-element.45), channel_id=1, source_target_pairs={{4,0},{8,4},{12,8},{16,12},{20,16},{24,20},{28,24},{32,28},{36,32}... | collective-permute-start | bytes 86024 | tf_op jit(solution)/shard_map/ppermute | solution.py:457
  90.5 21.9 %collective-permute-start.12 = (bf16[128,1024]{1,0:T(8,128)(2,1)S(1)}, bf16[128,1024]{1,0:T(8,128)(2,1)S(1)}, u32[]{:S(2)}, u32[]{:S(2)}) collective-permute-start(bf16[128,1024]{1,0:T(8,128)(2,1)S(1)} %conv_back.1.grads.g0), channel_id=1, source_target_pairs={{0,136},{8,0},{128,8},{136,128},{1,137},{9,1},{129,9},{137,129},{2... | collective-permute-start | bytes 786440 | tf_op jit(solution)/shard_map/ppermute | solution.py:349
  95.3 17.1 %collective-permute-start.11 = (bf16[128,1024]{1,0:T(8,128)(2,1)S(1)}, bf16[128,1024]{1,0:T(8,128)(2,1)S(1)}, u32[]{:S(2)}, u32[]{:S(2)}) collective-permute-start(bf16[128,1024]{1,0:T(8,128)(2,1)S(1)} %conv_back.1.grads.g0), channel_id=1, source_target_pairs={{0,128},{8,136},{128,0},{136,8},{1,129},{9,137},{129,1},{137,9},{2... | collective-permute-start | bytes 786440 | tf_op jit(solution)/shard_map/ppermute | solution.py:349
  95.3 17.6 %collective-permute-start.10 = (bf16[128,1024]{1,0:T(8,128)(2,1)S(1)}, bf16[128,1024]{1,0:T(8,128)(2,1)S(1)}, u32[]{:S(2)}, u32[]{:S(2)}) collective-permute-start(bf16[128,1024]{1,0:T(8,128)(2,1)S(1)} %conv_back.1.grads.g0), channel_id=1, source_target_pairs={{0,8},{8,128},{128,136},{136,0},{1,9},{9,129},{129,137},{137,1},{2... | collective-permute-start | bytes 786440 | tf_op jit(solution)/shard_map/ppermute | solution.py:349
  99.6 17.9 %all-to-all-start.2 = ((bf16[4,32,2560]{2,1,0:T(8,128)(2,1)}), bf16[4,32,2560]{2,1,0:T(8,128)(2,1)S(1)}, u32[]{:S(2)}, u32[]{:S(2)}) async-start(bf16[4,32,2560]{2,1,0:T(8,128)(2,1)} %input_grad.1), calls=%async_computation.2 | async-start | bytes 1310720 | tf_op jit(solution)/shard_map/all_to_all | solution.py:344
  110.1 3.4 %collective-permute-start.13 = (bf16[128,1024]{1,0:T(8,128)(2,1)S(1)}, bf16[128,1024]{1,0:T(8,128)(2,1)S(1)}, u32[]{:S(2)}, u32[]{:S(2)}) collective-permute-start(bf16[128,1024]{1,0:T(8,128)(2,1)S(1)} %conv_back.1.grads.g0), channel_id=1, source_target_pairs={{0,4},{4,0},{1,5},{5,1},{2,6},{6,2},{3,7},{7,3},{8,12},{12,8},{9,1... | collective-permute-start | bytes 786440 | tf_op jit(solution)/shard_map/ppermute | solution.py:349
  112.4 1.5 collective-permute-start.16
  112.4 1.9 %collective-permute-start.15 = (bf16[128,1024]{1,0:T(8,128)(2,1)S(1)}, bf16[128,1024]{1,0:T(8,128)(2,1)S(1)}, u32[]{:S(2)}, u32[]{:S(2)}) collective-permute-start(bf16[128,1024]{1,0:T(8,128)(2,1)S(1)} %collective-permute-done.11.g2), channel_id=1, source_target_pairs={{0,4},{4,0},{1,5},{5,1},{2,6},{6,2},{3,7},{7,3},{8,12},{12,8},{9,1... | collective-permute-start | bytes 786440 | tf_op jit(solution)/shard_map/ppermute | solution.py:349
  112.9 1.8 %collective-permute-start.14 = (bf16[128,1024]{1,0:T(8,128)(2,1)S(1)}, bf16[128,1024]{1,0:T(8,128)(2,1)S(1)}, u32[]{:S(2)}, u32[]{:S(2)}) collective-permute-start(bf16[128,1024]{1,0:T(8,128)(2,1)S(1)} %collective-permute-done.10.g1), channel_id=1, source_target_pairs={{0,4},{4,0},{1,5},{5,1},{2,6},{6,2},{3,7},{7,3},{8,12},{12,8},{9,1... | collective-permute-start | bytes 786440 | tf_op jit(solution)/shard_map/ppermute | solution.py:349
  138.6 19.4 %all-to-all-start.4 = ((bf16[8,40,768]{2,1,0:T(8,128)(2,1)}), bf16[8,40,768]{2,1,0:T(8,128)(2,1)S(1)}, u32[]{:S(2)}, u32[]{:S(2)}) async-start(bf16[8,40,768]{2,1,0:T(8,128)(2,1)} %get-tuple-element.48), calls=%async_computation.4 | async-start | bytes 983040 | tf_op jit(solution)/shard_map/all_to_all | solution.py:344
  (23 other events, 116.9 us)

commit v2 on v1

v2 whole, which is shorter than its diff:
```python
import math

import jax
import jax.numpy as jnp
from jax import lax
from jax.experimental import pallas as pl
from jax.experimental.pallas import tpu as pltpu
from jax.sharding import Mesh
from jax.sharding import PartitionSpec as P


HDIM = 64
SEQ = ("seq_0", "seq_1", "seq_2")
PAIRS = ("seq_0", "seq_1")
ROW4 = ("dp", "seq_1")
ROW8 = ("dp", "seq_1", "seq_2")
DP_SEQ = ("dp", "seq_0", "seq_1", "seq_2")
SEQ_CHAN = ("seq_0", "seq_1", "seq_2", "chan")
DP_SEQ_CHAN = ("dp", "seq_0", "seq_1", "seq_2", "chan")

F32 = jnp.float32
BF16 = jnp.bfloat16
HIGHEST = lax.Precision.HIGHEST
HALO = 16


def dot(a, b, ca=1, cb=0, precision=None):
    return lax.dot_general(
        a, b, (((ca,), (cb,)), ((), ())), precision=precision, preferred_element_type=F32
    )


def in_hbm(value):
    return pltpu.with_memory_space_constraint(value, pltpu.HBM)


def call(kernel, outs, ins, loads=(), stores=(), scratch=(), flops=0, early=False):
    count = len(ins)

    def wrapped(*refs):
        refs = list(refs)
        operands, results = refs[:count], refs[count : count + len(outs)]
        spare = refs[count + len(outs) :]
        sems = spare.pop()
        copies = []
        for k, position in enumerate(loads):
            buffer = spare.pop(0)
            copies.append(pltpu.make_async_copy(operands[position], buffer, sems.at[k]))
            operands[position] = buffer
        for copy in copies:
            copy.start()
        pending = {}
        for k, position in enumerate(stores):
            buffer = spare.pop(0)
            pending[position] = pltpu.make_async_copy(
                buffer, results[position], sems.at[len(loads) + k]
            )
            results[position] = buffer
        for copy in copies:
            copy.wait()
        started = []

        def flush(position):
            pending[position].start()
            started.append(position)

        if early:
            kernel(*operands, *results, *spare, flush=flush)
        else:
            kernel(*operands, *results, *spare)
        for position in stores:
            if position not in started:
                pending[position].start()
        for position in stores:
            pending[position].wait()

    specs, values = [], []
    for k, a in enumerate(ins):
        space = pltpu.VMEM
        if a.dtype == jnp.int32:
            space = pltpu.SMEM
        elif k in loads:
            space = pltpu.HBM
            a = in_hbm(a)
        specs.append(pl.BlockSpec(memory_space=space))
        values.append(a)
    buffers = [pltpu.VMEM(ins[k].shape, ins[k].dtype) for k in loads]
    buffers += [pltpu.VMEM(*outs[k]) for k in stores]
    return pl.pallas_call(
            wrapped,
            out_shape=[
                pltpu.HBM(s, d) if k in stores else jax.ShapeDtypeStruct(s, d)
                for k, (s, d) in enumerate(outs)
            ],
            in_specs=specs,
            out_specs=[
                pl.BlockSpec(memory_space=pltpu.HBM if k in stores else pltpu.VMEM)
                for k in range(len(outs))
            ],
            scratch_shapes=buffers
            + list(scratch)
            + [pltpu.SemaphoreType.DMA((len(loads) + len(stores) + 1,))],
            compiler_params=pltpu.CompilerParams(vmem_limit_bytes=24 << 20),
            cost_estimate=pl.CostEstimate(flops=flops, transcendentals=0, bytes_accessed=1 << 20),
    )(*values)


def heads_to_lanes(heads, width):
    head = lax.broadcasted_iota(jnp.int32, (heads, width), 0)
    lane = lax.broadcasted_iota(jnp.int32, (heads, width), 1)
    return (lane // HDIM == head).astype(F32)


def lanes_to_heads(width, heads):
    lane = lax.broadcasted_iota(jnp.int32, (width, heads), 0)
    head = lax.broadcasted_iota(jnp.int32, (width, heads), 1)
    return (lane // HDIM == head).astype(F32)


def lower(size):
    row = lax.broadcasted_iota(jnp.int32, (size, size), 0)
    col = lax.broadcasted_iota(jnp.int32, (size, size), 1)
    return row >= col


def silu_and_slope(v):
    gate = 1.0 / (1.0 + jnp.exp(-v))
    return v * gate, gate * (1.0 + v * (1.0 - gate))


def load_kernel(*refs):
    half = len(refs) // 2
    for source, out in zip(refs[:half], refs[half:]):
        out[...] = source[...]


def project_kernel(
    who, x0, x1, x2, x3, h0, h1, h2, h3, w_in, w_mix, w_step, k_in, k_mix, bias, decay_log, g,
    x_out, big, z_out, small, rows, keep, send, kept,
    xs, pi, pm, *, flush,
):
    chan, core = who[0], who[1]
    part = x0.shape[0]
    tokens = 4 * part
    width = k_in.shape[1]
    mixed = k_mix.shape[1]
    state_width = mixed // 2
    heads = bias.shape[1]
    for k, x in enumerate((x0, x1, x2, x3)):
        slot = lax.rem(chan + 4 - k, 4)
        xs[pl.ds(pl.multiple_of(HALO + slot * part, 16), part), :] = x[...]
    edge = h0.shape[0]
    xs[0:HALO, :] = jnp.zeros_like(xs[0:HALO, :])
    xs[0:edge, :] = h0[...] + h1[...] + h2[...] + h3[...]
    everything = xs[...]
    x_out[...] = xs[HALO:, :]
    flush(0)
    pi[...] = dot(everything, w_in[...]).astype(BF16).astype(F32)
    pm[...] = dot(everything, w_mix[...]).astype(BF16).astype(F32)
    pi[HALO - edge : HALO, :] = pi[0:edge, :]
    pm[HALO - edge : HALO, :] = pm[0:edge, :]
    raw = dot(xs[HALO:, :], w_step[...], 1, 1) + bias[...]

    def convolved(source, kernel):
        total = kernel[3:4, :] * source[HALO:, :]
        for k in range(3):
            start = HALO - 3 + k
            total = total + kernel[k : k + 1, :] * source[start : start + tokens, :]
        return total

    inner_act, inner_slope = silu_and_slope(convolved(pi, k_in))
    big[:, :width] = inner_act
    big[:, width : 2 * width] = inner_slope
    mix_act, mixer_slope = silu_and_slope(convolved(pm, k_mix))
    big[:, 2 * width : 2 * width + mixed] = mix_act
    big[:, 2 * width + mixed :] = mixer_slope
    flush(1)

    step = jnp.maximum(raw, 0.0) + jnp.log1p(jnp.exp(-jnp.abs(raw)))
    decay = -step * jnp.exp(decay_log[...])
    low = lower(tokens).astype(F32)
    total = dot(low, decay, precision=HIGHEST)
    rows[0] = dot(decay, low, 0, 1, precision=HIGHEST)
    row = lax.broadcasted_iota(jnp.int32, (tokens, tokens), 0)
    col = lax.broadcasted_iota(jnp.int32, (tokens, tokens), 1)
    rows[1] = dot(step, (row == col).astype(F32), 0, 0, precision=HIGHEST)
    last = total[tokens - 1 : tokens, :]
    ea = jnp.exp(total)
    tail = jnp.exp(last - total)
    small[0] = step
    small[1] = total
    small[2] = ea
    small[3] = tail
    small[4] = 1.0 / (1.0 + jnp.exp(-raw))
    spread = heads_to_lanes(heads, width)
    wide = dot(jnp.concatenate([tail * step, ea], axis=0), spread, precision=HIGHEST)
    zs = (wide[:tokens] * inner_act).astype(BF16)
    zg = (wide[tokens:] * g[...].astype(F32)).astype(BF16)
    z_out[:, :width] = zs
    z_out[:, width:] = zg
    for k in (2, 3, 4):
        flush(k)
    into = mix_act[:, :state_width].astype(BF16)
    out_of = mix_act[:, state_width:].astype(BF16)
    state = dot(into, zs, 0, 0)
    grad = dot(out_of, zg, 0, 0)
    lead = last.astype(BF16)
    keep[:, width:] = jnp.zeros_like(keep[:, width:])
    send[:, width:] = jnp.zeros_like(send[:, width:])
    keep[0:1, width : width + heads] = last
    send[0:1, width : width + heads] = lead
    send[1:2, width : width + heads] = (last - lead.astype(F32)).astype(BF16)

    @pl.when(core == 0)
    def _():
        keep[:, :width] = state
        send[:, :width] = grad.astype(BF16)

    @pl.when(core != 0)
    def _():
        keep[:, :width] = grad
        send[:, :width] = state.astype(BF16)

    kept[...] = keep[...]


def pair_kernel(keep, recv, out):
    groups, per = out.shape[0], out.shape[1]
    heads = out.shape[2] // HDIM - 2
    width = heads * HDIM
    spread = heads_to_lanes(heads, width)
    own = keep[0:8, width : width + heads]
    other = recv[0:16, width : width + heads].astype(F32)
    theirs = other[0:1] + other[1:2]
    wide = dot(jnp.broadcast_to(jnp.exp(theirs), (8, heads)), spread, precision=HIGHEST)
    pair = (wide[0:1] * keep[:, :width] + recv[:, :width].astype(F32)).astype(BF16)
    total = own[0:1] + theirs
    lead = total.astype(BF16)
    rest = (total - lead.astype(F32)).astype(BF16)
    out[:, :, :width] = pair.reshape(groups, per, width)
    out[:, :, width:] = jnp.zeros_like(out[:, :, width:])
    for k in range(groups):
        out[k, 0:1, width : width + heads] = lead
        out[k, 1:2, width : width + heads] = rest


def chain_kernel(who, recv, out, factors):
    forward = who[1] == 0
    groups = recv.shape[0]
    width = out.shape[2]
    heads = width // HDIM
    marks = recv[:, 0, width : width + heads].astype(F32)
    marks = marks + recv[:, 1, width : width + heads].astype(F32)
    factors[...] = dot(jnp.exp(marks), heads_to_lanes(heads, width), precision=HIGHEST)

    def step(k, state):
        slot = jnp.where(forward, k, groups - 1 - k)
        out[slot] = state.astype(BF16)
        return factors[pl.ds(slot, 1), :] * state + recv[slot, :, :width].astype(F32)

    lax.fori_loop(0, groups, step, jnp.zeros(out.shape[1:], F32), unroll=True)


def back_kernel(keep, before, own, send):
    groups, per, width = before.shape
    heads = width // HDIM
    last = jnp.broadcast_to(keep[0:1, width : width + heads], (8, heads))
    factor = dot(jnp.exp(last), heads_to_lanes(heads, width), precision=HIGHEST)[0:1]
    piece = before[...].reshape(groups * per, width)
    own[...] = piece
    send[...] = (factor * piece.astype(F32) + keep[:, :width]).astype(BF16)


def pack_kernel(who, x, *refs, half):
    outs, turned_x = refs[:-1], refs[-1]
    core, place = who[1], who[2]
    model = x.shape[1]
    lines = 8
    share = outs[0].shape[0] // lines
    for k in range(model // 128):
        lanes = slice(k * 128, (k + 1) * 128)
        turned_x[lanes, :] = x[:, lanes].astype(F32).T
    for k, out in enumerate(outs):
        steps, flip = divmod(k, 2)
        where = lax.rem(place + steps, 4)
        side = core if flip == 0 else 1 - core
        outer = where // half
        inner = 2 * (where - outer * half) + side
        for line in range(lines):
            start = share * ((outer * lines + line) * 2 * half + inner)
            out[line * share : (line + 1) * share, :] = turned_x[
                pl.ds(pl.multiple_of(start, 8), share), :
            ].astype(BF16)


def within_kernel(big, g, small, rows, u_out, row_out, col_out):
    tokens, width = g.shape
    mixed = (big.shape[1] - 2 * width) // 2
    state_width = mixed // 2
    into = big[:, 2 * width : 2 * width + state_width].astype(BF16)
    out_of = big[:, 2 * width + state_width : 2 * width + mixed].astype(BF16)
    scores = dot(out_of, into, 1, 1)
    causal = lower(tokens)
    lane = lax.broadcasted_iota(jnp.int32, (tokens, 128), 1)
    pull = jnp.zeros((tokens, tokens), F32)
    for pair in range(width // 128):
        lanes = slice(pair * 128, (pair + 1) * 128)
        x_pair = big[:, lanes].astype(BF16)
        g_pair = g[:, lanes]
        u_pair = jnp.zeros((tokens, 128), F32)
        for half in range(2):
            h = 2 * pair + half
            g_head = jnp.where(lane // HDIM == half, g_pair, jnp.zeros_like(g_pair))
            inner = dot(g_head, x_pair, 1, 1)
            spread = small[1, :, h : h + 1] - rows[0, h : h + 1, :]
            decay = jnp.where(causal, jnp.exp(jnp.where(causal, spread, 0.0)), 0.0)
            weights = decay * scores
            u_pair = u_pair + dot(weights.astype(BF16), g_head, 0, 0)
            step_row = rows[1, h : h + 1, :]
            both = weights * inner
            col_out[h : h + 1, :] = jnp.sum(both, axis=0, keepdims=True)
            row_out[:, h : h + 1] = jnp.sum(both * step_row, axis=1, keepdims=True)
            pull = pull + decay * inner * step_row
        u_out[:, lanes] = u_pair
    pull = pull.astype(BF16)
    u_out[:, width : width + state_width] = dot(pull, out_of, 0, 0)
    u_out[:, width + state_width :] = dot(pull, into)


def back_through_kernel(
    who, own, other, big, z, small, u, row_in, col_in, g, decay_log, skip, k_in, k_mix,
    pre_out, head_out, step_out, k_out, s0, gt,
):
    tokens, width = g.shape
    heads = small.shape[2]
    mixed = (big.shape[1] - 2 * width) // 2
    state_width = mixed // 2

    @pl.when(who[1] == 0)
    def _():
        s0[...] = own[...]
        gt[...] = other[...]

    @pl.when(who[1] != 0)
    def _():
        s0[...] = other[...]
        gt[...] = own[...]

    into = big[:, 2 * width : 2 * width + state_width].astype(BF16)
    out_of = big[:, 2 * width + state_width : 2 * width + mixed].astype(BF16)
    zs = z[:, :width]
    zg = z[:, width:]
    gb = dot(into, gt[...])
    sc = dot(out_of, s0[...])
    step = small[0]
    spread = heads_to_lanes(heads, width)
    gather = lanes_to_heads(width, heads)
    skip_rows = jnp.broadcast_to(skip[...], (8, heads))
    wide = dot(
        jnp.concatenate([step, small[3], skip_rows], axis=0), spread, precision=HIGHEST
    )
    tail_gb = wide[tokens : 2 * tokens] * gb
    x = big[:, :width]
    upstream = g[...].astype(F32)
    d_act = wide[:tokens] * (u[:, :width] + tail_gb) + wide[2 * tokens : 2 * tokens + 1] * upstream
    d_pre = d_act * big[:, width : 2 * width]
    pre_out[:, :width] = d_pre
    cross = jnp.sum(gt[...].astype(F32) * s0[...].astype(F32), axis=0, keepdims=True)
    sums = dot(
        jnp.concatenate(
            [x * tail_gb, zg.astype(F32) * sc, jnp.broadcast_to(cross, (8, width))], axis=0
        ),
        gather,
        precision=HIGHEST,
    )
    e_part = sums[:tokens]
    c_part = sums[tokens : 2 * tokens]
    f_part = sums[2 * tokens : 2 * tokens + 1]
    row = lax.broadcasted_iota(jnp.int32, (tokens, tokens), 0)
    col = lax.broadcasted_iota(jnp.int32, (tokens, tokens), 1)
    col_part = dot((row == col).astype(F32), col_in[...], 1, 1, precision=HIGHEST)
    e_step = step * e_part
    d_total = row_in[...] + c_part - step * col_part - e_step
    at_end = jnp.sum(e_step, axis=0, keepdims=True) + small[2, tokens - 1 : tokens, :] * f_part
    d_decay = dot((row <= col).astype(F32), d_total, precision=HIGHEST) + at_end
    d_step = col_part + e_part - d_decay * jnp.exp(decay_log[...])
    step_out[...] = jnp.zeros_like(step_out)
    step_out[:, :heads] = (d_step * small[4]).astype(BF16)
    d_into = u[:, width : width + state_width] + dot(zs, gt[...], 1, 1)
    d_out_of = u[:, width + state_width :] + dot(zg, s0[...], 1, 1)
    slopes = 2 * width + mixed
    pre_out[:, width : width + state_width] = d_into * big[:, slopes : slopes + state_width]
    pre_out[:, width + state_width :] = d_out_of * big[:, slopes + state_width :]
    head_out[...] = pre_out[0:8, :]
    k_out[:, :width] = k_in[...]
    k_out[:, width:] = k_mix[...]


def conv_back_kernel(pre, ahead, step, kernel, out, mix_out, padded):
    tokens = pre.shape[0]
    width = out.shape[1] - 128
    padded[:tokens, :] = pre[...]
    padded[tokens:, :] = ahead[...]

    def convolved(lanes):
        total = kernel[3:4, lanes] * padded[:tokens, lanes]
        for k in range(3):
            total = total + kernel[k : k + 1, lanes] * padded[3 - k : 3 - k + tokens, lanes]
        return total

    out[:, :width] = convolved(slice(0, width)).astype(BF16)
    out[:, width:] = step[...]
    mix_out[...] = convolved(slice(width, pre.shape[1])).astype(BF16)


def input_grad_kernel(who, grads, mix_grads, w_in, w_mix, w_step, *refs):
    outs, whole = refs[:4], refs[4]
    width = w_in.shape[1]
    heads = w_step.shape[0]
    total = dot(grads[:, :width], w_in[...], 1, 1)
    total = total + dot(mix_grads[...], w_mix[...], 1, 1)
    total = total + dot(grads[:, width : width + heads], w_step[...])
    whole[...] = total.astype(BF16)
    part = outs[0].shape[0]
    for k, out in enumerate(outs):
        slot = lax.rem(who[0] + k, 4)
        out[...] = whole[pl.ds(pl.multiple_of(slot * part, 16), part), :]


def add_kernel(m0, m1, m2, m3, out):
    total = m0[...].astype(F32) + m1[...].astype(F32) + m2[...].astype(F32) + m3[...].astype(F32)
    out[...] = total.astype(BF16)


def gathered_product(slabs, grads):
    total = None
    for slab, grad in zip(slabs, grads):
        part = dot(slab[...], grad[...])
        total = part if total is None else total + part
    return total


def inner_weight_kernel(*refs):
    refs[-1][...] = gathered_product(refs[:8], refs[8:16]).astype(BF16)


def mixer_weight_kernel(who, *refs):
    slabs, grads, inner, out = refs[:8], refs[8:16], refs[16], refs[17]
    chan = who[0]
    lines, share, _ = out.shape
    total = gathered_product(slabs, grads).astype(BF16)
    size = lines * share
    few = share // 4
    to_row = lax.broadcasted_iota(jnp.int32, (size, size), 0)
    from_row = lax.broadcasted_iota(jnp.int32, (size, size), 1)
    within_line = to_row - (to_row // share) * share
    group = within_line // few
    wanted = to_row - within_line + chan * few + (within_line - group * few)
    chosen = None
    for q in range(4):
        pick = ((from_row == wanted) & (group == q)).astype(BF16)
        part = dot(pick, total[:, q * 64 : (q + 1) * 64])
        chosen = part if chosen is None else chosen + part
    edge = inner.shape[1] - 64
    out[:, :, :] = inner[...].reshape(out.shape)
    out[:, :, edge:] = chosen.astype(BF16).reshape(lines, share, 64)


def total_kernel(terms, inner_out, mix_out, step_out, whole, *, norm):
    lines, share, _ = terms.shape
    width = inner_out.shape[1]
    few = share // 4
    total = terms[0].astype(F32)
    for k in range(1, lines):
        total = total + terms[k].astype(F32)
    whole[...] = total * norm
    inner_out[...] = whole[:, :width]
    edge = whole.shape[1] - 64
    for q in range(4):
        mix_out[:, q * 64 : (q + 1) * 64] = whole[q * few : (q + 1) * few, edge:]
    heads = step_out.shape[0]
    row = lax.broadcasted_iota(jnp.int32, (heads, 128), 0)
    col = lax.broadcasted_iota(jnp.int32, (heads, 128), 1)
    step_out[...] = dot(
        (row == col).astype(F32), whole[:, width : width + 128], 1, 1, precision=HIGHEST
    )


def a2a(value, axis):
    return lax.all_to_all(value, axis, split_axis=0, concat_axis=0, tiled=True)


def moves(steps, flip, count):
    return [
        (2 * d + c, 2 * ((d + steps) % (count // 2)) + (c ^ flip))
        for d in range(count // 2)
        for c in range(2)
    ]


def turned(value, axis, steps):
    count = lax.axis_size(axis)
    return lax.ppermute(value, axis, [(k, (k + steps) % count) for k in range(count)])


def layer(
    layer_input,
    inner_weight,
    mixer_weight,
    step_weight,
    conv_inner,
    conv_mixer,
    step_bias,
    decay_log,
    skip_gain,
    output_grad,
):
    own = layer_input[0]
    part, model = own.shape
    chans = lax.axis_size("chan")
    tokens = part * chans
    width = inner_weight.shape[1]
    heads = step_bias.shape[0]
    mixed = mixer_weight.shape[1]
    state_width = mixed // 2
    g = output_grad[0]
    who = jnp.stack(
        [lax.axis_index("chan"), lax.axis_index("seq_2"), lax.axis_index(ROW4)]
    ).astype(jnp.int32)
    bias = step_bias[None]
    rate = decay_log[None]
    skip = skip_gain[None]

    seq_count = lax.axis_size(SEQ)
    t, c = tokens, width

    arrived = [turned(own, "chan", k) for k in (1, 2, 3)]
    tail_rows = own[part - 4 :]
    halos = [
        lax.ppermute(
            tail_rows,
            SEQ_CHAN,
            [(s * chans + chans - 1, (s + 1) * chans + k) for s in range(seq_count - 1)],
        )
        for k in range(chans)
    ]
    sources = [
        own, inner_weight, mixer_weight, step_weight.T, conv_inner, conv_mixer, bias, rate, g
    ]
    near = call(
        load_kernel,
        [(v.shape, v.dtype) for v in sources],
        sources,
        loads=tuple(range(len(sources))),
        flops=700_000_000,
    )
    x, big, z, small, rows, keep, send, kept = call(
        project_kernel,
        [
            ((t, model), BF16),
            ((t, 2 * c + 2 * mixed), F32),
            ((t, 2 * c), BF16),
            ((5, t, heads), F32),
            ((2, heads, t), F32),
            ((state_width, c + 128), F32),
            ((state_width, c + 128), BF16),
            ((state_width, c + 128), F32),
        ],
        [who, near[0], *arrived, *halos, *near[1:]],
        stores=(0, 1, 2, 3, 4, 7),
        scratch=[
            pltpu.VMEM((t + HALO, model), BF16),
            pltpu.VMEM((t + HALO, c), F32),
            pltpu.VMEM((t + HALO, mixed), F32),
        ],
        flops=700_000_000,
        early=True,
    )
    got = turned(send, "seq_2", 1)
    groups = lax.axis_size(PAIRS)
    per = state_width // groups
    (pairs,) = call(pair_kernel, [((groups, per, c + 128), BF16)], [keep, got])
    pairs = a2a(pairs, PAIRS)

    u, row_part, col_part = call(
        within_kernel,
        [((t, c + mixed), F32), ((t, heads), F32), ((heads, t), F32)],
        [big, g, small, rows],
        loads=(0, 1, 2, 3),
        stores=(0, 1, 2),
        flops=700_000_000,
    )
    group8 = lax.axis_size(ROW8)
    share = model // lax.axis_size(DP_SEQ)
    lines = lax.axis_size("seq_0")
    slabs = call(
        lambda *refs: pack_kernel(*refs, half=lax.axis_size("seq_1")),
        [((lines * share, t), BF16)] * group8,
        [who, x],
        loads=(1,),
        scratch=[pltpu.VMEM((model, t), F32)],
        flops=500_000_000,
    )
    slabs = [slabs[0]] + [
        lax.ppermute(slabs[k], ROW8, moves(k // 2, k % 2, group8)) for k in range(1, group8)
    ]

    (befores,) = call(
        chain_kernel,
        [((groups, per, c), BF16)],
        [who, pairs],
        scratch=[pltpu.VMEM((groups, c), F32)],
    )
    befores = a2a(befores, PAIRS)
    mine, others = call(back_kernel, [((state_width, c), BF16)] * 2, [kept, befores], loads=(0,))
    others = turned(others, "seq_2", 1)
    pre, head, step_grad, kernels = call(
        back_through_kernel,
        [((t, c + mixed), F32), ((8, c + mixed), F32), ((t, 128), BF16), ((4, c + mixed), F32)],
        [
            who, mine, others, big, z, small, u, row_part, col_part, g, rate, skip, conv_inner,
            conv_mixer,
        ],
        loads=tuple(range(3, 14)),
        scratch=[pltpu.VMEM((state_width, c), BF16), pltpu.VMEM((state_width, c), BF16)],
        flops=500_000_000,
    )
    ahead = lax.ppermute(head, SEQ, [(k + 1, k) for k in range(seq_count - 1)])
    grads, mix_grads = call(
        conv_back_kernel,
        [((t, c + 128), BF16), ((t, mixed), BF16)],
        [pre, ahead, step_grad, kernels],
        scratch=[pltpu.VMEM((t + 8, c + mixed), F32)],
    )
    far, near, next_near = [turned(grads, ROW4, k) for k in (2, 1, 3)]
    same = [grads, near, far, next_near]
    shares = [turned(mix_grads, "chan", k) for k in (2, 1, 3)]
    (mix_total,) = call(add_kernel, [((t, mixed), BF16)], [mix_grads, *shares])
    far, near, next_near = [turned(mix_total, ROW4, k) for k in (2, 1, 3)]
    mix_same = [mix_total, near, far, next_near]
    swapped = [turned(v, "seq_2", 1) for v in same]
    mix_swapped = [turned(v, "seq_2", 1) for v in mix_same]
    partial = call(
        input_grad_kernel,
        [((part, model), BF16)] * chans,
        [who, grads, mix_grads, inner_weight, mixer_weight, step_weight.T],
        loads=(3, 4, 5),
        scratch=[pltpu.VMEM((tokens, model), BF16)],
        flops=500_000_000,
    )
    partial = [partial[0]] + [turned(partial[k], "chan", k) for k in (2, 1, 3)]
    (input_grad,) = call(add_kernel, [((part, model), BF16)], partial)
    (inner_terms,) = call(
        inner_weight_kernel,
        [((lines * share, c + 128), BF16)],
        [*slabs, *[v for pair in zip(same, swapped) for v in pair]],
        flops=700_000_000,
    )
    (terms,) = call(
        mixer_weight_kernel,
        [((lines, share, c + 128), BF16)],
        [who, *slabs, *[v for pair in zip(mix_same, mix_swapped) for v in pair], inner_terms],
        flops=700_000_000,
    )
    norm = 1.0 / math.sqrt(tokens * seq_count * lax.axis_size("dp"))
    terms = a2a(terms, "seq_0")
    inner_weight_grad, mixer_weight_grad, step_weight_grad = call(
        lambda *refs: total_kernel(*refs, norm=norm),
        [((share, c), F32), ((share // chans, mixed), F32), ((heads, share), F32)],
        [terms],
        scratch=[pltpu.VMEM((share, c + 128), F32)],
    )
    return input_grad[None], inner_weight_grad, mixer_weight_grad, step_weight_grad.T


def solution(mesh):
    split = Mesh(
        mesh.devices.reshape(mesh.shape["dp"], 8, 2, 2, mesh.shape["chan"]),
        ("dp", "seq_0", "seq_1", "seq_2", "chan"),
    )
    placed = (
        P("dp", SEQ_CHAN, None),
        P(None, "chan"),
        P(),
        P(None, "chan"),
        P(None, "chan"),
        P(),
        P("chan"),
        P("chan"),
        P("chan"),
        P("dp", SEQ, "chan"),
    )
    return jax.shard_map(
        layer,
        mesh=split,
        in_specs=placed,
        out_specs=(
            P("dp", SEQ_CHAN, None),
            P(DP_SEQ, "chan"),
            P(DP_SEQ_CHAN, None),
            P(DP_SEQ, "chan"),
        ),
        check_vma=False,
    )
```

time: 161 us -> 149 us (0.925)
  the two profiles are of different devices: /device:TPU:4 before, /device:TPU:1 now
where the time goes in v2:
time: 149 us
  starting transfers between devices  49.7 us (33%)
  blocking collectives  35 us (23%)
  waiting for transfers between devices  32.3 us (22%)
  Pallas kernels  29.8 us (20%)
    all_to_all x2, blocking collectives, a2a(): return lax.all_to_all(value, axis, split_axis=0, concat_axis=0, tiled=True)  35 us
    ppermute x25, starting transfers between devices, turned(): lax.ppermute(value, axis, [(k, (k + steps) % count) for k in range(count)])  33.3 us
    pallas_call x15, Pallas kernels, call(): pl.pallas_call(wrapped, out_shape=[pltpu.HBM(s, d) if k in stores else ja...  29.8 us
    ppermute x25, waiting for transfers between devices, turned(): lax.ppermute(value, axis, [(k, (k + steps) % count) for k in range(count)])  19.9 us
    ppermute x7, starting transfers between devices, layer(): lax.ppermute(slabs[k], ROW8, moves(k // 2, k % 2, group8))  7.72 us
    ppermute x1, waiting for transfers between devices, layer(): ahead = lax.ppermute(head, SEQ, [(k + 1, k) for k in range(seq_count - 1)])  4.68 us
    ppermute x4, waiting for transfers between devices, layer(): lax.ppermute(tail_rows, SEQ_CHAN, [(s * chans + chans - 1, (s + 1) * chan...  4.59 us
    all_to_all x1, starting transfers between devices, a2a(): return lax.all_to_all(value, axis, split_axis=0, concat_axis=0, tiled=True)  3.49 us
  transfers between devices with their start and end apart: 38, of which 11 were waited for; matrix products, arithmetic and copies ran while one was open for 0% of the time, Pallas kernels for 13%

profile of v2, /device:TPU:1, one launch (start us, length us, event | category | flops | bytes accessed | tf_op | source)
XLA Modules:
  0.0 148.8 jit_solution(2889471124923028162)
XLA Ops:
  2.8 8.7 %collective-permute-start.2 = (bf16[32,2560]{1,0:T(8,128)(2,1)}, bf16[32,2560]{1,0:T(8,128)(2,1)S(1)}, u32[]{:S(2)}, u32[]{:S(2)}) collective-permute-start(bf16[32,2560]{1,0:T(8,128)(2,1)} %bitcast.18), channel_id=1, source_target_pairs={{0,3},{1,0},{2,1},{3,2},{4,7},{5,4},{6,5},{7,6},{8,11},{9,8},{10,9... | collective-permute-start | bytes 491528 | tf_op jit(solution)/shard_map/ppermute | solution.py:503
  14.2 2.9 %shard_map.129 = (bf16[32,2560]{1,0:T(8,128)(2,1)S(1)}, bf16[2560,640]{1,0:T(8,128)(2,1)S(1)}, bf16[2560,256]{1,0:T(8,128)(2,1)S(1)}, bf16[10,2560]{1,0:T(8,128)...) custom-call(bf16[32,2560]{1,0:T(8,128)(2,1)} %bitcast.21, ...), custom_call_target="tpu_custom_call" | custom-call | flops 700000000 | bytes 1048576 | tf_op jit(solution)/shard_map/pallas_call | solution.py:89
  17.2 4.6 %collective-permute-done.3.refs_5_ = bf16[4,2560]{1,0:T(4,128)(2,1)S(1)} collective-permute-done((bf16[4,2560]{1,0:T(4,128)(2,1)S(1)}, bf16[4,2560]{1,0:T(4,128)(2,1)S(1)}, u32[]{:S(2)}, u32[]{:S(2)}) %collective-permute-start.3) | collective-permute-done | bytes 20512 | tf_op jit(solution)/shard_map/ppermute | solution.py:540
  21.8 3.8 %shard_map.130 = (bf16[128,2560]{1,0:T(8,128)(2,1)}, f32[128,1792]{1,0:T(8,128)}, bf16[128,1280]{1,0:T(8,128)(2,1)}, f32[5,128,10]{2,1,0:T(8,128)}, f32[2,10,128...) custom-call(s32[3]{0:T(128)S(1)} %pad_add_fusion.refs_0_, ...), custom_call_target="tpu_custom_call" | custom-call | flops 700000000 | bytes 1048576 | tf_op jit(solution)/shard_map/pallas_call | solution.py:89
  27.4 21.9 %all_to_all.15.refs_1_ = bf16[16,8,768]{2,1,0:T(8,128)(2,1)S(1)} all-to-all(bf16[16,8,768]{2,1,0:T(8,128)(2,1)S(1)} %shard_map.131), channel_id=1, replica_groups=mesh['dp'=2,'seq_0'=8,'seq_1'=2,'seq_2'=2,'chan'=4] {'seq_0','seq_1'}, dimensions={0} | all-to-all | bytes 393216 | tf_op jit(solution)/shard_map/all_to_all | solution.py:490
  50.1 13.1 %all_to_all.16.refs_1_ = bf16[16,8,640]{2,1,0:T(8,128)(2,1)S(1)} all-to-all(bf16[16,8,640]{2,1,0:T(8,128)(2,1)S(1)} %shard_map.132), channel_id=1, replica_groups=mesh['dp'=2,'seq_0'=8,'seq_1'=2,'seq_2'=2,'chan'=4] {'seq_0','seq_1'}, dimensions={0} | all-to-all | bytes 327680 | tf_op jit(solution)/shard_map/all_to_all | solution.py:490
  64.4 3.3 %collective-permute-start.8 = (bf16[128,640]{1,0:T(8,128)(2,1)S(1)}, bf16[128,640]{1,0:T(8,128)(2,1)S(1)}, u32[]{:S(2)}, u32[]{:S(2)}) collective-permute-start(bf16[128,640]{1,0:T(8,128)(2,1)S(1)} %get-tuple-element.60), channel_id=1, source_target_pairs={{0,4},{4,0},{1,5},{5,1},{2,6},{6,2},{3,7},{7,3},{8,12},{12,8},{9,1... | collective-permute-start | bytes 491528 | tf_op jit(solution)/shard_map/ppermute | solution.py:503
  70.1 2.7 %collective-permute-start.15 = (bf16[320,128]{1,0:T(8,128)(2,1)S(1)}, bf16[320,128]{1,0:T(8,128)(2,1)S(1)}, u32[]{:S(2)}, u32[]{:S(2)}) collective-permute-start(bf16[320,128]{1,0:T(8,128)(2,1)S(1)} %get-tuple-element.82), channel_id=1, source_target_pairs={{0,12},{4,8},{8,132},{12,128},{128,140},{132,136},{136,4},{140,0},... | collective-permute-start | bytes 245768 | tf_op jit(solution)/shard_map/ppermute | solution.py:605
  73.7 3.3 %shard_map.134 = (f32[128,896]{1,0:T(8,128)}, f32[128,10]{1,0:T(8,128)}, f32[10,128]{1,0:T(8,128)}) custom-call(f32[128,1792]{1,0:T(8,128)} %get-tuple-element.61.refs_0_.refs_3_, bf16[128,640]{1,0:T(8,128)(2,1)} %bitcast.14, f32[5,128,10]{2,1,0:T(8,128)} %get-tuple-element.63.refs_2_.refs_5_, f32[2,10,128]{2,1,0:T(8,128)} %get-tuple-element.64.refs_3_), custom_call_target="tpu_custom_call" | custom-call | flops 700000000 | bytes 1048576 | tf_op jit(solution)/shard_map/pallas_call | solution.py:89
  77.0 4.9 %shard_map.135 = (f32[128,896]{1,0:T(8,128)S(1)}, f32[8,896]{1,0:T(8,128)S(1)}, bf16[128,128]{1,0:T(8,128)(2,1)S(1)}, f32[4,896]{1,0:T(4,128)S(1)}) custom-call(s32[3]{0:T(128)S(1)} %pad_add_fusion.refs_0_, bf16[128,640]{1,0:T(8,128)(2,1)S(1)} %get-tuple-element.59.refs_1_, bf16[128,640]{1,0:T(8,128)(2,1)S(1)} %collective-permute-done.8.refs_2_, ...), custom_call_target="tpu_custom_call" | custom-call | flops 500000000 | bytes 1048576 | tf_op jit(solution)/shard_map/pallas_call | solution.py:89
  83.9 4.7 %collective-permute-done.9.refs_1_ = f32[8,896]{1,0:T(8,128)S(1)} collective-permute-done((f32[8,896]{1,0:T(8,128)S(1)}, f32[8,896]{1,0:T(8,128)S(1)}, u32[]{:S(2)}, u32[]{:S(2)}) %collective-permute-start.9) | collective-permute-done | bytes 28704 | tf_op jit(solution)/shard_map/ppermute | solution.py:628
  90.6 2.7 %collective-permute-start.31 = (bf16[128,768]{1,0:T(8,128)(2,1)S(1)}, bf16[128,768]{1,0:T(8,128)(2,1)S(1)}, u32[]{:S(2)}, u32[]{:S(2)}) collective-permute-start(bf16[128,768]{1,0:T(8,128)(2,1)S(1)} %get-tuple-element.72.refs_1_.refs_8_), channel_id=1, source_target_pairs={{0,8},{8,128},{128,136},{136,0},{1,9},{9,129},{129,137},{137,1},{2... | collective-permute-start | bytes 589832 | tf_op jit(solution)/shard_map/ppermute | solution.py:503
  94.7 3.2 %collective-permute-done.21.refs_2_ = bf16[128,256]{1,0:T(8,128)(2,1)S(1)} collective-permute-done((bf16[128,256]{1,0:T(8,128)(2,1)S(1)}, bf16[128,256]{1,0:T(8,128)(2,1)S(1)}, u32[]{:S(2)}, u32[]{:S(2)}) %collective-permute-start.21) | collective-permute-done | bytes 65568 | tf_op jit(solution)/shard_map/ppermute | solution.py:503
  99.3 3.6 %collective-permute-start.19 = (bf16[320,128]{1,0:T(8,128)(2,1)S(1)}, bf16[320,128]{1,0:T(8,128)(2,1)S(1)}, u32[]{:S(2)}, u32[]{:S(2)}) collective-permute-start(bf16[320,128]{1,0:T(8,128)(2,1)S(1)} %get-tuple-element.86), channel_id=1, source_target_pairs={{0,140},{4,136},{8,4},{12,0},{128,12},{132,8},{136,132},{140,128},... | collective-permute-start | bytes 245768 | tf_op jit(solution)/shard_map/ppermute | solution.py:605
  104.9 2.5 %collective-permute-done.19.refs_7_.refs_8_ = bf16[320,128]{1,0:T(8,128)(2,1)S(1)} collective-permute-done((bf16[320,128]{1,0:T(8,128)(2,1)S(1)}, bf16[320,128]{1,0:T(8,128)(2,1)S(1)}, u32[]{:S(2)}, u32[]{:S(2)}) %collective-permute-start.19) | collective-permute-done | bytes 81952 | tf_op jit(solution)/shard_map/ppermute | solution.py:605
  109.5 3.1 %collective-permute-done.26.refs_13_ = bf16[128,256]{1,0:T(8,128)(2,1)S(1)} collective-permute-done((bf16[128,256]{1,0:T(8,128)(2,1)S(1)}, bf16[128,256]{1,0:T(8,128)(2,1)S(1)}, u32[]{:S(2)}, u32[]{:S(2)}) %collective-permute-start.26) | collective-permute-done | bytes 65568 | tf_op jit(solution)/shard_map/ppermute | solution.py:503
  114.1 2.8 %collective-permute-done.24.refs_11_ = bf16[128,256]{1,0:T(8,128)(2,1)S(1)} collective-permute-done((bf16[128,256]{1,0:T(8,128)(2,1)S(1)}, bf16[128,256]{1,0:T(8,128)(2,1)S(1)}, u32[]{:S(2)}, u32[]{:S(2)}) %collective-permute-start.24) | collective-permute-done | bytes 65568 | tf_op jit(solution)/shard_map/ppermute | solution.py:503
  116.9 5.5 %collective-permute-start.23 = (bf16[128,256]{1,0:T(8,128)(2,1)S(1)}, bf16[128,256]{1,0:T(8,128)(2,1)S(1)}, u32[]{:S(2)}, u32[]{:S(2)}) collective-permute-start(bf16[128,256]{1,0:T(8,128)(2,1)S(1)} %shard_map.140.refs_9_), channel_id=1, source_target_pairs={{0,4},{4,0},{1,5},{5,1},{2,6},{6,2},{3,7},{7,3},{8,12},{12,8},{9,1... | collective-permute-start | bytes 196616 | tf_op jit(solution)/shard_map/ppermute | solution.py:503
  124.2 2.9 %shard_map.142 = bf16[8,40,768]{2,1,0:T(8,128)(2,1)} custom-call(s32[3]{0:T(128)S(1)} %pad_add_fusion.refs_0_, bf16[320,128]{1,0:T(8,128)(2,1)S(1)} %get-tuple-element.79.refs_0_.refs_1_, bf16[320,128]{1,0:T(8,128)(2,1)S(1)} %collective-permute-done.13.refs_1_.refs_2_, bf16[320,128]{1,0:T(8,128)(2,1)S(1)} %collective-permute-done.14.refs_2_.refs_3_, ...), custom_call_target="tpu_custom_call" | custom-call | flops 700000000 | bytes 1048576 | tf_op jit(solution)/shard_map/pallas_call | solution.py:89
  127.1 3.5 %all-to-all-start.2 = ((bf16[8,40,768]{2,1,0:T(8,128)(2,1)}), bf16[8,40,768]{2,1,0:T(8,128)(2,1)S(1)}, u32[]{:S(2)}, u32[]{:S(2)}) async-start(bf16[8,40,768]{2,1,0:T(8,128)(2,1)} %shard_map.142), calls=%async_computation.2 | async-start | bytes 983040 | tf_op jit(solution)/shard_map/all_to_all | solution.py:490
  130.6 4.6 %shard_map.137 = (bf16[32,2560]{1,0:T(8,128)(2,1)S(1)}, bf16[32,2560]{1,0:T(8,128)(2,1)S(1)}, bf16[32,2560]{1,0:T(8,128)(2,1)S(1)}, bf16[32,2560]{1,0:T(8,128)(2,1)S(1)}) custom-call(s32[3]{0:T(128)S(1)} %pad_add_fusion.refs_0_, bf16[128,768]{1,0:T(8,128)(2,1)S(1)} %get-tuple-element.72.refs_1_.refs_8_, ...), custom_call_target="tpu_custom_call" | custom-call | flops 500000000 | bytes 1048576 | tf_op jit(solution)/shard_map/pallas_call | solution.py:89
  135.9 2.6 %collective-permute-start.12 = (bf16[32,2560]{1,0:T(8,128)(2,1)S(1)}, bf16[32,2560]{1,0:T(8,128)(2,1)S(1)}, u32[]{:S(2)}, u32[]{:S(2)}) collective-permute-start(bf16[32,2560]{1,0:T(8,128)(2,1)S(1)} %get-tuple-element.77), channel_id=1, source_target_pairs={{0,3},{1,0},{2,1},{3,2},{4,7},{5,4},{6,5},{7,6},{8,11},{9,8},{10,9... | collective-permute-start | bytes 491528 | tf_op jit(solution)/shard_map/ppermute | solution.py:503
  138.5 3.7 %collective-permute-done.10.refs_1_ = bf16[32,2560]{1,0:T(8,128)(2,1)S(1)} collective-permute-done((bf16[32,2560]{1,0:T(8,128)(2,1)S(1)}, bf16[32,2560]{1,0:T(8,128)(2,1)S(1)}, u32[]{:S(2)}, u32[]{:S(2)}) %collective-permute-start.10) | collective-permute-done | bytes 163872 | tf_op jit(solution)/shard_map/ppermute | solution.py:503
  142.2 4.3 %collective-permute-done.11.refs_2_ = bf16[32,2560]{1,0:T(8,128)(2,1)S(1)} collective-permute-done((bf16[32,2560]{1,0:T(8,128)(2,1)S(1)}, bf16[32,2560]{1,0:T(8,128)(2,1)S(1)}, u32[]{:S(2)}, u32[]{:S(2)}) %collective-permute-start.11) | collective-permute-done | bytes 163872 | tf_op jit(solution)/shard_map/ppermute | solution.py:503
  (71 shorter events, 28.6 us)
Async XLA Ops:
  1.4 10.8 %collective-permute-start.6 = (bf16[4,2560]{1,0:T(4,128)(2,1)S(1)}, bf16[4,2560]{1,0:T(4,128)(2,1)S(1)}, u32[]{:S(2)}, u32[]{:S(2)}) collective-permute-start(bf16[4,2560]{1,0:T(4,128)(2,1)S(1)} %slice_bitcast_fusion), channel_id=1, source_target_pairs={{3,7},{7,11},{11,15},{15,19},{19,23},{23,27},{27,31},{31,35},{35,3... | collective-permute-start | bytes 61448 | tf_op jit(solution)/shard_map/ppermute | solution.py:540
  2.1 10.8 %collective-permute-start.5 = (bf16[4,2560]{1,0:T(4,128)(2,1)S(1)}, bf16[4,2560]{1,0:T(4,128)(2,1)S(1)}, u32[]{:S(2)}, u32[]{:S(2)}) collective-permute-start(bf16[4,2560]{1,0:T(4,128)(2,1)S(1)} %slice_bitcast_fusion), channel_id=1, source_target_pairs={{3,6},{7,10},{11,14},{15,18},{19,22},{23,26},{27,30},{31,34},{35,3... | collective-permute-start | bytes 61448 | tf_op jit(solution)/shard_map/ppermute | solution.py:540
  2.8 19.0 %collective-permute-start.2 = (bf16[32,2560]{1,0:T(8,128)(2,1)}, bf16[32,2560]{1,0:T(8,128)(2,1)S(1)}, u32[]{:S(2)}, u32[]{:S(2)}) collective-permute-start(bf16[32,2560]{1,0:T(8,128)(2,1)} %bitcast.18), channel_id=1, source_target_pairs={{0,3},{1,0},{2,1},{3,2},{4,7},{5,4},{6,5},{7,6},{8,11},{9,8},{10,9... | collective-permute-start | bytes 491528 | tf_op jit(solution)/shard_map/ppermute | solution.py:503
  11.5 10.3 %collective-permute-start.1 = (bf16[32,2560]{1,0:T(8,128)(2,1)}, bf16[32,2560]{1,0:T(8,128)(2,1)S(1)}, u32[]{:S(2)}, u32[]{:S(2)}) collective-permute-start(bf16[32,2560]{1,0:T(8,128)(2,1)} %bitcast.19), channel_id=1, source_target_pairs={{0,2},{1,3},{2,0},{3,1},{4,6},{5,7},{6,4},{7,5},{8,10},{9,11},{10,... | collective-permute-start | bytes 491528 | tf_op jit(solution)/shard_map/ppermute | solution.py:503
  11.5 10.3 %collective-permute-start = (bf16[32,2560]{1,0:T(8,128)(2,1)}, bf16[32,2560]{1,0:T(8,128)(2,1)S(1)}, u32[]{:S(2)}, u32[]{:S(2)}) collective-permute-start(bf16[32,2560]{1,0:T(8,128)(2,1)} %bitcast.20), channel_id=1, source_target_pairs={{0,1},{1,2},{2,3},{3,0},{4,5},{5,6},{6,7},{7,4},{8,9},{9,10},{10,1... | collective-permute-start | bytes 491528 | tf_op jit(solution)/shard_map/ppermute | solution.py:503
  12.9 8.8 %collective-permute-start.3 = (bf16[4,2560]{1,0:T(4,128)(2,1)S(1)}, bf16[4,2560]{1,0:T(4,128)(2,1)S(1)}, u32[]{:S(2)}, u32[]{:S(2)}) collective-permute-start(bf16[4,2560]{1,0:T(4,128)(2,1)S(1)} %slice_bitcast_fusion), channel_id=1, source_target_pairs={{3,4},{7,8},{11,12},{15,16},{19,20},{23,24},{27,28},{31,32},{35,36... | collective-permute-start | bytes 61448 | tf_op jit(solution)/shard_map/ppermute | solution.py:540
  64.4 12.6 %collective-permute-start.8 = (bf16[128,640]{1,0:T(8,128)(2,1)S(1)}, bf16[128,640]{1,0:T(8,128)(2,1)S(1)}, u32[]{:S(2)}, u32[]{:S(2)}) collective-permute-start(bf16[128,640]{1,0:T(8,128)(2,1)S(1)} %get-tuple-element.60), channel_id=1, source_target_pairs={{0,4},{4,0},{1,5},{5,1},{2,6},{6,2},{3,7},{7,3},{8,12},{12,8},{9,1... | collective-permute-start | bytes 491528 | tf_op jit(solution)/shard_map/ppermute | solution.py:503
  69.7 19.3 %collective-permute-start.13 = (bf16[320,128]{1,0:T(8,128)(2,1)S(1)}, bf16[320,128]{1,0:T(8,128)(2,1)S(1)}, u32[]{:S(2)}, u32[]{:S(2)}) collective-permute-start(bf16[320,128]{1,0:T(8,128)(2,1)S(1)} %get-tuple-element.80), channel_id=1, source_target_pairs={{0,4},{4,0},{8,12},{12,8},{128,132},{132,128},{136,140},{140,136},... | collective-permute-start | bytes 245768 | tf_op jit(solution)/shard_map/ppermute | solution.py:605
  69.8 19.3 %collective-permute-start.14 = (bf16[320,128]{1,0:T(8,128)(2,1)S(1)}, bf16[320,128]{1,0:T(8,128)(2,1)S(1)}, u32[]{:S(2)}, u32[]{:S(2)}) collective-permute-start(bf16[320,128]{1,0:T(8,128)(2,1)S(1)} %get-tuple-element.81), channel_id=1, source_target_pairs={{0,8},{4,12},{8,128},{12,132},{128,136},{132,140},{136,0},{140,4},... | collective-permute-start | bytes 245768 | tf_op jit(solution)/shard_map/ppermute | solution.py:605
  70.1 19.6 %collective-permute-start.15 = (bf16[320,128]{1,0:T(8,128)(2,1)S(1)}, bf16[320,128]{1,0:T(8,128)(2,1)S(1)}, u32[]{:S(2)}, u32[]{:S(2)}) collective-permute-start(bf16[320,128]{1,0:T(8,128)(2,1)S(1)} %get-tuple-element.82), channel_id=1, source_target_pairs={{0,12},{4,8},{8,132},{12,128},{128,140},{132,136},{136,4},{140,0},... | collective-permute-start | bytes 245768 | tf_op jit(solution)/shard_map/ppermute | solution.py:605
  72.8 17.8 %collective-permute-start.16 = (bf16[320,128]{1,0:T(8,128)(2,1)S(1)}, bf16[320,128]{1,0:T(8,128)(2,1)S(1)}, u32[]{:S(2)}, u32[]{:S(2)}) collective-permute-start(bf16[320,128]{1,0:T(8,128)(2,1)S(1)} %get-tuple-element.83), channel_id=1, source_target_pairs={{0,128},{4,132},{8,136},{12,140},{128,0},{132,4},{136,8},{140,12},... | collective-permute-start | bytes 245768 | tf_op jit(solution)/shard_map/ppermute | solution.py:605
  89.1 19.5 %collective-permute-start.35 = (bf16[128,768]{1,0:T(8,128)(2,1)S(1)}, bf16[128,768]{1,0:T(8,128)(2,1)S(1)}, u32[]{:S(2)}, u32[]{:S(2)}) collective-permute-start(bf16[128,768]{1,0:T(8,128)(2,1)S(1)} %get-tuple-element.72.refs_1_.refs_8_), channel_id=1, source_target_pairs={{0,136},{8,0},{128,8},{136,128},{1,137},{9,1},{129,9},{137,129},{2... | collective-permute-start | bytes 589832 | tf_op jit(solution)/shard_map/ppermute | solution.py:503
  89.8 18.9 %collective-permute-start.33 = (bf16[128,768]{1,0:T(8,128)(2,1)S(1)}, bf16[128,768]{1,0:T(8,128)(2,1)S(1)}, u32[]{:S(2)}, u32[]{:S(2)}) collective-permute-start(bf16[128,768]{1,0:T(8,128)(2,1)S(1)} %get-tuple-element.72.refs_1_.refs_8_), channel_id=1, source_target_pairs={{0,128},{8,136},{128,0},{136,8},{1,129},{9,137},{129,1},{137,9},{2... | collective-permute-start | bytes 589832 | tf_op jit(solution)/shard_map/ppermute | solution.py:503
  90.6 18.5 %collective-permute-start.31 = (bf16[128,768]{1,0:T(8,128)(2,1)S(1)}, bf16[128,768]{1,0:T(8,128)(2,1)S(1)}, u32[]{:S(2)}, u32[]{:S(2)}) collective-permute-start(bf16[128,768]{1,0:T(8,128)(2,1)S(1)} %get-tuple-element.72.refs_1_.refs_8_), channel_id=1, source_target_pairs={{0,8},{8,128},{128,136},{136,0},{1,9},{9,129},{129,137},{137,1},{2... | collective-permute-start | bytes 589832 | tf_op jit(solution)/shard_map/ppermute | solution.py:503
  99.3 8.1 %collective-permute-start.19 = (bf16[320,128]{1,0:T(8,128)(2,1)S(1)}, bf16[320,128]{1,0:T(8,128)(2,1)S(1)}, u32[]{:S(2)}, u32[]{:S(2)}) collective-permute-start(bf16[320,128]{1,0:T(8,128)(2,1)S(1)} %get-tuple-element.86), channel_id=1, source_target_pairs={{0,140},{4,136},{8,4},{12,0},{128,12},{132,8},{136,132},{140,128},... | collective-permute-start | bytes 245768 | tf_op jit(solution)/shard_map/ppermute | solution.py:605
  107.5 14.9 %collective-permute-start.30 = (bf16[128,768]{1,0:T(8,128)(2,1)S(1)}, bf16[128,768]{1,0:T(8,128)(2,1)S(1)}, u32[]{:S(2)}, u32[]{:S(2)}) collective-permute-start(bf16[128,768]{1,0:T(8,128)(2,1)S(1)} %get-tuple-element.72.refs_1_.refs_8_), channel_id=1, source_target_pairs={{0,4},{4,0},{1,5},{5,1},{2,6},{6,2},{3,7},{7,3},{8,12},{12,8},{9,1... | collective-permute-start | bytes 589832 | tf_op jit(solution)/shard_map/ppermute | solution.py:503
  108.6 13.8 %collective-permute-start.36 = (bf16[128,768]{1,0:T(8,128)(2,1)S(1)}, bf16[128,768]{1,0:T(8,128)(2,1)S(1)}, u32[]{:S(2)}, u32[]{:S(2)}) collective-permute-start(bf16[128,768]{1,0:T(8,128)(2,1)S(1)} %collective-permute-done.35.refs_14_), channel_id=1, source_target_pairs={{0,4},{4,0},{1,5},{5,1},{2,6},{6,2},{3,7},{7,3},{8,12},{12,8},{9,1... | collective-permute-start | bytes 589832 | tf_op jit(solution)/shard_map/ppermute | solution.py:503
  108.6 14.3 %collective-permute-start.34 = (bf16[128,768]{1,0:T(8,128)(2,1)S(1)}, bf16[128,768]{1,0:T(8,128)(2,1)S(1)}, u32[]{:S(2)}, u32[]{:S(2)}) collective-permute-start(bf16[128,768]{1,0:T(8,128)(2,1)S(1)} %collective-permute-done.33.refs_12_), channel_id=1, source_target_pairs={{0,4},{4,0},{1,5},{5,1},{2,6},{6,2},{3,7},{7,3},{8,12},{12,8},{9,1... | collective-permute-start | bytes 589832 | tf_op jit(solution)/shard_map/ppermute | solution.py:503
  109.2 13.9 %collective-permute-start.32 = (bf16[128,768]{1,0:T(8,128)(2,1)S(1)}, bf16[128,768]{1,0:T(8,128)(2,1)S(1)}, u32[]{:S(2)}, u32[]{:S(2)}) collective-permute-start(bf16[128,768]{1,0:T(8,128)(2,1)S(1)} %collective-permute-done.31.refs_10_), channel_id=1, source_target_pairs={{0,4},{4,0},{1,5},{5,1},{2,6},{6,2},{3,7},{7,3},{8,12},{12,8},{9,1... | collective-permute-start | bytes 589832 | tf_op jit(solution)/shard_map/ppermute | solution.py:503
  116.9 7.3 %collective-permute-start.23 = (bf16[128,256]{1,0:T(8,128)(2,1)S(1)}, bf16[128,256]{1,0:T(8,128)(2,1)S(1)}, u32[]{:S(2)}, u32[]{:S(2)}) collective-permute-start(bf16[128,256]{1,0:T(8,128)(2,1)S(1)} %shard_map.140.refs_9_), channel_id=1, source_target_pairs={{0,4},{4,0},{1,5},{5,1},{2,6},{6,2},{3,7},{7,3},{8,12},{12,8},{9,1... | collective-permute-start | bytes 196616 | tf_op jit(solution)/shard_map/ppermute | solution.py:503
  127.1 20.7 %all-to-all-start.2 = ((bf16[8,40,768]{2,1,0:T(8,128)(2,1)}), bf16[8,40,768]{2,1,0:T(8,128)(2,1)S(1)}, u32[]{:S(2)}, u32[]{:S(2)}) async-start(bf16[8,40,768]{2,1,0:T(8,128)(2,1)} %shard_map.142), calls=%async_computation.2 | async-start | bytes 983040 | tf_op jit(solution)/shard_map/all_to_all | solution.py:490
  135.3 7.0 %collective-permute-start.10 = (bf16[32,2560]{1,0:T(8,128)(2,1)S(1)}, bf16[32,2560]{1,0:T(8,128)(2,1)S(1)}, u32[]{:S(2)}, u32[]{:S(2)}) collective-permute-start(bf16[32,2560]{1,0:T(8,128)(2,1)S(1)} %get-tuple-element.75), channel_id=1, source_target_pairs={{0,2},{1,3},{2,0},{3,1},{4,6},{5,7},{6,4},{7,5},{8,10},{9,11},{10,... | collective-permute-start | bytes 491528 | tf_op jit(solution)/shard_map/ppermute | solution.py:503
  135.8 10.7 %collective-permute-start.11 = (bf16[32,2560]{1,0:T(8,128)(2,1)S(1)}, bf16[32,2560]{1,0:T(8,128)(2,1)S(1)}, u32[]{:S(2)}, u32[]{:S(2)}) collective-permute-start(bf16[32,2560]{1,0:T(8,128)(2,1)S(1)} %get-tuple-element.76), channel_id=1, source_target_pairs={{0,1},{1,2},{2,3},{3,0},{4,5},{5,6},{6,7},{7,4},{8,9},{9,10},{10,1... | collective-permute-start | bytes 491528 | tf_op jit(solution)/shard_map/ppermute | solution.py:503
  135.9 10.6 %collective-permute-start.12 = (bf16[32,2560]{1,0:T(8,128)(2,1)S(1)}, bf16[32,2560]{1,0:T(8,128)(2,1)S(1)}, u32[]{:S(2)}, u32[]{:S(2)}) collective-permute-start(bf16[32,2560]{1,0:T(8,128)(2,1)S(1)} %get-tuple-element.77), channel_id=1, source_target_pairs={{0,3},{1,0},{2,1},{3,2},{4,7},{5,4},{6,5},{7,6},{8,11},{9,8},{10,9... | collective-permute-start | bytes 491528 | tf_op jit(solution)/shard_map/ppermute | solution.py:503
  (14 other events, 56.7 us)

commit v3 on v2

--- a/solution.py
+++ b/solution.py
@@ -13,7 +13,6 @@
 SEQ = ("seq_0", "seq_1", "seq_2")
 PAIRS = ("seq_0", "seq_1")
 ROW4 = ("dp", "seq_1")
-ROW8 = ("dp", "seq_1", "seq_2")
 DP_SEQ = ("dp", "seq_0", "seq_1", "seq_2")
 SEQ_CHAN = ("seq_0", "seq_1", "seq_2", "chan")
 DP_SEQ_CHAN = ("dp", "seq_0", "seq_1", "seq_2", "chan")
@@ -34,7 +33,7 @@
     return pltpu.with_memory_space_constraint(value, pltpu.HBM)
 
 
-def call(kernel, outs, ins, loads=(), stores=(), scratch=(), flops=0, early=False):
+def call(kernel, outs, ins, loads=(), stores=(), far=(), scratch=(), flops=0, early=False):
     count = len(ins)
 
     def wrapped(*refs):
@@ -79,7 +78,7 @@
         space = pltpu.VMEM
         if a.dtype == jnp.int32:
             space = pltpu.SMEM
-        elif k in loads:
+        elif k in loads or k in far:
             space = pltpu.HBM
             a = in_hbm(a)
         specs.append(pl.BlockSpec(memory_space=space))
@@ -105,6 +104,33 @@
     )(*values)
 
 
+def fetch(values, after=None):
+    count = len(values)
+
+    def kernel(*refs):
+        sources, outs, sems = refs[:count], refs[-1 - count : -1], refs[-1]
+        copies = [
+            pltpu.make_async_copy(source, out, sems.at[k])
+            for k, (source, out) in enumerate(zip(sources, outs))
+        ]
+        for copy in copies:
+            copy.start()
+        for copy in copies:
+            copy.wait()
+
+    extra = [] if after is None else [after]
+    return pl.pallas_call(
+        kernel,
+        out_shape=[jax.ShapeDtypeStruct(v.shape, v.dtype) for v in values],
+        in_specs=[pl.BlockSpec(memory_space=pltpu.HBM)] * count
+        + [pl.BlockSpec(memory_space=pltpu.VMEM)] * len(extra),
+        out_specs=[pl.BlockSpec(memory_space=pltpu.VMEM)] * count,
+        scratch_shapes=[pltpu.SemaphoreType.DMA((count,))],
+        compiler_params=pltpu.CompilerParams(vmem_limit_bytes=16 << 20),
+        cost_estimate=pl.CostEstimate(flops=700_000_000, transcendentals=0, bytes_accessed=4 << 20),
+    )(*[in_hbm(v) for v in values], *extra)
+
+
 def heads_to_lanes(heads, width):
     head = lax.broadcasted_iota(jnp.int32, (heads, width), 0)
     lane = lax.broadcasted_iota(jnp.int32, (heads, width), 1)
@@ -126,12 +152,6 @@
 def silu_and_slope(v):
     gate = 1.0 / (1.0 + jnp.exp(-v))
     return v * gate, gate * (1.0 + v * (1.0 - gate))
-
-
-def load_kernel(*refs):
-    half = len(refs) // 2
-    for source, out in zip(refs[:half], refs[half:]):
-        out[...] = source[...]
 
 
 def project_kernel(
@@ -271,26 +291,30 @@
     send[...] = (factor * piece.astype(F32) + keep[:, :width]).astype(BF16)
 
 
-def pack_kernel(who, x, *refs, half):
-    outs, turned_x = refs[:-1], refs[-1]
+def pack_kernel(who, x, keep, send, turned_x, *, half):
     core, place = who[1], who[2]
     model = x.shape[1]
     lines = 8
-    share = outs[0].shape[0] // lines
+    share = keep.shape[1] // lines
     for k in range(model // 128):
         lanes = slice(k * 128, (k + 1) * 128)
         turned_x[lanes, :] = x[:, lanes].astype(F32).T
+    for out, side in ((keep, core), (send, 1 - core)):
+        for steps in range(4):
+            where = lax.rem(place + steps, 4)
+            outer = where // half
+            inner = 2 * (where - outer * half) + side
+            for line in range(lines):
+                start = share * ((outer * lines + line) * 2 * half + inner)
+                out[steps, line * share : (line + 1) * share, :] = turned_x[
+                    pl.ds(pl.multiple_of(start, 8), share), :
+                ].astype(BF16)
+
+
+def join_kernel(keep, got, *outs):
     for k, out in enumerate(outs):
-        steps, flip = divmod(k, 2)
-        where = lax.rem(place + steps, 4)
-        side = core if flip == 0 else 1 - core
-        outer = where // half
-        inner = 2 * (where - outer * half) + side
-        for line in range(lines):
-            start = share * ((outer * lines + line) * 2 * half + inner)
-            out[line * share : (line + 1) * share, :] = turned_x[
-                pl.ds(pl.multiple_of(start, 8), share), :
-            ].astype(BF16)
+        out[0] = keep[k]
+        out[1] = got[k]
 
 
 def within_kernel(big, g, small, rows, u_out, row_out, col_out):
@@ -413,7 +437,7 @@
     mix_out[...] = convolved(slice(width, pre.shape[1])).astype(BF16)
 
 
-def input_grad_kernel(who, grads, mix_grads, w_in, w_mix, w_step, *refs):
+def input_grad_kernel(who, grads, mix_grads, w_mix, w_step, w_in, *refs):
     outs, whole = refs[:4], refs[4]
     width = w_in.shape[1]
     heads = w_step.shape[0]
@@ -427,6 +451,10 @@
         out[...] = whole[pl.ds(pl.multiple_of(slot * part, 16), part), :]
 
 
+def pair_add_kernel(a, b, out):
+    out[...] = (a[...].astype(F32) + b[...].astype(F32)).astype(BF16)
+
+
 def add_kernel(m0, m1, m2, m3, out):
     total = m0[...].astype(F32) + m1[...].astype(F32) + m2[...].astype(F32) + m3[...].astype(F32)
     out[...] = total.astype(BF16)
@@ -434,36 +462,33 @@
 
 def gathered_product(slabs, grads):
     total = None
-    for slab, grad in zip(slabs, grads):
-        part = dot(slab[...], grad[...])
+    for k, grad in enumerate(grads):
+        part = dot(slabs[k // 2][k % 2], grad[...])
         total = part if total is None else total + part
     return total
 
 
 def inner_weight_kernel(*refs):
-    refs[-1][...] = gathered_product(refs[:8], refs[8:16]).astype(BF16)
+    refs[-1][...] = gathered_product(refs[:4], refs[4:12]).astype(BF16)
 
 
 def mixer_weight_kernel(who, *refs):
-    slabs, grads, inner, out = refs[:8], refs[8:16], refs[16], refs[17]
+    slabs, grads, inner, out = refs[:4], refs[4:12], refs[12], refs[13]
     chan = who[0]
     lines, share, _ = out.shape
     total = gathered_product(slabs, grads).astype(BF16)
-    size = lines * share
     few = share // 4
-    to_row = lax.broadcasted_iota(jnp.int32, (size, size), 0)
-    from_row = lax.broadcasted_iota(jnp.int32, (size, size), 1)
-    within_line = to_row - (to_row // share) * share
-    group = within_line // few
-    wanted = to_row - within_line + chan * few + (within_line - group * few)
-    chosen = None
-    for q in range(4):
-        pick = ((from_row == wanted) & (group == q)).astype(BF16)
-        part = dot(pick, total[:, q * 64 : (q + 1) * 64])
-        chosen = part if chosen is None else chosen + part
+    to_row = lax.broadcasted_iota(jnp.int32, (share, 4 * share), 0)
+    source = lax.broadcasted_iota(jnp.int32, (share, 4 * share), 1)
+    group = to_row // few
+    wanted = group * share + chan * few + (to_row - group * few)
+    pick = (source == wanted).astype(BF16)
     edge = inner.shape[1] - 64
     out[:, :, :] = inner[...].reshape(out.shape)
-    out[:, :, edge:] = chosen.astype(BF16).reshape(lines, share, 64)
+    for line in range(lines):
+        piece = total[line * share : (line + 1) * share, :]
+        stacked = jnp.concatenate([piece[:, q * 64 : (q + 1) * 64] for q in range(4)], axis=0)
+        out[line, :, edge:] = dot(pick, stacked).astype(BF16)
 
 
 def total_kernel(terms, inner_out, mix_out, step_out, whole, *, norm):
@@ -488,14 +513,6 @@
 
 def a2a(value, axis):
     return lax.all_to_all(value, axis, split_axis=0, concat_axis=0, tiled=True)
-
-
-def moves(steps, flip, count):
-    return [
-        (2 * d + c, 2 * ((d + steps) % (count // 2)) + (c ^ flip))
-        for d in range(count // 2)
-        for c in range(2)
-    ]
 
 
 def turned(value, axis, steps):
@@ -547,13 +564,7 @@
     sources = [
         own, inner_weight, mixer_weight, step_weight.T, conv_inner, conv_mixer, bias, rate, g
     ]
-    near = call(
-        load_kernel,
-        [(v.shape, v.dtype) for v in sources],
-        sources,
-        loads=tuple(range(len(sources))),
-        flops=700_000_000,
-    )
+    near = fetch(sources)
     x, big, z, small, rows, keep, send, kept = call(
         project_kernel,
         [
@@ -590,20 +601,29 @@
         stores=(0, 1, 2),
         flops=700_000_000,
     )
-    group8 = lax.axis_size(ROW8)
     share = model // lax.axis_size(DP_SEQ)
     lines = lax.axis_size("seq_0")
-    slabs = call(
+    slab_shape = (lines * share, t)
+    slab_keep, slab_send = call(
         lambda *refs: pack_kernel(*refs, half=lax.axis_size("seq_1")),
-        [((lines * share, t), BF16)] * group8,
+        [((4, *slab_shape), BF16)] * 2,
         [who, x],
         loads=(1,),
+        stores=(0, 1),
         scratch=[pltpu.VMEM((model, t), F32)],
         flops=500_000_000,
     )
-    slabs = [slabs[0]] + [
-        lax.ppermute(slabs[k], ROW8, moves(k // 2, k % 2, group8)) for k in range(1, group8)
-    ]
+    slab_got = turned(slab_send, "seq_2", 1)
+    slabs = call(
+        join_kernel,
+        [((2, *slab_shape), BF16)] * 4,
+        [slab_keep, slab_got],
+        loads=(0,),
+        stores=(0,),
+        flops=500_000_000,
+    )
+    far, close, next_close = [turned(slabs[k], ROW4, k) for k in (2, 1, 3)]
+    slabs = [slabs[0], close, far, next_close]
 
     (befores,) = call(
         chain_kernel,
@@ -614,14 +634,12 @@
     befores = a2a(befores, PAIRS)
     mine, others = call(back_kernel, [((state_width, c), BF16)] * 2, [kept, befores], loads=(0,))
     others = turned(others, "seq_2", 1)
+    sources = [big, z, small, u, row_part, col_part, g, rate, skip, conv_inner, conv_mixer]
+    fetched = fetch(sources, after=mine)
     pre, head, step_grad, kernels = call(
         back_through_kernel,
         [((t, c + mixed), F32), ((8, c + mixed), F32), ((t, 128), BF16), ((4, c + mixed), F32)],
-        [
-            who, mine, others, big, z, small, u, row_part, col_part, g, rate, skip, conv_inner,
-            conv_mixer,
-        ],
-        loads=tuple(range(3, 14)),
+        [who, mine, others, *fetched],
         scratch=[pltpu.VMEM((state_width, c), BF16), pltpu.VMEM((state_width, c), BF16)],
         flops=500_000_000,
     )
@@ -634,8 +652,10 @@
     )
     far, near, next_near = [turned(grads, ROW4, k) for k in (2, 1, 3)]
     same = [grads, near, far, next_near]
-    shares = [turned(mix_grads, "chan", k) for k in (2, 1, 3)]
-    (mix_total,) = call(add_kernel, [((t, mixed), BF16)], [mix_grads, *shares])
+    mix_total = mix_grads
+    for partners in ([1, 0, 3, 2], [3, 2, 1, 0]):
+        theirs = lax.ppermute(mix_total, "chan", list(enumerate(partners)))
+        (mix_total,) = call(pair_add_kernel, [((t, mixed), BF16)], [mix_total, theirs])
     far, near, next_near = [turned(mix_total, ROW4, k) for k in (2, 1, 3)]
     mix_same = [mix_total, near, far, next_near]
     swapped = [turned(v, "seq_2", 1) for v in same]
@@ -643,8 +663,8 @@
     partial = call(
         input_grad_kernel,
         [((part, model), BF16)] * chans,
-        [who, grads, mix_grads, inner_weight, mixer_weight, step_weight.T],
-        loads=(3, 4, 5),
+        [who, grads, mix_grads, mixer_weight, step_weight.T, inner_weight],
+        stores=(0, 1, 2, 3),
         scratch=[pltpu.VMEM((tokens, model), BF16)],
         flops=500_000_000,
     )

time: 149 us -> 144 us (0.966)
  blocking collectives: 35 us -> 21.9 us
  waiting for transfers between devices: 32.3 us -> 38 us
  local copies, waits for them, and re-layouts: 0.79 us -> 5.26 us
  starting transfers between devices: 49.7 us -> 46.3 us
    all_to_all x2 -> x1, blocking collectives: 35 us -> 21.9 us  [a2a(): return lax.all_to_all(value, axis, split_axis=0, concat_axis=0, tiled=True)]
    ppermute x7 -> x2, starting transfers between devices: 7.72 us -> 0.19 us  [layer(): theirs = lax.ppermute(mix_total, 'chan', list(enumerate(partners)))]
    all_to_all x1 -> x2, waiting for transfers between devices: 0.53 us -> 5.39 us  [a2a(): return lax.all_to_all(value, axis, split_axis=0, concat_axis=0, tiled=True)]
    unnamed x0 -> x22, local copies, waits for them, and re-layouts: none -> 4.47 us
    all_to_all x1 -> x2, starting transfers between devices: 3.49 us -> 7.89 us  [a2a(): return lax.all_to_all(value, axis, split_axis=0, concat_axis=0, tiled=True)]
    pallas_call x0 -> x2, Pallas kernels: none -> 4.23 us  [fetch(): pl.pallas_call(kernel, out_shape=[jax.ShapeDtypeStruct(v.shape, v.dtype)...]
    pallas_call x15 -> x16, Pallas kernels: 29.8 us -> 26.3 us  [call(): pl.pallas_call(wrapped, out_shape=[pltpu.HBM(s, d) if k in stores else ja...]
    ppermute x7 -> x2, waiting for transfers between devices: 2.54 us -> 4.19 us  [layer(): theirs = lax.ppermute(mix_total, 'chan', list(enumerate(partners)))]
  transfers between devices with their start and end apart: 38 -> 35, of which waited for: 11 -> 11; matrix products, arithmetic and copies ran while one was open for 0% -> 0% of each run, Pallas kernels for 13% -> 15%
where the time goes in v3:
time: 144 us; the launch traced here: 143 us
  starting transfers between devices  46.3 us (32%)
  waiting for transfers between devices  38 us (26%)
  Pallas kernels  30.6 us (21%)
  blocking collectives  21.9 us (15%)
  local copies, waits for them, and re-layouts  5.26 us (4%)
    ppermute x26, starting transfers between devices, turned(): lax.ppermute(value, axis, [(k, (k + steps) % count) for k in range(count)])  32.7 us
    pallas_call x16, Pallas kernels, call(): pl.pallas_call(wrapped, out_shape=[pltpu.HBM(s, d) if k in stores else ja...  26.3 us
    all_to_all x1, blocking collectives, a2a(): return lax.all_to_all(value, axis, split_axis=0, concat_axis=0, tiled=True)  21.9 us
    ppermute x26, waiting for transfers between devices, turned(): lax.ppermute(value, axis, [(k, (k + steps) % count) for k in range(count)])  19.8 us
    all_to_all x2, starting transfers between devices, a2a(): return lax.all_to_all(value, axis, split_axis=0, concat_axis=0, tiled=True)  7.89 us
    all_to_all x2, waiting for transfers between devices, a2a(): return lax.all_to_all(value, axis, split_axis=0, concat_axis=0, tiled=True)  5.39 us
    ppermute x4, waiting for transfers between devices, layer(): lax.ppermute(tail_rows, SEQ_CHAN, [(s * chans + chans - 1, (s + 1) * chan...  4.97 us
    unnamed x22, local copies, waits for them, and re-layouts  4.47 us
  transfers between devices with their start and end apart: 35, of which 11 were waited for; matrix products, arithmetic and copies ran while one was open for 0% of the time, Pallas kernels for 15%

profile of v3, /device:TPU:1, one launch (start us, length us, event | category | flops | bytes accessed | tf_op | source)
XLA Modules:
  0.0 143.3 jit_solution(8085832328183473449)
XLA Ops:
  2.8 8.7 %collective-permute-start.2 = (bf16[32,2560]{1,0:T(8,128)(2,1)}, bf16[32,2560]{1,0:T(8,128)(2,1)S(1)}, u32[]{:S(2)}, u32[]{:S(2)}) collective-permute-start(bf16[32,2560]{1,0:T(8,128)(2,1)} %bitcast.15), channel_id=1, source_target_pairs={{0,3},{1,0},{2,1},{3,2},{4,7},{5,4},{6,5},{7,6},{8,11},{9,8},{10,9... | collective-permute-start | bytes 491528 | tf_op jit(solution)/shard_map/ppermute | solution.py:520
  14.2 2.6 %shard_map.129 = (bf16[32,2560]{1,0:T(8,128)(2,1)S(1)}, bf16[2560,640]{1,0:T(8,128)(2,1)S(1)}, bf16[2560,256]{1,0:T(8,128)(2,1)S(1)}, bf16[10,2560]{1,0:T(8,128)...) custom-call(bf16[32,2560]{1,0:T(8,128)(2,1)} %bitcast.18, ...), custom_call_target="tpu_custom_call" | custom-call | flops 700000000 | bytes 4194304 | tf_op jit(solution)/shard_map/pallas_call | solution.py:122
  16.8 5.0 %collective-permute-done.3.refs_5_ = bf16[4,2560]{1,0:T(4,128)(2,1)S(1)} collective-permute-done((bf16[4,2560]{1,0:T(4,128)(2,1)S(1)}, bf16[4,2560]{1,0:T(4,128)(2,1)S(1)}, u32[]{:S(2)}, u32[]{:S(2)}) %collective-permute-start.3) | collective-permute-done | bytes 20512 | tf_op jit(solution)/shard_map/ppermute | solution.py:557
  21.8 3.8 %shard_map.130 = (bf16[128,2560]{1,0:T(8,128)(2,1)}, f32[128,1792]{1,0:T(8,128)}, bf16[128,1280]{1,0:T(8,128)(2,1)}, f32[5,128,10]{2,1,0:T(8,128)}, f32[2,10,128...) custom-call(s32[3]{0:T(128)S(1)} %pad_add_fusion.refs_0_, ...), custom_call_target="tpu_custom_call" | custom-call | flops 700000000 | bytes 1048576 | tf_op jit(solution)/shard_map/pallas_call | solution.py:88
  27.4 21.9 %all_to_all.15.refs_1_ = bf16[16,8,768]{2,1,0:T(8,128)(2,1)S(1)} all-to-all(bf16[16,8,768]{2,1,0:T(8,128)(2,1)S(1)} %shard_map.131), channel_id=1, replica_groups=mesh['dp'=2,'seq_0'=8,'seq_1'=2,'seq_2'=2,'chan'=4] {'seq_0','seq_1'}, dimensions={0} | all-to-all | bytes 393216 | tf_op jit(solution)/shard_map/all_to_all | solution.py:515
  50.7 3.5 %all-to-all-start.1 = ((bf16[16,8,640]{2,1,0:T(8,128)(2,1)}), bf16[16,8,640]{2,1,0:T(8,128)(2,1)S(1)}, u32[]{:S(2)}, u32[]{:S(2)}) async-start(bf16[16,8,640]{2,1,0:T(8,128)(2,1)} %shard_map.132), calls=%async_computation.1 | async-start | bytes 327680 | tf_op jit(solution)/shard_map/all_to_all | solution.py:515
  54.3 2.8 %shard_map.140 = (bf16[4,320,128]{2,1,0:T(8,128)(2,1)}, bf16[4,320,128]{2,1,0:T(8,128)(2,1)}) custom-call(s32[3]{0:T(128)S(1)} %pad_add_fusion.refs_0_, bf16[128,2560]{1,0:T(8,128)(2,1)} %get-tuple-element.98.refs_1_), custom_call_target="tpu_custom_call" | custom-call | flops 500000000 | bytes 1048576 | tf_op jit(solution)/shard_map/pallas_call | solution.py:88
  57.1 2.2 %collective-permute-start.13 = (bf16[4,320,128]{2,1,0:T(8,128)(2,1)}, bf16[4,320,128]{2,1,0:T(8,128)(2,1)S(1)}, u32[]{:S(2)}, u32[]{:S(2)}) collective-permute-start(bf16[4,320,128]{2,1,0:T(8,128)(2,1)} %get-tuple-element.100), channel_id=1, source_target_pairs={{0,4},{4,0},{1,5},{5,1},{2,6},{6,2},{3,7},{7,3},{8,12},{12,8},{9,1... | collective-permute-start | bytes 983048 | tf_op jit(solution)/shard_map/ppermute | solution.py:520
  59.3 5.4 %all-to-all-done.1.refs_1_ = bf16[16,8,640]{2,1,0:T(8,128)(2,1)S(1)} async-done(((bf16[16,8,640]{2,1,0:T(8,128)(2,1)}), bf16[16,8,640]{2,1,0:T(8,128)(2,1)S(1)}, u32[]{:S(2)}, u32[]{:S(2)}) %all-to-all-start.1) | async-done | bytes 163872 | tf_op jit(solution)/shard_map/all_to_all | solution.py:515
  65.9 3.4 %collective-permute-start.8 = (bf16[128,640]{1,0:T(8,128)(2,1)S(1)}, bf16[128,640]{1,0:T(8,128)(2,1)S(1)}, u32[]{:S(2)}, u32[]{:S(2)}) collective-permute-start(bf16[128,640]{1,0:T(8,128)(2,1)S(1)} %get-tuple-element.69), channel_id=1, source_target_pairs={{0,4},{4,0},{1,5},{5,1},{2,6},{6,2},{3,7},{7,3},{8,12},{12,8},{9,1... | collective-permute-start | bytes 491528 | tf_op jit(solution)/shard_map/ppermute | solution.py:520
  69.3 3.3 %shard_map.134 = (f32[128,896]{1,0:T(8,128)}, f32[128,10]{1,0:T(8,128)}, f32[10,128]{1,0:T(8,128)}) custom-call(f32[128,1792]{1,0:T(8,128)} %get-tuple-element.70.refs_0_, bf16[128,640]{1,0:T(8,128)(2,1)} %bitcast.20, f32[5,128,10]{2,1,0:T(8,128)} %get-tuple-element.72.refs_2_, f32[2,10,128]{2,1,0:T(8,128)} %get-tuple-element.73.refs_3_), custom_call_target="tpu_custom_call" | custom-call | flops 700000000 | bytes 1048576 | tf_op jit(solution)/shard_map/pallas_call | solution.py:88
  76.3 3.1 %shard_map.136 = (f32[128,896]{1,0:T(8,128)S(1)}, f32[8,896]{1,0:T(8,128)S(1)}, bf16[128,128]{1,0:T(8,128)(2,1)S(1)}, f32[4,896]{1,0:T(4,128)S(1)}) custom-call(s32[3]{0:T(128)S(1)} %pad_add_fusion.refs_0_, bf16[128,640]{1,0:T(8,128)(2,1)S(1)} %get-tuple-element.68.refs_11_.refs_1_, bf16[128,640]{1,0:T(8,128)(2,1)S(1)} %collective-permute-done.8.refs_2_, ...), custom_call_target="tpu_custom_call" | custom-call | flops 500000000 | bytes 1048576 | tf_op jit(solution)/shard_map/pallas_call | solution.py:88
  82.5 3.7 %collective-permute-done.9.refs_1_ = f32[8,896]{1,0:T(8,128)S(1)} collective-permute-done((f32[8,896]{1,0:T(8,128)S(1)}, f32[8,896]{1,0:T(8,128)S(1)}, u32[]{:S(2)}, u32[]{:S(2)}) %collective-permute-start.9) | collective-permute-done | bytes 28704 | tf_op jit(solution)/shard_map/ppermute | solution.py:646
  86.6 3.5 %collective-permute-start.31 = (bf16[128,768]{1,0:T(8,128)(2,1)S(1)}, bf16[128,768]{1,0:T(8,128)(2,1)S(1)}, u32[]{:S(2)}, u32[]{:S(2)}) collective-permute-start(bf16[128,768]{1,0:T(8,128)(2,1)S(1)} %get-tuple-element.92.refs_1_.refs_4_), channel_id=1, source_target_pairs={{0,136},{8,0},{128,8},{136,128},{1,137},{9,1},{129,9},{137,129},{2... | collective-permute-start | bytes 589832 | tf_op jit(solution)/shard_map/ppermute | solution.py:520
  90.1 3.0 %collective-permute-start.27 = (bf16[128,768]{1,0:T(8,128)(2,1)S(1)}, bf16[128,768]{1,0:T(8,128)(2,1)S(1)}, u32[]{:S(2)}, u32[]{:S(2)}) collective-permute-start(bf16[128,768]{1,0:T(8,128)(2,1)S(1)} %get-tuple-element.92.refs_1_.refs_4_), channel_id=1, source_target_pairs={{0,8},{8,128},{128,136},{136,0},{1,9},{9,129},{129,137},{137,1},{2... | collective-permute-start | bytes 589832 | tf_op jit(solution)/shard_map/ppermute | solution.py:520
  93.7 4.2 %collective-permute-done.18.refs_1_ = bf16[128,256]{1,0:T(8,128)(2,1)S(1)} collective-permute-done((bf16[128,256]{1,0:T(8,128)(2,1)S(1)}, bf16[128,256]{1,0:T(8,128)(2,1)S(1)}, u32[]{:S(2)}, u32[]{:S(2)}) %collective-permute-start.18) | collective-permute-done | bytes 65568 | tf_op jit(solution)/shard_map/ppermute | solution.py:657
  99.5 2.4 %collective-permute-done.16.refs_3_.refs_4_ = bf16[2,320,128]{2,1,0:T(8,128)(2,1)S(1)} collective-permute-done((bf16[2,320,128]{2,1,0:T(8,128)(2,1)S(1)}, bf16[2,320,128]{2,1,0:T(8,128)(2,1)S(1)}, u32[]{:S(2)}, u32[]{:S(2)}) %collective-permute-start.16) | collective-permute-done | bytes 163872 | tf_op jit(solution)/shard_map/ppermute | solution.py:520
  103.5 3.6 %collective-permute-done.24.refs_11_ = bf16[128,256]{1,0:T(8,128)(2,1)S(1)} collective-permute-done((bf16[128,256]{1,0:T(8,128)(2,1)S(1)}, bf16[128,256]{1,0:T(8,128)(2,1)S(1)}, u32[]{:S(2)}, u32[]{:S(2)}) %collective-permute-start.24) | collective-permute-done | bytes 65568 | tf_op jit(solution)/shard_map/ppermute | solution.py:520
  108.3 3.1 %collective-permute-done.20.refs_7_ = bf16[128,256]{1,0:T(8,128)(2,1)S(1)} collective-permute-done((bf16[128,256]{1,0:T(8,128)(2,1)S(1)}, bf16[128,256]{1,0:T(8,128)(2,1)S(1)}, u32[]{:S(2)}, u32[]{:S(2)}) %collective-permute-start.20) | collective-permute-done | bytes 65568 | tf_op jit(solution)/shard_map/ppermute | solution.py:520
  111.4 2.3 %collective-permute-start.25 = (bf16[128,256]{1,0:T(8,128)(2,1)S(1)}, bf16[128,256]{1,0:T(8,128)(2,1)S(1)}, u32[]{:S(2)}, u32[]{:S(2)}) collective-permute-start(bf16[128,256]{1,0:T(8,128)(2,1)S(1)} %collective-permute-done.24.refs_11_), channel_id=1, source_target_pairs={{0,4},{4,0},{1,5},{5,1},{2,6},{6,2},{3,7},{7,3},{8,12},{12,8},{9,1... | collective-permute-start | bytes 196616 | tf_op jit(solution)/shard_map/ppermute | solution.py:520
  117.8 4.4 %all-to-all-start.2 = ((bf16[8,40,768]{2,1,0:T(8,128)(2,1)}), bf16[8,40,768]{2,1,0:T(8,128)(2,1)}, u32[]{:S(2)}, u32[]{:S(2)}) async-start(bf16[8,40,768]{2,1,0:T(8,128)(2,1)} %copy-done.2), calls=%async_computation.2 | async-start | bytes 983040 | tf_op jit(solution)/shard_map/all_to_all | solution.py:515
  125.0 3.2 %shard_map.138 = (bf16[32,2560]{1,0:T(8,128)(2,1)}, bf16[32,2560]{1,0:T(8,128)(2,1)}, bf16[32,2560]{1,0:T(8,128)(2,1)}, bf16[32,2560]{1,0:T(8,128)(2,1)}) custom-call(s32[3]{0:T(128)S(1)} %copy-done.10, bf16[128,768]{1,0:T(8,128)(2,1)S(1)} %get-tuple-element.92.refs_1_.refs_4_, bf16[128,256]{1,0:T(8,128)(2,1)S(1)} %copy-done.5, ...), custom_call_target="tpu_custom_call" | custom-call | flops 500000000 | bytes 1048576 | tf_op jit(solution)/shard_map/pallas_call | solution.py:88
  131.4 4.2 %collective-permute-done.10.refs_1_ = bf16[32,2560]{1,0:T(8,128)(2,1)S(1)} collective-permute-done((bf16[32,2560]{1,0:T(8,128)(2,1)}, bf16[32,2560]{1,0:T(8,128)(2,1)S(1)}, u32[]{:S(2)}, u32[]{:S(2)}) %collective-permute-start.10) | collective-permute-done | bytes 163872 | tf_op jit(solution)/shard_map/ppermute | solution.py:520
  135.6 4.0 %collective-permute-done.11.refs_2_ = bf16[32,2560]{1,0:T(8,128)(2,1)S(1)} collective-permute-done((bf16[32,2560]{1,0:T(8,128)(2,1)}, bf16[32,2560]{1,0:T(8,128)(2,1)S(1)}, u32[]{:S(2)}, u32[]{:S(2)}) %collective-permute-start.11) | collective-permute-done | bytes 163872 | tf_op jit(solution)/shard_map/ppermute | solution.py:520
  (89 shorter events, 34.9 us)
Async XLA Ops:
  1.4 10.8 %collective-permute-start.6 = (bf16[4,2560]{1,0:T(4,128)(2,1)S(1)}, bf16[4,2560]{1,0:T(4,128)(2,1)S(1)}, u32[]{:S(2)}, u32[]{:S(2)}) collective-permute-start(bf16[4,2560]{1,0:T(4,128)(2,1)S(1)} %slice_bitcast_fusion), channel_id=1, source_target_pairs={{3,7},{7,11},{11,15},{15,19},{19,23},{23,27},{27,31},{31,35},{35,3... | collective-permute-start | bytes 61448 | tf_op jit(solution)/shard_map/ppermute | solution.py:557
  2.1 10.8 %collective-permute-start.5 = (bf16[4,2560]{1,0:T(4,128)(2,1)S(1)}, bf16[4,2560]{1,0:T(4,128)(2,1)S(1)}, u32[]{:S(2)}, u32[]{:S(2)}) collective-permute-start(bf16[4,2560]{1,0:T(4,128)(2,1)S(1)} %slice_bitcast_fusion), channel_id=1, source_target_pairs={{3,6},{7,10},{11,14},{15,18},{19,22},{23,26},{27,30},{31,34},{35,3... | collective-permute-start | bytes 61448 | tf_op jit(solution)/shard_map/ppermute | solution.py:557
  2.8 19.0 %collective-permute-start.2 = (bf16[32,2560]{1,0:T(8,128)(2,1)}, bf16[32,2560]{1,0:T(8,128)(2,1)S(1)}, u32[]{:S(2)}, u32[]{:S(2)}) collective-permute-start(bf16[32,2560]{1,0:T(8,128)(2,1)} %bitcast.15), channel_id=1, source_target_pairs={{0,3},{1,0},{2,1},{3,2},{4,7},{5,4},{6,5},{7,6},{8,11},{9,8},{10,9... | collective-permute-start | bytes 491528 | tf_op jit(solution)/shard_map/ppermute | solution.py:520
  11.5 10.3 %collective-permute-start.1 = (bf16[32,2560]{1,0:T(8,128)(2,1)}, bf16[32,2560]{1,0:T(8,128)(2,1)S(1)}, u32[]{:S(2)}, u32[]{:S(2)}) collective-permute-start(bf16[32,2560]{1,0:T(8,128)(2,1)} %bitcast.16), channel_id=1, source_target_pairs={{0,2},{1,3},{2,0},{3,1},{4,6},{5,7},{6,4},{7,5},{8,10},{9,11},{10,... | collective-permute-start | bytes 491528 | tf_op jit(solution)/shard_map/ppermute | solution.py:520
  11.5 10.3 %collective-permute-start = (bf16[32,2560]{1,0:T(8,128)(2,1)}, bf16[32,2560]{1,0:T(8,128)(2,1)S(1)}, u32[]{:S(2)}, u32[]{:S(2)}) collective-permute-start(bf16[32,2560]{1,0:T(8,128)(2,1)} %bitcast.17), channel_id=1, source_target_pairs={{0,1},{1,2},{2,3},{3,0},{4,5},{5,6},{6,7},{7,4},{8,9},{9,10},{10,1... | collective-permute-start | bytes 491528 | tf_op jit(solution)/shard_map/ppermute | solution.py:520
  12.9 8.8 %collective-permute-start.3 = (bf16[4,2560]{1,0:T(4,128)(2,1)S(1)}, bf16[4,2560]{1,0:T(4,128)(2,1)S(1)}, u32[]{:S(2)}, u32[]{:S(2)}) collective-permute-start(bf16[4,2560]{1,0:T(4,128)(2,1)S(1)} %slice_bitcast_fusion), channel_id=1, source_target_pairs={{3,4},{7,8},{11,12},{15,16},{19,20},{23,24},{27,28},{31,32},{35,36... | collective-permute-start | bytes 61448 | tf_op jit(solution)/shard_map/ppermute | solution.py:557
  50.7 14.0 %all-to-all-start.1 = ((bf16[16,8,640]{2,1,0:T(8,128)(2,1)}), bf16[16,8,640]{2,1,0:T(8,128)(2,1)S(1)}, u32[]{:S(2)}, u32[]{:S(2)}) async-start(bf16[16,8,640]{2,1,0:T(8,128)(2,1)} %shard_map.132), calls=%async_computation.1 | async-start | bytes 327680 | tf_op jit(solution)/shard_map/all_to_all | solution.py:515
  57.1 15.5 %collective-permute-start.13 = (bf16[4,320,128]{2,1,0:T(8,128)(2,1)}, bf16[4,320,128]{2,1,0:T(8,128)(2,1)S(1)}, u32[]{:S(2)}, u32[]{:S(2)}) collective-permute-start(bf16[4,320,128]{2,1,0:T(8,128)(2,1)} %get-tuple-element.100), channel_id=1, source_target_pairs={{0,4},{4,0},{1,5},{5,1},{2,6},{6,2},{3,7},{7,3},{8,12},{12,8},{9,1... | collective-permute-start | bytes 983048 | tf_op jit(solution)/shard_map/ppermute | solution.py:520
  65.9 10.4 %collective-permute-start.8 = (bf16[128,640]{1,0:T(8,128)(2,1)S(1)}, bf16[128,640]{1,0:T(8,128)(2,1)S(1)}, u32[]{:S(2)}, u32[]{:S(2)}) collective-permute-start(bf16[128,640]{1,0:T(8,128)(2,1)S(1)} %get-tuple-element.69), channel_id=1, source_target_pairs={{0,4},{4,0},{1,5},{5,1},{2,6},{6,2},{3,7},{7,3},{8,12},{12,8},{9,1... | collective-permute-start | bytes 491528 | tf_op jit(solution)/shard_map/ppermute | solution.py:520
  74.3 18.8 %collective-permute-start.14 = (bf16[2,320,128]{2,1,0:T(8,128)(2,1)S(1)}, bf16[2,320,128]{2,1,0:T(8,128)(2,1)S(1)}, u32[]{:S(2)}, u32[]{:S(2)}) collective-permute-start(bf16[2,320,128]{2,1,0:T(8,128)(2,1)S(1)} %get-tuple-element.102), channel_id=1, source_target_pairs={{0,8},{8,128},{128,136},{136,0},{1,9},{9,129},{129,137},{137,1},{2... | collective-permute-start | bytes 491528 | tf_op jit(solution)/shard_map/ppermute | solution.py:520
  79.4 6.7 %collective-permute-start.9 = (f32[8,896]{1,0:T(8,128)S(1)}, f32[8,896]{1,0:T(8,128)S(1)}, u32[]{:S(2)}, u32[]{:S(2)}) collective-permute-start(f32[8,896]{1,0:T(8,128)S(1)} %get-tuple-element.89), channel_id=1, source_target_pairs={{4,0},{8,4},{12,8},{16,12},{20,16},{24,20},{28,24},{32,28},{36,32}... | collective-permute-start | bytes 86024 | tf_op jit(solution)/shard_map/ppermute | solution.py:646
  81.6 11.6 %collective-permute-start.15 = (bf16[2,320,128]{2,1,0:T(8,128)(2,1)S(1)}, bf16[2,320,128]{2,1,0:T(8,128)(2,1)S(1)}, u32[]{:S(2)}, u32[]{:S(2)}) collective-permute-start(bf16[2,320,128]{2,1,0:T(8,128)(2,1)S(1)} %get-tuple-element.103), channel_id=1, source_target_pairs={{0,128},{8,136},{128,0},{136,8},{1,129},{9,137},{129,1},{137,9},{2... | collective-permute-start | bytes 491528 | tf_op jit(solution)/shard_map/ppermute | solution.py:520
  86.6 11.3 %collective-permute-start.31 = (bf16[128,768]{1,0:T(8,128)(2,1)S(1)}, bf16[128,768]{1,0:T(8,128)(2,1)S(1)}, u32[]{:S(2)}, u32[]{:S(2)}) collective-permute-start(bf16[128,768]{1,0:T(8,128)(2,1)S(1)} %get-tuple-element.92.refs_1_.refs_4_), channel_id=1, source_target_pairs={{0,136},{8,0},{128,8},{136,128},{1,137},{9,1},{129,9},{137,129},{2... | collective-permute-start | bytes 589832 | tf_op jit(solution)/shard_map/ppermute | solution.py:520
  90.1 8.3 %collective-permute-start.29 = (bf16[128,768]{1,0:T(8,128)(2,1)S(1)}, bf16[128,768]{1,0:T(8,128)(2,1)S(1)}, u32[]{:S(2)}, u32[]{:S(2)}) collective-permute-start(bf16[128,768]{1,0:T(8,128)(2,1)S(1)} %get-tuple-element.92.refs_1_.refs_4_), channel_id=1, source_target_pairs={{0,128},{8,136},{128,0},{136,8},{1,129},{9,137},{129,1},{137,9},{2... | collective-permute-start | bytes 589832 | tf_op jit(solution)/shard_map/ppermute | solution.py:520
  90.1 9.3 %collective-permute-start.27 = (bf16[128,768]{1,0:T(8,128)(2,1)S(1)}, bf16[128,768]{1,0:T(8,128)(2,1)S(1)}, u32[]{:S(2)}, u32[]{:S(2)}) collective-permute-start(bf16[128,768]{1,0:T(8,128)(2,1)S(1)} %get-tuple-element.92.refs_1_.refs_4_), channel_id=1, source_target_pairs={{0,8},{8,128},{128,136},{136,0},{1,9},{9,129},{129,137},{137,1},{2... | collective-permute-start | bytes 589832 | tf_op jit(solution)/shard_map/ppermute | solution.py:520
  93.3 8.6 %collective-permute-start.16 = (bf16[2,320,128]{2,1,0:T(8,128)(2,1)S(1)}, bf16[2,320,128]{2,1,0:T(8,128)(2,1)S(1)}, u32[]{:S(2)}, u32[]{:S(2)}) collective-permute-start(bf16[2,320,128]{2,1,0:T(8,128)(2,1)S(1)} %get-tuple-element.104), channel_id=1, source_target_pairs={{0,136},{8,0},{128,8},{136,128},{1,137},{9,1},{129,9},{137,129},{2... | collective-permute-start | bytes 491528 | tf_op jit(solution)/shard_map/ppermute | solution.py:520
  97.9 15.9 %collective-permute-start.32 = (bf16[128,768]{1,0:T(8,128)(2,1)S(1)}, bf16[128,768]{1,0:T(8,128)(2,1)S(1)}, u32[]{:S(2)}, u32[]{:S(2)}) collective-permute-start(bf16[128,768]{1,0:T(8,128)(2,1)S(1)} %collective-permute-done.31.refs_10_), channel_id=1, source_target_pairs={{0,4},{4,0},{1,5},{5,1},{2,6},{6,2},{3,7},{7,3},{8,12},{12,8},{9,1... | collective-permute-start | bytes 589832 | tf_op jit(solution)/shard_map/ppermute | solution.py:520
  98.4 15.4 %collective-permute-start.30 = (bf16[128,768]{1,0:T(8,128)(2,1)S(1)}, bf16[128,768]{1,0:T(8,128)(2,1)S(1)}, u32[]{:S(2)}, u32[]{:S(2)}) collective-permute-start(bf16[128,768]{1,0:T(8,128)(2,1)S(1)} %collective-permute-done.29.refs_8_), channel_id=1, source_target_pairs={{0,4},{4,0},{1,5},{5,1},{2,6},{6,2},{3,7},{7,3},{8,12},{12,8},{9,1... | collective-permute-start | bytes 589832 | tf_op jit(solution)/shard_map/ppermute | solution.py:520
  99.4 14.9 %collective-permute-start.28 = (bf16[128,768]{1,0:T(8,128)(2,1)S(1)}, bf16[128,768]{1,0:T(8,128)(2,1)S(1)}, u32[]{:S(2)}, u32[]{:S(2)}) collective-permute-start(bf16[128,768]{1,0:T(8,128)(2,1)S(1)} %collective-permute-done.27.refs_6_), channel_id=1, source_target_pairs={{0,4},{4,0},{1,5},{5,1},{2,6},{6,2},{3,7},{7,3},{8,12},{12,8},{9,1... | collective-permute-start | bytes 589832 | tf_op jit(solution)/shard_map/ppermute | solution.py:520
  107.1 8.4 %collective-permute-start.19 = (bf16[128,256]{1,0:T(8,128)(2,1)S(1)}, bf16[128,256]{1,0:T(8,128)(2,1)S(1)}, u32[]{:S(2)}, u32[]{:S(2)}) collective-permute-start(bf16[128,256]{1,0:T(8,128)(2,1)S(1)} %shard_map.143.refs_5_), channel_id=1, source_target_pairs={{0,4},{4,0},{1,5},{5,1},{2,6},{6,2},{3,7},{7,3},{8,12},{12,8},{9,1... | collective-permute-start | bytes 196616 | tf_op jit(solution)/shard_map/ppermute | solution.py:520
  117.8 23.5 %all-to-all-start.2 = ((bf16[8,40,768]{2,1,0:T(8,128)(2,1)}), bf16[8,40,768]{2,1,0:T(8,128)(2,1)}, u32[]{:S(2)}, u32[]{:S(2)}) async-start(bf16[8,40,768]{2,1,0:T(8,128)(2,1)} %copy-done.2), calls=%async_computation.2 | async-start | bytes 983040 | tf_op jit(solution)/shard_map/all_to_all | solution.py:515
  128.1 7.5 %collective-permute-start.10 = (bf16[32,2560]{1,0:T(8,128)(2,1)}, bf16[32,2560]{1,0:T(8,128)(2,1)S(1)}, u32[]{:S(2)}, u32[]{:S(2)}) collective-permute-start(bf16[32,2560]{1,0:T(8,128)(2,1)} %get-tuple-element.95), channel_id=1, source_target_pairs={{0,2},{1,3},{2,0},{3,1},{4,6},{5,7},{6,4},{7,5},{8,10},{9,11},{10,... | collective-permute-start | bytes 491528 | tf_op jit(solution)/shard_map/ppermute | solution.py:520
  128.2 11.4 %collective-permute-start.11 = (bf16[32,2560]{1,0:T(8,128)(2,1)}, bf16[32,2560]{1,0:T(8,128)(2,1)S(1)}, u32[]{:S(2)}, u32[]{:S(2)}) collective-permute-start(bf16[32,2560]{1,0:T(8,128)(2,1)} %get-tuple-element.96), channel_id=1, source_target_pairs={{0,1},{1,2},{2,3},{3,0},{4,5},{5,6},{6,7},{7,4},{8,9},{9,10},{10,1... | collective-permute-start | bytes 491528 | tf_op jit(solution)/shard_map/ppermute | solution.py:520
  129.2 10.4 %collective-permute-start.12 = (bf16[32,2560]{1,0:T(8,128)(2,1)}, bf16[32,2560]{1,0:T(8,128)(2,1)S(1)}, u32[]{:S(2)}, u32[]{:S(2)}) collective-permute-start(bf16[32,2560]{1,0:T(8,128)(2,1)} %get-tuple-element.97), channel_id=1, source_target_pairs={{0,3},{1,0},{2,1},{3,2},{4,7},{5,4},{6,5},{7,6},{8,11},{9,8},{10,9... | collective-permute-start | bytes 491528 | tf_op jit(solution)/shard_map/ppermute | solution.py:520
  (22 other events, 271.3 us)

commit v4 on v3

--- a/solution.py
+++ b/solution.py
@@ -551,7 +551,9 @@
     seq_count = lax.axis_size(SEQ)
     t, c = tokens, width
 
-    arrived = [turned(own, "chan", k) for k in (1, 2, 3)]
+    arrived = []
+    for k in (1, 2, 3):
+        arrived.append(turned(own, "chan", k))
     tail_rows = own[part - 4 :]
     halos = [
         lax.ppermute(
@@ -623,7 +625,7 @@
         flops=500_000_000,
     )
     far, close, next_close = [turned(slabs[k], ROW4, k) for k in (2, 1, 3)]
-    slabs = [slabs[0], close, far, next_close]
+    slabs = fetch([slabs[0], close, far, next_close])
 
     (befores,) = call(
         chain_kernel,

time: 144 us -> 144 us (level)
  waiting for transfers between devices: 38 us -> 36.5 us
    pallas_call x2 -> x3, Pallas kernels: 4.23 us -> 5.42 us  [fetch(): pl.pallas_call(kernel, out_shape=[jax.ShapeDtypeStruct(v.shape, v.dtype)...]
    unnamed x22 -> x26, local copies, waits for them, and re-layouts: 4.47 us -> 4.51 us
  transfers between devices with their start and end apart: 35 -> 35, of which waited for: 11 -> 11; matrix products, arithmetic and copies ran while one was open for 0% -> 0% of each run, Pallas kernels for 15% -> 16%
where the time goes in v4:
time: 144 us; the launch traced here: 143 us
  starting transfers between devices  46.5 us (32%)
  waiting for transfers between devices  36.5 us (25%)
  Pallas kernels  31.8 us (22%)
  blocking collectives  21.9 us (15%)
  local copies, waits for them, and re-layouts  5.31 us (4%)
    ppermute x26, starting transfers between devices, turned(): lax.ppermute(value, axis, [(k, (k + steps) % count) for k in range(count)])  32.9 us
    pallas_call x16, Pallas kernels, call(): pl.pallas_call(wrapped, out_shape=[pltpu.HBM(s, d) if k in stores else ja...  26.3 us
    all_to_all x1, blocking collectives, a2a(): return lax.all_to_all(value, axis, split_axis=0, concat_axis=0, tiled=True)  21.9 us
    ppermute x26, waiting for transfers between devices, turned(): lax.ppermute(value, axis, [(k, (k + steps) % count) for k in range(count)])  18.3 us
    all_to_all x2, starting transfers between devices, a2a(): return lax.all_to_all(value, axis, split_axis=0, concat_axis=0, tiled=True)  7.87 us
    pallas_call x3, Pallas kernels, fetch(): pl.pallas_call(kernel, out_shape=[jax.ShapeDtypeStruct(v.shape, v.dtype)...  5.42 us
    all_to_all x2, waiting for transfers between devices, a2a(): return lax.all_to_all(value, axis, split_axis=0, concat_axis=0, tiled=True)  5.39 us
    ppermute x4, waiting for transfers between devices, layer(): lax.ppermute(tail_rows, SEQ_CHAN, [(s * chans + chans - 1, (s + 1) * chan...  4.97 us
  transfers between devices with their start and end apart: 35, of which 11 were waited for; matrix products, arithmetic and copies ran while one was open for 0% of the time, Pallas kernels for 16%

profile of v4, /device:TPU:1, one launch (start us, length us, event | category | flops | bytes accessed | tf_op | source)
XLA Modules:
  0.0 143.3 jit_solution(2296672420193584656)
XLA Ops:
  2.8 8.7 %collective-permute-start.2 = (bf16[32,2560]{1,0:T(8,128)(2,1)}, bf16[32,2560]{1,0:T(8,128)(2,1)S(1)}, u32[]{:S(2)}, u32[]{:S(2)}) collective-permute-start(bf16[32,2560]{1,0:T(8,128)(2,1)} %bitcast.15), channel_id=1, source_target_pairs={{0,3},{1,0},{2,1},{3,2},{4,7},{5,4},{6,5},{7,6},{8,11},{9,8},{10,9... | collective-permute-start | bytes 491528 | tf_op jit(solution)/shard_map/ppermute | solution.py:520
  14.2 2.6 %shard_map.129 = (bf16[32,2560]{1,0:T(8,128)(2,1)S(1)}, bf16[2560,640]{1,0:T(8,128)(2,1)S(1)}, bf16[2560,256]{1,0:T(8,128)(2,1)S(1)}, bf16[10,2560]{1,0:T(8,128)...) custom-call(bf16[32,2560]{1,0:T(8,128)(2,1)} %bitcast.18, ...), custom_call_target="tpu_custom_call" | custom-call | flops 700000000 | bytes 4194304 | tf_op jit(solution)/shard_map/pallas_call | solution.py:122
  16.8 5.0 %collective-permute-done.3.refs_5_ = bf16[4,2560]{1,0:T(4,128)(2,1)S(1)} collective-permute-done((bf16[4,2560]{1,0:T(4,128)(2,1)S(1)}, bf16[4,2560]{1,0:T(4,128)(2,1)S(1)}, u32[]{:S(2)}, u32[]{:S(2)}) %collective-permute-start.3) | collective-permute-done | bytes 20512 | tf_op jit(solution)/shard_map/ppermute | solution.py:559
  21.8 3.8 %shard_map.130 = (bf16[128,2560]{1,0:T(8,128)(2,1)}, f32[128,1792]{1,0:T(8,128)}, bf16[128,1280]{1,0:T(8,128)(2,1)}, f32[5,128,10]{2,1,0:T(8,128)}, f32[2,10,128...) custom-call(s32[3]{0:T(128)S(1)} %pad_add_fusion.refs_0_, ...), custom_call_target="tpu_custom_call" | custom-call | flops 700000000 | bytes 1048576 | tf_op jit(solution)/shard_map/pallas_call | solution.py:88
  27.4 21.9 %all_to_all.15.refs_1_ = bf16[16,8,768]{2,1,0:T(8,128)(2,1)S(1)} all-to-all(bf16[16,8,768]{2,1,0:T(8,128)(2,1)S(1)} %shard_map.131), channel_id=1, replica_groups=mesh['dp'=2,'seq_0'=8,'seq_1'=2,'seq_2'=2,'chan'=4] {'seq_0','seq_1'}, dimensions={0} | all-to-all | bytes 393216 | tf_op jit(solution)/shard_map/all_to_all | solution.py:515
  50.7 3.5 %all-to-all-start.1 = ((bf16[16,8,640]{2,1,0:T(8,128)(2,1)}), bf16[16,8,640]{2,1,0:T(8,128)(2,1)S(1)}, u32[]{:S(2)}, u32[]{:S(2)}) async-start(bf16[16,8,640]{2,1,0:T(8,128)(2,1)} %shard_map.132), calls=%async_computation.1 | async-start | bytes 327680 | tf_op jit(solution)/shard_map/all_to_all | solution.py:515
  54.3 2.8 %shard_map.140 = (bf16[4,320,128]{2,1,0:T(8,128)(2,1)}, bf16[4,320,128]{2,1,0:T(8,128)(2,1)}) custom-call(s32[3]{0:T(128)S(1)} %pad_add_fusion.refs_0_, bf16[128,2560]{1,0:T(8,128)(2,1)} %get-tuple-element.102.refs_1_), custom_call_target="tpu_custom_call" | custom-call | flops 500000000 | bytes 1048576 | tf_op jit(solution)/shard_map/pallas_call | solution.py:88
  57.1 2.2 %collective-permute-start.13 = (bf16[4,320,128]{2,1,0:T(8,128)(2,1)}, bf16[4,320,128]{2,1,0:T(8,128)(2,1)S(1)}, u32[]{:S(2)}, u32[]{:S(2)}) collective-permute-start(bf16[4,320,128]{2,1,0:T(8,128)(2,1)} %get-tuple-element.104), channel_id=1, source_target_pairs={{0,4},{4,0},{1,5},{5,1},{2,6},{6,2},{3,7},{7,3},{8,12},{12,8},{9,1... | collective-permute-start | bytes 983048 | tf_op jit(solution)/shard_map/ppermute | solution.py:520
  59.3 5.4 %all-to-all-done.1.refs_1_ = bf16[16,8,640]{2,1,0:T(8,128)(2,1)S(1)} async-done(((bf16[16,8,640]{2,1,0:T(8,128)(2,1)}), bf16[16,8,640]{2,1,0:T(8,128)(2,1)S(1)}, u32[]{:S(2)}, u32[]{:S(2)}) %all-to-all-start.1) | async-done | bytes 163872 | tf_op jit(solution)/shard_map/all_to_all | solution.py:515
  65.9 3.4 %collective-permute-start.8 = (bf16[128,640]{1,0:T(8,128)(2,1)S(1)}, bf16[128,640]{1,0:T(8,128)(2,1)S(1)}, u32[]{:S(2)}, u32[]{:S(2)}) collective-permute-start(bf16[128,640]{1,0:T(8,128)(2,1)S(1)} %get-tuple-element.73), channel_id=1, source_target_pairs={{0,4},{4,0},{1,5},{5,1},{2,6},{6,2},{3,7},{7,3},{8,12},{12,8},{9,1... | collective-permute-start | bytes 491528 | tf_op jit(solution)/shard_map/ppermute | solution.py:520
  69.3 3.3 %shard_map.134 = (f32[128,896]{1,0:T(8,128)}, f32[128,10]{1,0:T(8,128)}, f32[10,128]{1,0:T(8,128)}) custom-call(f32[128,1792]{1,0:T(8,128)} %get-tuple-element.74.refs_0_, bf16[128,640]{1,0:T(8,128)(2,1)} %bitcast.20, f32[5,128,10]{2,1,0:T(8,128)} %get-tuple-element.76.refs_2_, f32[2,10,128]{2,1,0:T(8,128)} %get-tuple-element.77.refs_3_), custom_call_target="tpu_custom_call" | custom-call | flops 700000000 | bytes 1048576 | tf_op jit(solution)/shard_map/pallas_call | solution.py:88
  76.4 3.1 %shard_map.136 = (f32[128,896]{1,0:T(8,128)S(1)}, f32[8,896]{1,0:T(8,128)S(1)}, bf16[128,128]{1,0:T(8,128)(2,1)S(1)}, f32[4,896]{1,0:T(4,128)S(1)}) custom-call(s32[3]{0:T(128)S(1)} %pad_add_fusion.refs_0_, bf16[128,640]{1,0:T(8,128)(2,1)S(1)} %get-tuple-element.72.refs_11_.refs_1_, bf16[128,640]{1,0:T(8,128)(2,1)S(1)} %collective-permute-done.8.refs_2_, ...), custom_call_target="tpu_custom_call" | custom-call | flops 500000000 | bytes 1048576 | tf_op jit(solution)/shard_map/pallas_call | solution.py:88
  82.5 3.7 %collective-permute-done.9.refs_1_ = f32[8,896]{1,0:T(8,128)S(1)} collective-permute-done((f32[8,896]{1,0:T(8,128)S(1)}, f32[8,896]{1,0:T(8,128)S(1)}, u32[]{:S(2)}, u32[]{:S(2)}) %collective-permute-start.9) | collective-permute-done | bytes 28704 | tf_op jit(solution)/shard_map/ppermute | solution.py:648
  86.6 3.5 %collective-permute-start.31 = (bf16[128,768]{1,0:T(8,128)(2,1)S(1)}, bf16[128,768]{1,0:T(8,128)(2,1)S(1)}, u32[]{:S(2)}, u32[]{:S(2)}) collective-permute-start(bf16[128,768]{1,0:T(8,128)(2,1)S(1)} %get-tuple-element.96.refs_1_.refs_4_), channel_id=1, source_target_pairs={{0,136},{8,0},{128,8},{136,128},{1,137},{9,1},{129,9},{137,129},{2... | collective-permute-start | bytes 589832 | tf_op jit(solution)/shard_map/ppermute | solution.py:520
  90.1 3.0 %collective-permute-start.27 = (bf16[128,768]{1,0:T(8,128)(2,1)S(1)}, bf16[128,768]{1,0:T(8,128)(2,1)S(1)}, u32[]{:S(2)}, u32[]{:S(2)}) collective-permute-start(bf16[128,768]{1,0:T(8,128)(2,1)S(1)} %get-tuple-element.96.refs_1_.refs_4_), channel_id=1, source_target_pairs={{0,8},{8,128},{128,136},{136,0},{1,9},{9,129},{129,137},{137,1},{2... | collective-permute-start | bytes 589832 | tf_op jit(solution)/shard_map/ppermute | solution.py:520
  93.7 4.2 %collective-permute-done.18.refs_1_ = bf16[128,256]{1,0:T(8,128)(2,1)S(1)} collective-permute-done((bf16[128,256]{1,0:T(8,128)(2,1)S(1)}, bf16[128,256]{1,0:T(8,128)(2,1)S(1)}, u32[]{:S(2)}, u32[]{:S(2)}) %collective-permute-start.18) | collective-permute-done | bytes 65568 | tf_op jit(solution)/shard_map/ppermute | solution.py:659
  99.5 2.4 %collective-permute-done.16.refs_3_ = bf16[2,320,128]{2,1,0:T(8,128)(2,1)S(1)} collective-permute-done((bf16[2,320,128]{2,1,0:T(8,128)(2,1)S(1)}, bf16[2,320,128]{2,1,0:T(8,128)(2,1)S(1)}, u32[]{:S(2)}, u32[]{:S(2)}) %collective-permute-start.16) | collective-permute-done | bytes 163872 | tf_op jit(solution)/shard_map/ppermute | solution.py:520
  103.5 3.6 %collective-permute-done.24.refs_11_ = bf16[128,256]{1,0:T(8,128)(2,1)S(1)} collective-permute-done((bf16[128,256]{1,0:T(8,128)(2,1)S(1)}, bf16[128,256]{1,0:T(8,128)(2,1)S(1)}, u32[]{:S(2)}, u32[]{:S(2)}) %collective-permute-start.24) | collective-permute-done | bytes 65568 | tf_op jit(solution)/shard_map/ppermute | solution.py:520
  111.4 2.3 %collective-permute-start.25 = (bf16[128,256]{1,0:T(8,128)(2,1)S(1)}, bf16[128,256]{1,0:T(8,128)(2,1)S(1)}, u32[]{:S(2)}, u32[]{:S(2)}) collective-permute-start(bf16[128,256]{1,0:T(8,128)(2,1)S(1)} %collective-permute-done.24.refs_11_), channel_id=1, source_target_pairs={{0,4},{4,0},{1,5},{5,1},{2,6},{6,2},{3,7},{7,3},{8,12},{12,8},{9,1... | collective-permute-start | bytes 196616 | tf_op jit(solution)/shard_map/ppermute | solution.py:520
  117.8 4.3 %all-to-all-start.2 = ((bf16[8,40,768]{2,1,0:T(8,128)(2,1)}), bf16[8,40,768]{2,1,0:T(8,128)(2,1)}, u32[]{:S(2)}, u32[]{:S(2)}) async-start(bf16[8,40,768]{2,1,0:T(8,128)(2,1)} %copy-done.2), calls=%async_computation.2 | async-start | bytes 983040 | tf_op jit(solution)/shard_map/all_to_all | solution.py:515
  125.0 3.1 %shard_map.138 = (bf16[32,2560]{1,0:T(8,128)(2,1)}, bf16[32,2560]{1,0:T(8,128)(2,1)}, bf16[32,2560]{1,0:T(8,128)(2,1)}, bf16[32,2560]{1,0:T(8,128)(2,1)}) custom-call(s32[3]{0:T(128)S(1)} %copy-done.9, bf16[128,768]{1,0:T(8,128)(2,1)S(1)} %get-tuple-element.96.refs_1_.refs_4_, bf16[128,256]{1,0:T(8,128)(2,1)S(1)} %copy-done.5, ...), custom_call_target="tpu_custom_call" | custom-call | flops 500000000 | bytes 1048576 | tf_op jit(solution)/shard_map/pallas_call | solution.py:88
  129.2 2.3 %collective-permute-start.12 = (bf16[32,2560]{1,0:T(8,128)(2,1)}, bf16[32,2560]{1,0:T(8,128)(2,1)S(1)}, u32[]{:S(2)}, u32[]{:S(2)}) collective-permute-start(bf16[32,2560]{1,0:T(8,128)(2,1)} %get-tuple-element.101), channel_id=1, source_target_pairs={{0,3},{1,0},{2,1},{3,2},{4,7},{5,4},{6,5},{7,6},{8,11},{9,8},{10,9... | collective-permute-start | bytes 491528 | tf_op jit(solution)/shard_map/ppermute | solution.py:520
  131.5 3.9 %collective-permute-done.10.refs_1_ = bf16[32,2560]{1,0:T(8,128)(2,1)S(1)} collective-permute-done((bf16[32,2560]{1,0:T(8,128)(2,1)}, bf16[32,2560]{1,0:T(8,128)(2,1)S(1)}, u32[]{:S(2)}, u32[]{:S(2)}) %collective-permute-start.10) | collective-permute-done | bytes 163872 | tf_op jit(solution)/shard_map/ppermute | solution.py:520
  135.4 4.2 %collective-permute-done.11.refs_2_ = bf16[32,2560]{1,0:T(8,128)(2,1)S(1)} collective-permute-done((bf16[32,2560]{1,0:T(8,128)(2,1)}, bf16[32,2560]{1,0:T(8,128)(2,1)S(1)}, u32[]{:S(2)}, u32[]{:S(2)}) %collective-permute-start.11) | collective-permute-done | bytes 163872 | tf_op jit(solution)/shard_map/ppermute | solution.py:520
  (94 shorter events, 35.9 us)
Async XLA Ops:
  1.4 10.8 %collective-permute-start.6 = (bf16[4,2560]{1,0:T(4,128)(2,1)S(1)}, bf16[4,2560]{1,0:T(4,128)(2,1)S(1)}, u32[]{:S(2)}, u32[]{:S(2)}) collective-permute-start(bf16[4,2560]{1,0:T(4,128)(2,1)S(1)} %slice_bitcast_fusion), channel_id=1, source_target_pairs={{3,7},{7,11},{11,15},{15,19},{19,23},{23,27},{27,31},{31,35},{35,3... | collective-permute-start | bytes 61448 | tf_op jit(solution)/shard_map/ppermute | solution.py:559
  2.1 10.8 %collective-permute-start.5 = (bf16[4,2560]{1,0:T(4,128)(2,1)S(1)}, bf16[4,2560]{1,0:T(4,128)(2,1)S(1)}, u32[]{:S(2)}, u32[]{:S(2)}) collective-permute-start(bf16[4,2560]{1,0:T(4,128)(2,1)S(1)} %slice_bitcast_fusion), channel_id=1, source_target_pairs={{3,6},{7,10},{11,14},{15,18},{19,22},{23,26},{27,30},{31,34},{35,3... | collective-permute-start | bytes 61448 | tf_op jit(solution)/shard_map/ppermute | solution.py:559
  2.8 19.0 %collective-permute-start.2 = (bf16[32,2560]{1,0:T(8,128)(2,1)}, bf16[32,2560]{1,0:T(8,128)(2,1)S(1)}, u32[]{:S(2)}, u32[]{:S(2)}) collective-permute-start(bf16[32,2560]{1,0:T(8,128)(2,1)} %bitcast.15), channel_id=1, source_target_pairs={{0,3},{1,0},{2,1},{3,2},{4,7},{5,4},{6,5},{7,6},{8,11},{9,8},{10,9... | collective-permute-start | bytes 491528 | tf_op jit(solution)/shard_map/ppermute | solution.py:520
  11.5 10.3 %collective-permute-start.1 = (bf16[32,2560]{1,0:T(8,128)(2,1)}, bf16[32,2560]{1,0:T(8,128)(2,1)S(1)}, u32[]{:S(2)}, u32[]{:S(2)}) collective-permute-start(bf16[32,2560]{1,0:T(8,128)(2,1)} %bitcast.16), channel_id=1, source_target_pairs={{0,2},{1,3},{2,0},{3,1},{4,6},{5,7},{6,4},{7,5},{8,10},{9,11},{10,... | collective-permute-start | bytes 491528 | tf_op jit(solution)/shard_map/ppermute | solution.py:520
  11.5 10.3 %collective-permute-start = (bf16[32,2560]{1,0:T(8,128)(2,1)}, bf16[32,2560]{1,0:T(8,128)(2,1)S(1)}, u32[]{:S(2)}, u32[]{:S(2)}) collective-permute-start(bf16[32,2560]{1,0:T(8,128)(2,1)} %bitcast.17), channel_id=1, source_target_pairs={{0,1},{1,2},{2,3},{3,0},{4,5},{5,6},{6,7},{7,4},{8,9},{9,10},{10,1... | collective-permute-start | bytes 491528 | tf_op jit(solution)/shard_map/ppermute | solution.py:520
  12.9 8.8 %collective-permute-start.3 = (bf16[4,2560]{1,0:T(4,128)(2,1)S(1)}, bf16[4,2560]{1,0:T(4,128)(2,1)S(1)}, u32[]{:S(2)}, u32[]{:S(2)}) collective-permute-start(bf16[4,2560]{1,0:T(4,128)(2,1)S(1)} %slice_bitcast_fusion), channel_id=1, source_target_pairs={{3,4},{7,8},{11,12},{15,16},{19,20},{23,24},{27,28},{31,32},{35,36... | collective-permute-start | bytes 61448 | tf_op jit(solution)/shard_map/ppermute | solution.py:559
  50.7 14.0 %all-to-all-start.1 = ((bf16[16,8,640]{2,1,0:T(8,128)(2,1)}), bf16[16,8,640]{2,1,0:T(8,128)(2,1)S(1)}, u32[]{:S(2)}, u32[]{:S(2)}) async-start(bf16[16,8,640]{2,1,0:T(8,128)(2,1)} %shard_map.132), calls=%async_computation.1 | async-start | bytes 327680 | tf_op jit(solution)/shard_map/all_to_all | solution.py:515
  57.1 15.6 %collective-permute-start.13 = (bf16[4,320,128]{2,1,0:T(8,128)(2,1)}, bf16[4,320,128]{2,1,0:T(8,128)(2,1)S(1)}, u32[]{:S(2)}, u32[]{:S(2)}) collective-permute-start(bf16[4,320,128]{2,1,0:T(8,128)(2,1)} %get-tuple-element.104), channel_id=1, source_target_pairs={{0,4},{4,0},{1,5},{5,1},{2,6},{6,2},{3,7},{7,3},{8,12},{12,8},{9,1... | collective-permute-start | bytes 983048 | tf_op jit(solution)/shard_map/ppermute | solution.py:520
  65.9 10.4 %collective-permute-start.8 = (bf16[128,640]{1,0:T(8,128)(2,1)S(1)}, bf16[128,640]{1,0:T(8,128)(2,1)S(1)}, u32[]{:S(2)}, u32[]{:S(2)}) collective-permute-start(bf16[128,640]{1,0:T(8,128)(2,1)S(1)} %get-tuple-element.73), channel_id=1, source_target_pairs={{0,4},{4,0},{1,5},{5,1},{2,6},{6,2},{3,7},{7,3},{8,12},{12,8},{9,1... | collective-permute-start | bytes 491528 | tf_op jit(solution)/shard_map/ppermute | solution.py:520
  74.3 18.8 %collective-permute-start.14 = (bf16[2,320,128]{2,1,0:T(8,128)(2,1)S(1)}, bf16[2,320,128]{2,1,0:T(8,128)(2,1)S(1)}, u32[]{:S(2)}, u32[]{:S(2)}) collective-permute-start(bf16[2,320,128]{2,1,0:T(8,128)(2,1)S(1)} %get-tuple-element.106), channel_id=1, source_target_pairs={{0,8},{8,128},{128,136},{136,0},{1,9},{9,129},{129,137},{137,1},{2... | collective-permute-start | bytes 491528 | tf_op jit(solution)/shard_map/ppermute | solution.py:520
  79.4 6.7 %collective-permute-start.9 = (f32[8,896]{1,0:T(8,128)S(1)}, f32[8,896]{1,0:T(8,128)S(1)}, u32[]{:S(2)}, u32[]{:S(2)}) collective-permute-start(f32[8,896]{1,0:T(8,128)S(1)} %get-tuple-element.93), channel_id=1, source_target_pairs={{4,0},{8,4},{12,8},{16,12},{20,16},{24,20},{28,24},{32,28},{36,32}... | collective-permute-start | bytes 86024 | tf_op jit(solution)/shard_map/ppermute | solution.py:648
  81.6 11.6 %collective-permute-start.15 = (bf16[2,320,128]{2,1,0:T(8,128)(2,1)S(1)}, bf16[2,320,128]{2,1,0:T(8,128)(2,1)S(1)}, u32[]{:S(2)}, u32[]{:S(2)}) collective-permute-start(bf16[2,320,128]{2,1,0:T(8,128)(2,1)S(1)} %get-tuple-element.107), channel_id=1, source_target_pairs={{0,128},{8,136},{128,0},{136,8},{1,129},{9,137},{129,1},{137,9},{2... | collective-permute-start | bytes 491528 | tf_op jit(solution)/shard_map/ppermute | solution.py:520
  86.6 11.2 %collective-permute-start.31 = (bf16[128,768]{1,0:T(8,128)(2,1)S(1)}, bf16[128,768]{1,0:T(8,128)(2,1)S(1)}, u32[]{:S(2)}, u32[]{:S(2)}) collective-permute-start(bf16[128,768]{1,0:T(8,128)(2,1)S(1)} %get-tuple-element.96.refs_1_.refs_4_), channel_id=1, source_target_pairs={{0,136},{8,0},{128,8},{136,128},{1,137},{9,1},{129,9},{137,129},{2... | collective-permute-start | bytes 589832 | tf_op jit(solution)/shard_map/ppermute | solution.py:520
  90.1 8.3 %collective-permute-start.29 = (bf16[128,768]{1,0:T(8,128)(2,1)S(1)}, bf16[128,768]{1,0:T(8,128)(2,1)S(1)}, u32[]{:S(2)}, u32[]{:S(2)}) collective-permute-start(bf16[128,768]{1,0:T(8,128)(2,1)S(1)} %get-tuple-element.96.refs_1_.refs_4_), channel_id=1, source_target_pairs={{0,128},{8,136},{128,0},{136,8},{1,129},{9,137},{129,1},{137,9},{2... | collective-permute-start | bytes 589832 | tf_op jit(solution)/shard_map/ppermute | solution.py:520
  90.1 9.3 %collective-permute-start.27 = (bf16[128,768]{1,0:T(8,128)(2,1)S(1)}, bf16[128,768]{1,0:T(8,128)(2,1)S(1)}, u32[]{:S(2)}, u32[]{:S(2)}) collective-permute-start(bf16[128,768]{1,0:T(8,128)(2,1)S(1)} %get-tuple-element.96.refs_1_.refs_4_), channel_id=1, source_target_pairs={{0,8},{8,128},{128,136},{136,0},{1,9},{9,129},{129,137},{137,1},{2... | collective-permute-start | bytes 589832 | tf_op jit(solution)/shard_map/ppermute | solution.py:520
  93.3 8.6 %collective-permute-start.16 = (bf16[2,320,128]{2,1,0:T(8,128)(2,1)S(1)}, bf16[2,320,128]{2,1,0:T(8,128)(2,1)S(1)}, u32[]{:S(2)}, u32[]{:S(2)}) collective-permute-start(bf16[2,320,128]{2,1,0:T(8,128)(2,1)S(1)} %get-tuple-element.108), channel_id=1, source_target_pairs={{0,136},{8,0},{128,8},{136,128},{1,137},{9,1},{129,9},{137,129},{2... | collective-permute-start | bytes 491528 | tf_op jit(solution)/shard_map/ppermute | solution.py:520
  97.8 15.9 %collective-permute-start.32 = (bf16[128,768]{1,0:T(8,128)(2,1)S(1)}, bf16[128,768]{1,0:T(8,128)(2,1)S(1)}, u32[]{:S(2)}, u32[]{:S(2)}) collective-permute-start(bf16[128,768]{1,0:T(8,128)(2,1)S(1)} %collective-permute-done.31.refs_10_), channel_id=1, source_target_pairs={{0,4},{4,0},{1,5},{5,1},{2,6},{6,2},{3,7},{7,3},{8,12},{12,8},{9,1... | collective-permute-start | bytes 589832 | tf_op jit(solution)/shard_map/ppermute | solution.py:520
  98.4 15.4 %collective-permute-start.30 = (bf16[128,768]{1,0:T(8,128)(2,1)S(1)}, bf16[128,768]{1,0:T(8,128)(2,1)S(1)}, u32[]{:S(2)}, u32[]{:S(2)}) collective-permute-start(bf16[128,768]{1,0:T(8,128)(2,1)S(1)} %collective-permute-done.29.refs_8_), channel_id=1, source_target_pairs={{0,4},{4,0},{1,5},{5,1},{2,6},{6,2},{3,7},{7,3},{8,12},{12,8},{9,1... | collective-permute-start | bytes 589832 | tf_op jit(solution)/shard_map/ppermute | solution.py:520
  99.4 14.9 %collective-permute-start.28 = (bf16[128,768]{1,0:T(8,128)(2,1)S(1)}, bf16[128,768]{1,0:T(8,128)(2,1)S(1)}, u32[]{:S(2)}, u32[]{:S(2)}) collective-permute-start(bf16[128,768]{1,0:T(8,128)(2,1)S(1)} %collective-permute-done.27.refs_6_), channel_id=1, source_target_pairs={{0,4},{4,0},{1,5},{5,1},{2,6},{6,2},{3,7},{7,3},{8,12},{12,8},{9,1... | collective-permute-start | bytes 589832 | tf_op jit(solution)/shard_map/ppermute | solution.py:520
  108.4 7.1 %collective-permute-start.19 = (bf16[128,256]{1,0:T(8,128)(2,1)S(1)}, bf16[128,256]{1,0:T(8,128)(2,1)S(1)}, u32[]{:S(2)}, u32[]{:S(2)}) collective-permute-start(bf16[128,256]{1,0:T(8,128)(2,1)S(1)} %shard_map.144.refs_5_), channel_id=1, source_target_pairs={{0,4},{4,0},{1,5},{5,1},{2,6},{6,2},{3,7},{7,3},{8,12},{12,8},{9,1... | collective-permute-start | bytes 196616 | tf_op jit(solution)/shard_map/ppermute | solution.py:520
  117.8 23.5 %all-to-all-start.2 = ((bf16[8,40,768]{2,1,0:T(8,128)(2,1)}), bf16[8,40,768]{2,1,0:T(8,128)(2,1)}, u32[]{:S(2)}, u32[]{:S(2)}) async-start(bf16[8,40,768]{2,1,0:T(8,128)(2,1)} %copy-done.2), calls=%async_computation.2 | async-start | bytes 983040 | tf_op jit(solution)/shard_map/all_to_all | solution.py:515
  128.1 7.3 %collective-permute-start.10 = (bf16[32,2560]{1,0:T(8,128)(2,1)}, bf16[32,2560]{1,0:T(8,128)(2,1)S(1)}, u32[]{:S(2)}, u32[]{:S(2)}) collective-permute-start(bf16[32,2560]{1,0:T(8,128)(2,1)} %get-tuple-element.99), channel_id=1, source_target_pairs={{0,2},{1,3},{2,0},{3,1},{4,6},{5,7},{6,4},{7,5},{8,10},{9,11},{10,... | collective-permute-start | bytes 491528 | tf_op jit(solution)/shard_map/ppermute | solution.py:520
  128.2 11.3 %collective-permute-start.11 = (bf16[32,2560]{1,0:T(8,128)(2,1)}, bf16[32,2560]{1,0:T(8,128)(2,1)S(1)}, u32[]{:S(2)}, u32[]{:S(2)}) collective-permute-start(bf16[32,2560]{1,0:T(8,128)(2,1)} %get-tuple-element.100), channel_id=1, source_target_pairs={{0,1},{1,2},{2,3},{3,0},{4,5},{5,6},{6,7},{7,4},{8,9},{9,10},{10,1... | collective-permute-start | bytes 491528 | tf_op jit(solution)/shard_map/ppermute | solution.py:520
  129.2 10.4 %collective-permute-start.12 = (bf16[32,2560]{1,0:T(8,128)(2,1)}, bf16[32,2560]{1,0:T(8,128)(2,1)S(1)}, u32[]{:S(2)}, u32[]{:S(2)}) collective-permute-start(bf16[32,2560]{1,0:T(8,128)(2,1)} %get-tuple-element.101), channel_id=1, source_target_pairs={{0,3},{1,0},{2,1},{3,2},{4,7},{5,4},{6,5},{7,6},{8,11},{9,8},{10,9... | collective-permute-start | bytes 491528 | tf_op jit(solution)/shard_map/ppermute | solution.py:520
  (24 other events, 235.2 us)

commit v5 on v4

--- a/solution.py
+++ b/solution.py
@@ -189,11 +189,11 @@
         return total
 
     inner_act, inner_slope = silu_and_slope(convolved(pi, k_in))
-    big[:, :width] = inner_act
-    big[:, width : 2 * width] = inner_slope
+    big[:, :width] = inner_act.astype(BF16)
+    big[:, width : 2 * width] = inner_slope.astype(BF16)
     mix_act, mixer_slope = silu_and_slope(convolved(pm, k_mix))
-    big[:, 2 * width : 2 * width + mixed] = mix_act
-    big[:, 2 * width + mixed :] = mixer_slope
+    big[:, 2 * width : 2 * width + mixed] = mix_act.astype(BF16)
+    big[:, 2 * width + mixed :] = mixer_slope.astype(BF16)
     flush(1)
 
     step = jnp.maximum(raw, 0.0) + jnp.log1p(jnp.exp(-jnp.abs(raw)))
@@ -321,15 +321,15 @@
     tokens, width = g.shape
     mixed = (big.shape[1] - 2 * width) // 2
     state_width = mixed // 2
-    into = big[:, 2 * width : 2 * width + state_width].astype(BF16)
-    out_of = big[:, 2 * width + state_width : 2 * width + mixed].astype(BF16)
+    into = big[:, 2 * width : 2 * width + state_width]
+    out_of = big[:, 2 * width + state_width : 2 * width + mixed]
     scores = dot(out_of, into, 1, 1)
     causal = lower(tokens)
     lane = lax.broadcasted_iota(jnp.int32, (tokens, 128), 1)
     pull = jnp.zeros((tokens, tokens), F32)
     for pair in range(width // 128):
         lanes = slice(pair * 128, (pair + 1) * 128)
-        x_pair = big[:, lanes].astype(BF16)
+        x_pair = big[:, lanes]
         g_pair = g[:, lanes]
         u_pair = jnp.zeros((tokens, 128), F32)
         for half in range(2):
@@ -370,8 +370,8 @@
         s0[...] = other[...]
         gt[...] = own[...]
 
-    into = big[:, 2 * width : 2 * width + state_width].astype(BF16)
-    out_of = big[:, 2 * width + state_width : 2 * width + mixed].astype(BF16)
+    into = big[:, 2 * width : 2 * width + state_width]
+    out_of = big[:, 2 * width + state_width : 2 * width + mixed]
     zs = z[:, :width]
     zg = z[:, width:]
     gb = dot(into, gt[...])
@@ -384,10 +384,10 @@
         jnp.concatenate([step, small[3], skip_rows], axis=0), spread, precision=HIGHEST
     )
     tail_gb = wide[tokens : 2 * tokens] * gb
-    x = big[:, :width]
+    x = big[:, :width].astype(F32)
     upstream = g[...].astype(F32)
     d_act = wide[:tokens] * (u[:, :width] + tail_gb) + wide[2 * tokens : 2 * tokens + 1] * upstream
-    d_pre = d_act * big[:, width : 2 * width]
+    d_pre = d_act * big[:, width : 2 * width].astype(F32)
     pre_out[:, :width] = d_pre
     cross = jnp.sum(gt[...].astype(F32) * s0[...].astype(F32), axis=0, keepdims=True)
     sums = dot(
@@ -413,8 +413,8 @@
     d_into = u[:, width : width + state_width] + dot(zs, gt[...], 1, 1)
     d_out_of = u[:, width + state_width :] + dot(zg, s0[...], 1, 1)
     slopes = 2 * width + mixed
-    pre_out[:, width : width + state_width] = d_into * big[:, slopes : slopes + state_width]
-    pre_out[:, width + state_width :] = d_out_of * big[:, slopes + state_width :]
+    pre_out[:, width : width + state_width] = d_into * big[:, slopes : slopes + state_width].astype(F32)
+    pre_out[:, width + state_width :] = d_out_of * big[:, slopes + state_width :].astype(F32)
     head_out[...] = pre_out[0:8, :]
     k_out[:, :width] = k_in[...]
     k_out[:, width:] = k_mix[...]
@@ -571,7 +571,7 @@
         project_kernel,
         [
             ((t, model), BF16),
-            ((t, 2 * c + 2 * mixed), F32),
+            ((t, 2 * c + 2 * mixed), BF16),
             ((t, 2 * c), BF16),
             ((5, t, heads), F32),
             ((2, heads, t), F32),

time: 144 us -> 144 us (level)
  no operation moved by 1% of the time
where the time goes in v5:
time: 144 us; the launch traced here: 143 us
  starting transfers between devices  46.5 us (32%)
  waiting for transfers between devices  36.5 us (25%)
  Pallas kernels  31.5 us (22%)
  blocking collectives  21.9 us (15%)
  local copies, waits for them, and re-layouts  5.36 us (4%)
    ppermute x26, starting transfers between devices, turned(): lax.ppermute(value, axis, [(k, (k + steps) % count) for k in range(count)])  32.9 us
    pallas_call x16, Pallas kernels, call(): pl.pallas_call(wrapped, out_shape=[pltpu.HBM(s, d) if k in stores else ja...  26.2 us
    all_to_all x1, blocking collectives, a2a(): return lax.all_to_all(value, axis, split_axis=0, concat_axis=0, tiled=True)  21.9 us
    ppermute x26, waiting for transfers between devices, turned(): lax.ppermute(value, axis, [(k, (k + steps) % count) for k in range(count)])  18.3 us
    all_to_all x2, starting transfers between devices, a2a(): return lax.all_to_all(value, axis, split_axis=0, concat_axis=0, tiled=True)  7.87 us
    all_to_all x2, waiting for transfers between devices, a2a(): return lax.all_to_all(value, axis, split_axis=0, concat_axis=0, tiled=True)  5.4 us
    pallas_call x3, Pallas kernels, fetch(): pl.pallas_call(kernel, out_shape=[jax.ShapeDtypeStruct(v.shape, v.dtype)...  5.28 us
    ppermute x4, waiting for transfers between devices, layer(): lax.ppermute(tail_rows, SEQ_CHAN, [(s * chans + chans - 1, (s + 1) * chan...  4.97 us
  transfers between devices with their start and end apart: 35, of which 11 were waited for; matrix products, arithmetic and copies ran while one was open for 0% of the time, Pallas kernels for 16%

profile of v5, /device:TPU:1, one launch (start us, length us, event | category | flops | bytes accessed | tf_op | source)
XLA Modules:
  0.0 143.1 jit_solution(924014712436614965)
XLA Ops:
  2.8 8.7 %collective-permute-start.2 = (bf16[32,2560]{1,0:T(8,128)(2,1)}, bf16[32,2560]{1,0:T(8,128)(2,1)S(1)}, u32[]{:S(2)}, u32[]{:S(2)}) collective-permute-start(bf16[32,2560]{1,0:T(8,128)(2,1)} %bitcast.15), channel_id=1, source_target_pairs={{0,3},{1,0},{2,1},{3,2},{4,7},{5,4},{6,5},{7,6},{8,11},{9,8},{10,9... | collective-permute-start | bytes 491528 | tf_op jit(solution)/shard_map/ppermute | solution.py:520
  14.2 2.6 %shard_map.129 = (bf16[32,2560]{1,0:T(8,128)(2,1)S(1)}, bf16[2560,640]{1,0:T(8,128)(2,1)S(1)}, bf16[2560,256]{1,0:T(8,128)(2,1)S(1)}, bf16[10,2560]{1,0:T(8,128)...) custom-call(bf16[32,2560]{1,0:T(8,128)(2,1)} %bitcast.18, ...), custom_call_target="tpu_custom_call" | custom-call | flops 700000000 | bytes 4194304 | tf_op jit(solution)/shard_map/pallas_call | solution.py:122
  16.8 5.0 %collective-permute-done.3.refs_5_ = bf16[4,2560]{1,0:T(4,128)(2,1)S(1)} collective-permute-done((bf16[4,2560]{1,0:T(4,128)(2,1)S(1)}, bf16[4,2560]{1,0:T(4,128)(2,1)S(1)}, u32[]{:S(2)}, u32[]{:S(2)}) %collective-permute-start.3) | collective-permute-done | bytes 20512 | tf_op jit(solution)/shard_map/ppermute | solution.py:559
  21.8 3.8 %shard_map.130 = (bf16[128,2560]{1,0:T(8,128)(2,1)}, bf16[128,1792]{1,0:T(8,128)(2,1)}, bf16[128,1280]{1,0:T(8,128)(2,1)}, f32[5,128,10]{2,1,0:T(8,128)}, f32[2,...) custom-call(s32[3]{0:T(128)S(1)} %pad_add_fusion.refs_0_, ...), custom_call_target="tpu_custom_call" | custom-call | flops 700000000 | bytes 1048576 | tf_op jit(solution)/shard_map/pallas_call | solution.py:88
  27.4 21.9 %all_to_all.15.refs_1_ = bf16[16,8,768]{2,1,0:T(8,128)(2,1)S(1)} all-to-all(bf16[16,8,768]{2,1,0:T(8,128)(2,1)S(1)} %shard_map.131), channel_id=1, replica_groups=mesh['dp'=2,'seq_0'=8,'seq_1'=2,'seq_2'=2,'chan'=4] {'seq_0','seq_1'}, dimensions={0} | all-to-all | bytes 393216 | tf_op jit(solution)/shard_map/all_to_all | solution.py:515
  50.7 3.5 %all-to-all-start.1 = ((bf16[16,8,640]{2,1,0:T(8,128)(2,1)}), bf16[16,8,640]{2,1,0:T(8,128)(2,1)S(1)}, u32[]{:S(2)}, u32[]{:S(2)}) async-start(bf16[16,8,640]{2,1,0:T(8,128)(2,1)} %shard_map.132), calls=%async_computation.1 | async-start | bytes 327680 | tf_op jit(solution)/shard_map/all_to_all | solution.py:515
  54.3 2.8 %shard_map.140 = (bf16[4,320,128]{2,1,0:T(8,128)(2,1)}, bf16[4,320,128]{2,1,0:T(8,128)(2,1)}) custom-call(s32[3]{0:T(128)S(1)} %pad_add_fusion.refs_0_, bf16[128,2560]{1,0:T(8,128)(2,1)} %get-tuple-element.102.refs_1_), custom_call_target="tpu_custom_call" | custom-call | flops 500000000 | bytes 1048576 | tf_op jit(solution)/shard_map/pallas_call | solution.py:88
  57.1 2.2 %collective-permute-start.13 = (bf16[4,320,128]{2,1,0:T(8,128)(2,1)}, bf16[4,320,128]{2,1,0:T(8,128)(2,1)S(1)}, u32[]{:S(2)}, u32[]{:S(2)}) collective-permute-start(bf16[4,320,128]{2,1,0:T(8,128)(2,1)} %get-tuple-element.104), channel_id=1, source_target_pairs={{0,4},{4,0},{1,5},{5,1},{2,6},{6,2},{3,7},{7,3},{8,12},{12,8},{9,1... | collective-permute-start | bytes 983048 | tf_op jit(solution)/shard_map/ppermute | solution.py:520
  59.3 5.4 %all-to-all-done.1.refs_1_ = bf16[16,8,640]{2,1,0:T(8,128)(2,1)S(1)} async-done(((bf16[16,8,640]{2,1,0:T(8,128)(2,1)}), bf16[16,8,640]{2,1,0:T(8,128)(2,1)S(1)}, u32[]{:S(2)}, u32[]{:S(2)}) %all-to-all-start.1) | async-done | bytes 163872 | tf_op jit(solution)/shard_map/all_to_all | solution.py:515
  65.9 3.4 %collective-permute-start.8 = (bf16[128,640]{1,0:T(8,128)(2,1)S(1)}, bf16[128,640]{1,0:T(8,128)(2,1)S(1)}, u32[]{:S(2)}, u32[]{:S(2)}) collective-permute-start(bf16[128,640]{1,0:T(8,128)(2,1)S(1)} %get-tuple-element.73), channel_id=1, source_target_pairs={{0,4},{4,0},{1,5},{5,1},{2,6},{6,2},{3,7},{7,3},{8,12},{12,8},{9,1... | collective-permute-start | bytes 491528 | tf_op jit(solution)/shard_map/ppermute | solution.py:520
  69.3 3.2 %shard_map.134 = (f32[128,896]{1,0:T(8,128)}, f32[128,10]{1,0:T(8,128)}, f32[10,128]{1,0:T(8,128)}) custom-call(bf16[128,1792]{1,0:T(8,128)(2,1)} %get-tuple-element.74.refs_0_, bf16[128,640]{1,0:T(8,128)(2,1)} %bitcast.20, f32[5,128,10]{2,1,0:T(8,128)} %get-tuple-element.76.refs_2_, f32[2,10,128]{2,1,0:T(8,128)} %get-tuple-element.77.refs_3_), custom_call_target="tpu_custom_call" | custom-call | flops 700000000 | bytes 1048576 | tf_op jit(solution)/shard_map/pallas_call | solution.py:88
  76.1 3.1 %shard_map.136 = (f32[128,896]{1,0:T(8,128)S(1)}, f32[8,896]{1,0:T(8,128)S(1)}, bf16[128,128]{1,0:T(8,128)(2,1)S(1)}, f32[4,896]{1,0:T(4,128)S(1)}) custom-call(s32[3]{0:T(128)S(1)} %pad_add_fusion.refs_0_, bf16[128,640]{1,0:T(8,128)(2,1)S(1)} %get-tuple-element.72.refs_11_.refs_1_, bf16[128,640]{1,0:T(8,128)(2,1)S(1)} %collective-permute-done.8.refs_2_, ...), custom_call_target="tpu_custom_call" | custom-call | flops 500000000 | bytes 1048576 | tf_op jit(solution)/shard_map/pallas_call | solution.py:88
  82.2 3.6 %collective-permute-done.9.refs_1_ = f32[8,896]{1,0:T(8,128)S(1)} collective-permute-done((f32[8,896]{1,0:T(8,128)S(1)}, f32[8,896]{1,0:T(8,128)S(1)}, u32[]{:S(2)}, u32[]{:S(2)}) %collective-permute-start.9) | collective-permute-done | bytes 28704 | tf_op jit(solution)/shard_map/ppermute | solution.py:648
  86.4 3.5 %collective-permute-start.31 = (bf16[128,768]{1,0:T(8,128)(2,1)S(1)}, bf16[128,768]{1,0:T(8,128)(2,1)S(1)}, u32[]{:S(2)}, u32[]{:S(2)}) collective-permute-start(bf16[128,768]{1,0:T(8,128)(2,1)S(1)} %get-tuple-element.96.refs_1_.refs_4_), channel_id=1, source_target_pairs={{0,136},{8,0},{128,8},{136,128},{1,137},{9,1},{129,9},{137,129},{2... | collective-permute-start | bytes 589832 | tf_op jit(solution)/shard_map/ppermute | solution.py:520
  89.9 3.0 %collective-permute-start.27 = (bf16[128,768]{1,0:T(8,128)(2,1)S(1)}, bf16[128,768]{1,0:T(8,128)(2,1)S(1)}, u32[]{:S(2)}, u32[]{:S(2)}) collective-permute-start(bf16[128,768]{1,0:T(8,128)(2,1)S(1)} %get-tuple-element.96.refs_1_.refs_4_), channel_id=1, source_target_pairs={{0,8},{8,128},{128,136},{136,0},{1,9},{9,129},{129,137},{137,1},{2... | collective-permute-start | bytes 589832 | tf_op jit(solution)/shard_map/ppermute | solution.py:520
  93.4 4.2 %collective-permute-done.18.refs_1_ = bf16[128,256]{1,0:T(8,128)(2,1)S(1)} collective-permute-done((bf16[128,256]{1,0:T(8,128)(2,1)S(1)}, bf16[128,256]{1,0:T(8,128)(2,1)S(1)}, u32[]{:S(2)}, u32[]{:S(2)}) %collective-permute-start.18) | collective-permute-done | bytes 65568 | tf_op jit(solution)/shard_map/ppermute | solution.py:659
  99.2 2.4 %collective-permute-done.16.refs_3_ = bf16[2,320,128]{2,1,0:T(8,128)(2,1)S(1)} collective-permute-done((bf16[2,320,128]{2,1,0:T(8,128)(2,1)S(1)}, bf16[2,320,128]{2,1,0:T(8,128)(2,1)S(1)}, u32[]{:S(2)}, u32[]{:S(2)}) %collective-permute-start.16) | collective-permute-done | bytes 163872 | tf_op jit(solution)/shard_map/ppermute | solution.py:520
  103.3 3.6 %collective-permute-done.24.refs_11_ = bf16[128,256]{1,0:T(8,128)(2,1)S(1)} collective-permute-done((bf16[128,256]{1,0:T(8,128)(2,1)S(1)}, bf16[128,256]{1,0:T(8,128)(2,1)S(1)}, u32[]{:S(2)}, u32[]{:S(2)}) %collective-permute-start.24) | collective-permute-done | bytes 65568 | tf_op jit(solution)/shard_map/ppermute | solution.py:520
  111.2 2.3 %collective-permute-start.25 = (bf16[128,256]{1,0:T(8,128)(2,1)S(1)}, bf16[128,256]{1,0:T(8,128)(2,1)S(1)}, u32[]{:S(2)}, u32[]{:S(2)}) collective-permute-start(bf16[128,256]{1,0:T(8,128)(2,1)S(1)} %collective-permute-done.24.refs_11_), channel_id=1, source_target_pairs={{0,4},{4,0},{1,5},{5,1},{2,6},{6,2},{3,7},{7,3},{8,12},{12,8},{9,1... | collective-permute-start | bytes 196616 | tf_op jit(solution)/shard_map/ppermute | solution.py:520
  117.6 4.3 %all-to-all-start.2 = ((bf16[8,40,768]{2,1,0:T(8,128)(2,1)}), bf16[8,40,768]{2,1,0:T(8,128)(2,1)}, u32[]{:S(2)}, u32[]{:S(2)}) async-start(bf16[8,40,768]{2,1,0:T(8,128)(2,1)} %copy-done.2), calls=%async_computation.2 | async-start | bytes 983040 | tf_op jit(solution)/shard_map/all_to_all | solution.py:515
  124.8 3.1 %shard_map.138 = (bf16[32,2560]{1,0:T(8,128)(2,1)}, bf16[32,2560]{1,0:T(8,128)(2,1)}, bf16[32,2560]{1,0:T(8,128)(2,1)}, bf16[32,2560]{1,0:T(8,128)(2,1)}) custom-call(s32[3]{0:T(128)S(1)} %copy-done.9, bf16[128,768]{1,0:T(8,128)(2,1)S(1)} %get-tuple-element.96.refs_1_.refs_4_, bf16[128,256]{1,0:T(8,128)(2,1)S(1)} %copy-done.5, ...), custom_call_target="tpu_custom_call" | custom-call | flops 500000000 | bytes 1048576 | tf_op jit(solution)/shard_map/pallas_call | solution.py:88
  129.0 2.3 %collective-permute-start.12 = (bf16[32,2560]{1,0:T(8,128)(2,1)}, bf16[32,2560]{1,0:T(8,128)(2,1)S(1)}, u32[]{:S(2)}, u32[]{:S(2)}) collective-permute-start(bf16[32,2560]{1,0:T(8,128)(2,1)} %get-tuple-element.101), channel_id=1, source_target_pairs={{0,3},{1,0},{2,1},{3,2},{4,7},{5,4},{6,5},{7,6},{8,11},{9,8},{10,9... | collective-permute-start | bytes 491528 | tf_op jit(solution)/shard_map/ppermute | solution.py:520
  131.3 3.9 %collective-permute-done.10.refs_1_ = bf16[32,2560]{1,0:T(8,128)(2,1)S(1)} collective-permute-done((bf16[32,2560]{1,0:T(8,128)(2,1)}, bf16[32,2560]{1,0:T(8,128)(2,1)S(1)}, u32[]{:S(2)}, u32[]{:S(2)}) %collective-permute-start.10) | collective-permute-done | bytes 163872 | tf_op jit(solution)/shard_map/ppermute | solution.py:520
  135.2 4.2 %collective-permute-done.11.refs_2_ = bf16[32,2560]{1,0:T(8,128)(2,1)S(1)} collective-permute-done((bf16[32,2560]{1,0:T(8,128)(2,1)}, bf16[32,2560]{1,0:T(8,128)(2,1)S(1)}, u32[]{:S(2)}, u32[]{:S(2)}) %collective-permute-start.11) | collective-permute-done | bytes 163872 | tf_op jit(solution)/shard_map/ppermute | solution.py:520
  (94 shorter events, 35.8 us)
Async XLA Ops:
  1.4 10.8 %collective-permute-start.6 = (bf16[4,2560]{1,0:T(4,128)(2,1)S(1)}, bf16[4,2560]{1,0:T(4,128)(2,1)S(1)}, u32[]{:S(2)}, u32[]{:S(2)}) collective-permute-start(bf16[4,2560]{1,0:T(4,128)(2,1)S(1)} %slice_bitcast_fusion), channel_id=1, source_target_pairs={{3,7},{7,11},{11,15},{15,19},{19,23},{23,27},{27,31},{31,35},{35,3... | collective-permute-start | bytes 61448 | tf_op jit(solution)/shard_map/ppermute | solution.py:559
  2.1 10.8 %collective-permute-start.5 = (bf16[4,2560]{1,0:T(4,128)(2,1)S(1)}, bf16[4,2560]{1,0:T(4,128)(2,1)S(1)}, u32[]{:S(2)}, u32[]{:S(2)}) collective-permute-start(bf16[4,2560]{1,0:T(4,128)(2,1)S(1)} %slice_bitcast_fusion), channel_id=1, source_target_pairs={{3,6},{7,10},{11,14},{15,18},{19,22},{23,26},{27,30},{31,34},{35,3... | collective-permute-start | bytes 61448 | tf_op jit(solution)/shard_map/ppermute | solution.py:559
  2.8 19.0 %collective-permute-start.2 = (bf16[32,2560]{1,0:T(8,128)(2,1)}, bf16[32,2560]{1,0:T(8,128)(2,1)S(1)}, u32[]{:S(2)}, u32[]{:S(2)}) collective-permute-start(bf16[32,2560]{1,0:T(8,128)(2,1)} %bitcast.15), channel_id=1, source_target_pairs={{0,3},{1,0},{2,1},{3,2},{4,7},{5,4},{6,5},{7,6},{8,11},{9,8},{10,9... | collective-permute-start | bytes 491528 | tf_op jit(solution)/shard_map/ppermute | solution.py:520
  11.5 10.3 %collective-permute-start.1 = (bf16[32,2560]{1,0:T(8,128)(2,1)}, bf16[32,2560]{1,0:T(8,128)(2,1)S(1)}, u32[]{:S(2)}, u32[]{:S(2)}) collective-permute-start(bf16[32,2560]{1,0:T(8,128)(2,1)} %bitcast.16), channel_id=1, source_target_pairs={{0,2},{1,3},{2,0},{3,1},{4,6},{5,7},{6,4},{7,5},{8,10},{9,11},{10,... | collective-permute-start | bytes 491528 | tf_op jit(solution)/shard_map/ppermute | solution.py:520
  11.5 10.3 %collective-permute-start = (bf16[32,2560]{1,0:T(8,128)(2,1)}, bf16[32,2560]{1,0:T(8,128)(2,1)S(1)}, u32[]{:S(2)}, u32[]{:S(2)}) collective-permute-start(bf16[32,2560]{1,0:T(8,128)(2,1)} %bitcast.17), channel_id=1, source_target_pairs={{0,1},{1,2},{2,3},{3,0},{4,5},{5,6},{6,7},{7,4},{8,9},{9,10},{10,1... | collective-permute-start | bytes 491528 | tf_op jit(solution)/shard_map/ppermute | solution.py:520
  12.9 8.8 %collective-permute-start.3 = (bf16[4,2560]{1,0:T(4,128)(2,1)S(1)}, bf16[4,2560]{1,0:T(4,128)(2,1)S(1)}, u32[]{:S(2)}, u32[]{:S(2)}) collective-permute-start(bf16[4,2560]{1,0:T(4,128)(2,1)S(1)} %slice_bitcast_fusion), channel_id=1, source_target_pairs={{3,4},{7,8},{11,12},{15,16},{19,20},{23,24},{27,28},{31,32},{35,36... | collective-permute-start | bytes 61448 | tf_op jit(solution)/shard_map/ppermute | solution.py:559
  50.7 14.0 %all-to-all-start.1 = ((bf16[16,8,640]{2,1,0:T(8,128)(2,1)}), bf16[16,8,640]{2,1,0:T(8,128)(2,1)S(1)}, u32[]{:S(2)}, u32[]{:S(2)}) async-start(bf16[16,8,640]{2,1,0:T(8,128)(2,1)} %shard_map.132), calls=%async_computation.1 | async-start | bytes 327680 | tf_op jit(solution)/shard_map/all_to_all | solution.py:515
  57.1 15.4 %collective-permute-start.13 = (bf16[4,320,128]{2,1,0:T(8,128)(2,1)}, bf16[4,320,128]{2,1,0:T(8,128)(2,1)S(1)}, u32[]{:S(2)}, u32[]{:S(2)}) collective-permute-start(bf16[4,320,128]{2,1,0:T(8,128)(2,1)} %get-tuple-element.104), channel_id=1, source_target_pairs={{0,4},{4,0},{1,5},{5,1},{2,6},{6,2},{3,7},{7,3},{8,12},{12,8},{9,1... | collective-permute-start | bytes 983048 | tf_op jit(solution)/shard_map/ppermute | solution.py:520
  65.9 10.2 %collective-permute-start.8 = (bf16[128,640]{1,0:T(8,128)(2,1)S(1)}, bf16[128,640]{1,0:T(8,128)(2,1)S(1)}, u32[]{:S(2)}, u32[]{:S(2)}) collective-permute-start(bf16[128,640]{1,0:T(8,128)(2,1)S(1)} %get-tuple-element.73), channel_id=1, source_target_pairs={{0,4},{4,0},{1,5},{5,1},{2,6},{6,2},{3,7},{7,3},{8,12},{12,8},{9,1... | collective-permute-start | bytes 491528 | tf_op jit(solution)/shard_map/ppermute | solution.py:520
  74.2 18.7 %collective-permute-start.14 = (bf16[2,320,128]{2,1,0:T(8,128)(2,1)S(1)}, bf16[2,320,128]{2,1,0:T(8,128)(2,1)S(1)}, u32[]{:S(2)}, u32[]{:S(2)}) collective-permute-start(bf16[2,320,128]{2,1,0:T(8,128)(2,1)S(1)} %get-tuple-element.106), channel_id=1, source_target_pairs={{0,8},{8,128},{128,136},{136,0},{1,9},{9,129},{129,137},{137,1},{2... | collective-permute-start | bytes 491528 | tf_op jit(solution)/shard_map/ppermute | solution.py:520
  79.2 6.7 %collective-permute-start.9 = (f32[8,896]{1,0:T(8,128)S(1)}, f32[8,896]{1,0:T(8,128)S(1)}, u32[]{:S(2)}, u32[]{:S(2)}) collective-permute-start(f32[8,896]{1,0:T(8,128)S(1)} %get-tuple-element.93), channel_id=1, source_target_pairs={{4,0},{8,4},{12,8},{16,12},{20,16},{24,20},{28,24},{32,28},{36,32}... | collective-permute-start | bytes 86024 | tf_op jit(solution)/shard_map/ppermute | solution.py:648
  81.4 11.6 %collective-permute-start.15 = (bf16[2,320,128]{2,1,0:T(8,128)(2,1)S(1)}, bf16[2,320,128]{2,1,0:T(8,128)(2,1)S(1)}, u32[]{:S(2)}, u32[]{:S(2)}) collective-permute-start(bf16[2,320,128]{2,1,0:T(8,128)(2,1)S(1)} %get-tuple-element.107), channel_id=1, source_target_pairs={{0,128},{8,136},{128,0},{136,8},{1,129},{9,137},{129,1},{137,9},{2... | collective-permute-start | bytes 491528 | tf_op jit(solution)/shard_map/ppermute | solution.py:520
  86.4 11.2 %collective-permute-start.31 = (bf16[128,768]{1,0:T(8,128)(2,1)S(1)}, bf16[128,768]{1,0:T(8,128)(2,1)S(1)}, u32[]{:S(2)}, u32[]{:S(2)}) collective-permute-start(bf16[128,768]{1,0:T(8,128)(2,1)S(1)} %get-tuple-element.96.refs_1_.refs_4_), channel_id=1, source_target_pairs={{0,136},{8,0},{128,8},{136,128},{1,137},{9,1},{129,9},{137,129},{2... | collective-permute-start | bytes 589832 | tf_op jit(solution)/shard_map/ppermute | solution.py:520
  89.8 8.3 %collective-permute-start.29 = (bf16[128,768]{1,0:T(8,128)(2,1)S(1)}, bf16[128,768]{1,0:T(8,128)(2,1)S(1)}, u32[]{:S(2)}, u32[]{:S(2)}) collective-permute-start(bf16[128,768]{1,0:T(8,128)(2,1)S(1)} %get-tuple-element.96.refs_1_.refs_4_), channel_id=1, source_target_pairs={{0,128},{8,136},{128,0},{136,8},{1,129},{9,137},{129,1},{137,9},{2... | collective-permute-start | bytes 589832 | tf_op jit(solution)/shard_map/ppermute | solution.py:520
  89.9 9.3 %collective-permute-start.27 = (bf16[128,768]{1,0:T(8,128)(2,1)S(1)}, bf16[128,768]{1,0:T(8,128)(2,1)S(1)}, u32[]{:S(2)}, u32[]{:S(2)}) collective-permute-start(bf16[128,768]{1,0:T(8,128)(2,1)S(1)} %get-tuple-element.96.refs_1_.refs_4_), channel_id=1, source_target_pairs={{0,8},{8,128},{128,136},{136,0},{1,9},{9,129},{129,137},{137,1},{2... | collective-permute-start | bytes 589832 | tf_op jit(solution)/shard_map/ppermute | solution.py:520
  93.0 8.6 %collective-permute-start.16 = (bf16[2,320,128]{2,1,0:T(8,128)(2,1)S(1)}, bf16[2,320,128]{2,1,0:T(8,128)(2,1)S(1)}, u32[]{:S(2)}, u32[]{:S(2)}) collective-permute-start(bf16[2,320,128]{2,1,0:T(8,128)(2,1)S(1)} %get-tuple-element.108), channel_id=1, source_target_pairs={{0,136},{8,0},{128,8},{136,128},{1,137},{9,1},{129,9},{137,129},{2... | collective-permute-start | bytes 491528 | tf_op jit(solution)/shard_map/ppermute | solution.py:520
  97.6 15.9 %collective-permute-start.32 = (bf16[128,768]{1,0:T(8,128)(2,1)S(1)}, bf16[128,768]{1,0:T(8,128)(2,1)S(1)}, u32[]{:S(2)}, u32[]{:S(2)}) collective-permute-start(bf16[128,768]{1,0:T(8,128)(2,1)S(1)} %collective-permute-done.31.refs_10_), channel_id=1, source_target_pairs={{0,4},{4,0},{1,5},{5,1},{2,6},{6,2},{3,7},{7,3},{8,12},{12,8},{9,1... | collective-permute-start | bytes 589832 | tf_op jit(solution)/shard_map/ppermute | solution.py:520
  98.1 15.4 %collective-permute-start.30 = (bf16[128,768]{1,0:T(8,128)(2,1)S(1)}, bf16[128,768]{1,0:T(8,128)(2,1)S(1)}, u32[]{:S(2)}, u32[]{:S(2)}) collective-permute-start(bf16[128,768]{1,0:T(8,128)(2,1)S(1)} %collective-permute-done.29.refs_8_), channel_id=1, source_target_pairs={{0,4},{4,0},{1,5},{5,1},{2,6},{6,2},{3,7},{7,3},{8,12},{12,8},{9,1... | collective-permute-start | bytes 589832 | tf_op jit(solution)/shard_map/ppermute | solution.py:520
  99.2 14.9 %collective-permute-start.28 = (bf16[128,768]{1,0:T(8,128)(2,1)S(1)}, bf16[128,768]{1,0:T(8,128)(2,1)S(1)}, u32[]{:S(2)}, u32[]{:S(2)}) collective-permute-start(bf16[128,768]{1,0:T(8,128)(2,1)S(1)} %collective-permute-done.27.refs_6_), channel_id=1, source_target_pairs={{0,4},{4,0},{1,5},{5,1},{2,6},{6,2},{3,7},{7,3},{8,12},{12,8},{9,1... | collective-permute-start | bytes 589832 | tf_op jit(solution)/shard_map/ppermute | solution.py:520
  108.1 7.1 %collective-permute-start.19 = (bf16[128,256]{1,0:T(8,128)(2,1)S(1)}, bf16[128,256]{1,0:T(8,128)(2,1)S(1)}, u32[]{:S(2)}, u32[]{:S(2)}) collective-permute-start(bf16[128,256]{1,0:T(8,128)(2,1)S(1)} %shard_map.144.refs_5_), channel_id=1, source_target_pairs={{0,4},{4,0},{1,5},{5,1},{2,6},{6,2},{3,7},{7,3},{8,12},{12,8},{9,1... | collective-permute-start | bytes 196616 | tf_op jit(solution)/shard_map/ppermute | solution.py:520
  117.6 23.5 %all-to-all-start.2 = ((bf16[8,40,768]{2,1,0:T(8,128)(2,1)}), bf16[8,40,768]{2,1,0:T(8,128)(2,1)}, u32[]{:S(2)}, u32[]{:S(2)}) async-start(bf16[8,40,768]{2,1,0:T(8,128)(2,1)} %copy-done.2), calls=%async_computation.2 | async-start | bytes 983040 | tf_op jit(solution)/shard_map/all_to_all | solution.py:515
  127.9 7.3 %collective-permute-start.10 = (bf16[32,2560]{1,0:T(8,128)(2,1)}, bf16[32,2560]{1,0:T(8,128)(2,1)S(1)}, u32[]{:S(2)}, u32[]{:S(2)}) collective-permute-start(bf16[32,2560]{1,0:T(8,128)(2,1)} %get-tuple-element.99), channel_id=1, source_target_pairs={{0,2},{1,3},{2,0},{3,1},{4,6},{5,7},{6,4},{7,5},{8,10},{9,11},{10,... | collective-permute-start | bytes 491528 | tf_op jit(solution)/shard_map/ppermute | solution.py:520
  128.0 11.3 %collective-permute-start.11 = (bf16[32,2560]{1,0:T(8,128)(2,1)}, bf16[32,2560]{1,0:T(8,128)(2,1)S(1)}, u32[]{:S(2)}, u32[]{:S(2)}) collective-permute-start(bf16[32,2560]{1,0:T(8,128)(2,1)} %get-tuple-element.100), channel_id=1, source_target_pairs={{0,1},{1,2},{2,3},{3,0},{4,5},{5,6},{6,7},{7,4},{8,9},{9,10},{10,1... | collective-permute-start | bytes 491528 | tf_op jit(solution)/shard_map/ppermute | solution.py:520
  129.0 10.4 %collective-permute-start.12 = (bf16[32,2560]{1,0:T(8,128)(2,1)}, bf16[32,2560]{1,0:T(8,128)(2,1)S(1)}, u32[]{:S(2)}, u32[]{:S(2)}) collective-permute-start(bf16[32,2560]{1,0:T(8,128)(2,1)} %get-tuple-element.101), channel_id=1, source_target_pairs={{0,3},{1,0},{2,1},{3,2},{4,7},{5,4},{6,5},{7,6},{8,11},{9,8},{10,9... | collective-permute-start | bytes 491528 | tf_op jit(solution)/shard_map/ppermute | solution.py:520
  (24 other events, 235.0 us)

commit v6 on v4

--- a/solution.py
+++ b/solution.py
@@ -555,14 +555,15 @@
     for k in (1, 2, 3):
         arrived.append(turned(own, "chan", k))
     tail_rows = own[part - 4 :]
-    halos = [
-        lax.ppermute(
-            tail_rows,
-            SEQ_CHAN,
-            [(s * chans + chans - 1, (s + 1) * chans + k) for s in range(seq_count - 1)],
+    halos = []
+    for k in range(chans):
+        halos.append(
+            lax.ppermute(
+                tail_rows,
+                SEQ_CHAN,
+                [(s * chans + chans - 1, (s + 1) * chans + k) for s in range(seq_count - 1)],
+            )
         )
-        for k in range(chans)
-    ]
     sources = [
         own, inner_weight, mixer_weight, step_weight.T, conv_inner, conv_mixer, bias, rate, g
     ]

time: 144 us -> 144 us (level)
  no operation moved by 1% of the time
where the time goes in v6:
time: 144 us; the launch traced here: 143 us
  starting transfers between devices  46.5 us (32%)
  waiting for transfers between devices  36.5 us (25%)
  Pallas kernels  31.8 us (22%)
  blocking collectives  21.9 us (15%)
  local copies, waits for them, and re-layouts  5.31 us (4%)
    ppermute x26, starting transfers between devices, turned(): lax.ppermute(value, axis, [(k, (k + steps) % count) for k in range(count)])  32.9 us
    pallas_call x16, Pallas kernels, call(): pl.pallas_call(wrapped, out_shape=[pltpu.HBM(s, d) if k in stores else ja...  26.3 us
    all_to_all x1, blocking collectives, a2a(): return lax.all_to_all(value, axis, split_axis=0, concat_axis=0, tiled=True)  21.9 us
    ppermute x26, waiting for transfers between devices, turned(): lax.ppermute(value, axis, [(k, (k + steps) % count) for k in range(count)])  18.3 us
    all_to_all x2, starting transfers between devices, a2a(): return lax.all_to_all(value, axis, split_axis=0, concat_axis=0, tiled=True)  7.87 us
    pallas_call x3, Pallas kernels, fetch(): pl.pallas_call(kernel, out_shape=[jax.ShapeDtypeStruct(v.shape, v.dtype)...  5.42 us
    all_to_all x2, waiting for transfers between devices, a2a(): return lax.all_to_all(value, axis, split_axis=0, concat_axis=0, tiled=True)  5.39 us
    ppermute x4, waiting for transfers between devices, layer(): lax.ppermute(tail_rows, SEQ_CHAN, [(s * chans + chans - 1, (s + 1) * chan...  4.97 us
  transfers between devices with their start and end apart: 35, of which 11 were waited for; matrix products, arithmetic and copies ran while one was open for 0% of the time, Pallas kernels for 16%

profile of v6, /device:TPU:1, one launch (start us, length us, event | category | flops | bytes accessed | tf_op | source)
XLA Modules:
  0.0 143.3 jit_solution(2296672420193584656)
XLA Ops:
  2.8 8.7 %collective-permute-start.2 = (bf16[32,2560]{1,0:T(8,128)(2,1)}, bf16[32,2560]{1,0:T(8,128)(2,1)S(1)}, u32[]{:S(2)}, u32[]{:S(2)}) collective-permute-start(bf16[32,2560]{1,0:T(8,128)(2,1)} %bitcast.15), channel_id=1, source_target_pairs={{0,3},{1,0},{2,1},{3,2},{4,7},{5,4},{6,5},{7,6},{8,11},{9,8},{10,9... | collective-permute-start | bytes 491528 | tf_op jit(solution)/shard_map/ppermute | solution.py:520
  14.2 2.6 %shard_map.129 = (bf16[32,2560]{1,0:T(8,128)(2,1)S(1)}, bf16[2560,640]{1,0:T(8,128)(2,1)S(1)}, bf16[2560,256]{1,0:T(8,128)(2,1)S(1)}, bf16[10,2560]{1,0:T(8,128)...) custom-call(bf16[32,2560]{1,0:T(8,128)(2,1)} %bitcast.18, ...), custom_call_target="tpu_custom_call" | custom-call | flops 700000000 | bytes 4194304 | tf_op jit(solution)/shard_map/pallas_call | solution.py:122
  16.8 5.0 %collective-permute-done.3.refs_5_ = bf16[4,2560]{1,0:T(4,128)(2,1)S(1)} collective-permute-done((bf16[4,2560]{1,0:T(4,128)(2,1)S(1)}, bf16[4,2560]{1,0:T(4,128)(2,1)S(1)}, u32[]{:S(2)}, u32[]{:S(2)}) %collective-permute-start.3) | collective-permute-done | bytes 20512 | tf_op jit(solution)/shard_map/ppermute | solution.py:561
  21.8 3.8 %shard_map.130 = (bf16[128,2560]{1,0:T(8,128)(2,1)}, f32[128,1792]{1,0:T(8,128)}, bf16[128,1280]{1,0:T(8,128)(2,1)}, f32[5,128,10]{2,1,0:T(8,128)}, f32[2,10,128...) custom-call(s32[3]{0:T(128)S(1)} %pad_add_fusion.refs_0_, ...), custom_call_target="tpu_custom_call" | custom-call | flops 700000000 | bytes 1048576 | tf_op jit(solution)/shard_map/pallas_call | solution.py:88
  27.4 21.9 %all_to_all.15.refs_1_ = bf16[16,8,768]{2,1,0:T(8,128)(2,1)S(1)} all-to-all(bf16[16,8,768]{2,1,0:T(8,128)(2,1)S(1)} %shard_map.131), channel_id=1, replica_groups=mesh['dp'=2,'seq_0'=8,'seq_1'=2,'seq_2'=2,'chan'=4] {'seq_0','seq_1'}, dimensions={0} | all-to-all | bytes 393216 | tf_op jit(solution)/shard_map/all_to_all | solution.py:515
  50.7 3.5 %all-to-all-start.1 = ((bf16[16,8,640]{2,1,0:T(8,128)(2,1)}), bf16[16,8,640]{2,1,0:T(8,128)(2,1)S(1)}, u32[]{:S(2)}, u32[]{:S(2)}) async-start(bf16[16,8,640]{2,1,0:T(8,128)(2,1)} %shard_map.132), calls=%async_computation.1 | async-start | bytes 327680 | tf_op jit(solution)/shard_map/all_to_all | solution.py:515
  54.3 2.8 %shard_map.140 = (bf16[4,320,128]{2,1,0:T(8,128)(2,1)}, bf16[4,320,128]{2,1,0:T(8,128)(2,1)}) custom-call(s32[3]{0:T(128)S(1)} %pad_add_fusion.refs_0_, bf16[128,2560]{1,0:T(8,128)(2,1)} %get-tuple-element.102.refs_1_), custom_call_target="tpu_custom_call" | custom-call | flops 500000000 | bytes 1048576 | tf_op jit(solution)/shard_map/pallas_call | solution.py:88
  57.1 2.2 %collective-permute-start.13 = (bf16[4,320,128]{2,1,0:T(8,128)(2,1)}, bf16[4,320,128]{2,1,0:T(8,128)(2,1)S(1)}, u32[]{:S(2)}, u32[]{:S(2)}) collective-permute-start(bf16[4,320,128]{2,1,0:T(8,128)(2,1)} %get-tuple-element.104), channel_id=1, source_target_pairs={{0,4},{4,0},{1,5},{5,1},{2,6},{6,2},{3,7},{7,3},{8,12},{12,8},{9,1... | collective-permute-start | bytes 983048 | tf_op jit(solution)/shard_map/ppermute | solution.py:520
  59.3 5.4 %all-to-all-done.1.refs_1_ = bf16[16,8,640]{2,1,0:T(8,128)(2,1)S(1)} async-done(((bf16[16,8,640]{2,1,0:T(8,128)(2,1)}), bf16[16,8,640]{2,1,0:T(8,128)(2,1)S(1)}, u32[]{:S(2)}, u32[]{:S(2)}) %all-to-all-start.1) | async-done | bytes 163872 | tf_op jit(solution)/shard_map/all_to_all | solution.py:515
  65.9 3.4 %collective-permute-start.8 = (bf16[128,640]{1,0:T(8,128)(2,1)S(1)}, bf16[128,640]{1,0:T(8,128)(2,1)S(1)}, u32[]{:S(2)}, u32[]{:S(2)}) collective-permute-start(bf16[128,640]{1,0:T(8,128)(2,1)S(1)} %get-tuple-element.73), channel_id=1, source_target_pairs={{0,4},{4,0},{1,5},{5,1},{2,6},{6,2},{3,7},{7,3},{8,12},{12,8},{9,1... | collective-permute-start | bytes 491528 | tf_op jit(solution)/shard_map/ppermute | solution.py:520
  69.3 3.3 %shard_map.134 = (f32[128,896]{1,0:T(8,128)}, f32[128,10]{1,0:T(8,128)}, f32[10,128]{1,0:T(8,128)}) custom-call(f32[128,1792]{1,0:T(8,128)} %get-tuple-element.74.refs_0_, bf16[128,640]{1,0:T(8,128)(2,1)} %bitcast.20, f32[5,128,10]{2,1,0:T(8,128)} %get-tuple-element.76.refs_2_, f32[2,10,128]{2,1,0:T(8,128)} %get-tuple-element.77.refs_3_), custom_call_target="tpu_custom_call" | custom-call | flops 700000000 | bytes 1048576 | tf_op jit(solution)/shard_map/pallas_call | solution.py:88
  76.4 3.1 %shard_map.136 = (f32[128,896]{1,0:T(8,128)S(1)}, f32[8,896]{1,0:T(8,128)S(1)}, bf16[128,128]{1,0:T(8,128)(2,1)S(1)}, f32[4,896]{1,0:T(4,128)S(1)}) custom-call(s32[3]{0:T(128)S(1)} %pad_add_fusion.refs_0_, bf16[128,640]{1,0:T(8,128)(2,1)S(1)} %get-tuple-element.72.refs_11_.refs_1_, bf16[128,640]{1,0:T(8,128)(2,1)S(1)} %collective-permute-done.8.refs_2_, ...), custom_call_target="tpu_custom_call" | custom-call | flops 500000000 | bytes 1048576 | tf_op jit(solution)/shard_map/pallas_call | solution.py:88
  82.5 3.7 %collective-permute-done.9.refs_1_ = f32[8,896]{1,0:T(8,128)S(1)} collective-permute-done((f32[8,896]{1,0:T(8,128)S(1)}, f32[8,896]{1,0:T(8,128)S(1)}, u32[]{:S(2)}, u32[]{:S(2)}) %collective-permute-start.9) | collective-permute-done | bytes 28704 | tf_op jit(solution)/shard_map/ppermute | solution.py:649
  86.6 3.5 %collective-permute-start.31 = (bf16[128,768]{1,0:T(8,128)(2,1)S(1)}, bf16[128,768]{1,0:T(8,128)(2,1)S(1)}, u32[]{:S(2)}, u32[]{:S(2)}) collective-permute-start(bf16[128,768]{1,0:T(8,128)(2,1)S(1)} %get-tuple-element.96.refs_1_.refs_4_), channel_id=1, source_target_pairs={{0,136},{8,0},{128,8},{136,128},{1,137},{9,1},{129,9},{137,129},{2... | collective-permute-start | bytes 589832 | tf_op jit(solution)/shard_map/ppermute | solution.py:520
  90.1 3.0 %collective-permute-start.27 = (bf16[128,768]{1,0:T(8,128)(2,1)S(1)}, bf16[128,768]{1,0:T(8,128)(2,1)S(1)}, u32[]{:S(2)}, u32[]{:S(2)}) collective-permute-start(bf16[128,768]{1,0:T(8,128)(2,1)S(1)} %get-tuple-element.96.refs_1_.refs_4_), channel_id=1, source_target_pairs={{0,8},{8,128},{128,136},{136,0},{1,9},{9,129},{129,137},{137,1},{2... | collective-permute-start | bytes 589832 | tf_op jit(solution)/shard_map/ppermute | solution.py:520
  93.7 4.2 %collective-permute-done.18.refs_1_ = bf16[128,256]{1,0:T(8,128)(2,1)S(1)} collective-permute-done((bf16[128,256]{1,0:T(8,128)(2,1)S(1)}, bf16[128,256]{1,0:T(8,128)(2,1)S(1)}, u32[]{:S(2)}, u32[]{:S(2)}) %collective-permute-start.18) | collective-permute-done | bytes 65568 | tf_op jit(solution)/shard_map/ppermute | solution.py:660
  99.5 2.4 %collective-permute-done.16.refs_3_ = bf16[2,320,128]{2,1,0:T(8,128)(2,1)S(1)} collective-permute-done((bf16[2,320,128]{2,1,0:T(8,128)(2,1)S(1)}, bf16[2,320,128]{2,1,0:T(8,128)(2,1)S(1)}, u32[]{:S(2)}, u32[]{:S(2)}) %collective-permute-start.16) | collective-permute-done | bytes 163872 | tf_op jit(solution)/shard_map/ppermute | solution.py:520
  103.5 3.6 %collective-permute-done.24.refs_11_ = bf16[128,256]{1,0:T(8,128)(2,1)S(1)} collective-permute-done((bf16[128,256]{1,0:T(8,128)(2,1)S(1)}, bf16[128,256]{1,0:T(8,128)(2,1)S(1)}, u32[]{:S(2)}, u32[]{:S(2)}) %collective-permute-start.24) | collective-permute-done | bytes 65568 | tf_op jit(solution)/shard_map/ppermute | solution.py:520
  111.4 2.3 %collective-permute-start.25 = (bf16[128,256]{1,0:T(8,128)(2,1)S(1)}, bf16[128,256]{1,0:T(8,128)(2,1)S(1)}, u32[]{:S(2)}, u32[]{:S(2)}) collective-permute-start(bf16[128,256]{1,0:T(8,128)(2,1)S(1)} %collective-permute-done.24.refs_11_), channel_id=1, source_target_pairs={{0,4},{4,0},{1,5},{5,1},{2,6},{6,2},{3,7},{7,3},{8,12},{12,8},{9,1... | collective-permute-start | bytes 196616 | tf_op jit(solution)/shard_map/ppermute | solution.py:520
  117.8 4.3 %all-to-all-start.2 = ((bf16[8,40,768]{2,1,0:T(8,128)(2,1)}), bf16[8,40,768]{2,1,0:T(8,128)(2,1)}, u32[]{:S(2)}, u32[]{:S(2)}) async-start(bf16[8,40,768]{2,1,0:T(8,128)(2,1)} %copy-done.2), calls=%async_computation.2 | async-start | bytes 983040 | tf_op jit(solution)/shard_map/all_to_all | solution.py:515
  125.0 3.1 %shard_map.138 = (bf16[32,2560]{1,0:T(8,128)(2,1)}, bf16[32,2560]{1,0:T(8,128)(2,1)}, bf16[32,2560]{1,0:T(8,128)(2,1)}, bf16[32,2560]{1,0:T(8,128)(2,1)}) custom-call(s32[3]{0:T(128)S(1)} %copy-done.9, bf16[128,768]{1,0:T(8,128)(2,1)S(1)} %get-tuple-element.96.refs_1_.refs_4_, bf16[128,256]{1,0:T(8,128)(2,1)S(1)} %copy-done.5, ...), custom_call_target="tpu_custom_call" | custom-call | flops 500000000 | bytes 1048576 | tf_op jit(solution)/shard_map/pallas_call | solution.py:88
  129.2 2.3 %collective-permute-start.12 = (bf16[32,2560]{1,0:T(8,128)(2,1)}, bf16[32,2560]{1,0:T(8,128)(2,1)S(1)}, u32[]{:S(2)}, u32[]{:S(2)}) collective-permute-start(bf16[32,2560]{1,0:T(8,128)(2,1)} %get-tuple-element.101), channel_id=1, source_target_pairs={{0,3},{1,0},{2,1},{3,2},{4,7},{5,4},{6,5},{7,6},{8,11},{9,8},{10,9... | collective-permute-start | bytes 491528 | tf_op jit(solution)/shard_map/ppermute | solution.py:520
  131.5 3.9 %collective-permute-done.10.refs_1_ = bf16[32,2560]{1,0:T(8,128)(2,1)S(1)} collective-permute-done((bf16[32,2560]{1,0:T(8,128)(2,1)}, bf16[32,2560]{1,0:T(8,128)(2,1)S(1)}, u32[]{:S(2)}, u32[]{:S(2)}) %collective-permute-start.10) | collective-permute-done | bytes 163872 | tf_op jit(solution)/shard_map/ppermute | solution.py:520
  135.4 4.2 %collective-permute-done.11.refs_2_ = bf16[32,2560]{1,0:T(8,128)(2,1)S(1)} collective-permute-done((bf16[32,2560]{1,0:T(8,128)(2,1)}, bf16[32,2560]{1,0:T(8,128)(2,1)S(1)}, u32[]{:S(2)}, u32[]{:S(2)}) %collective-permute-start.11) | collective-permute-done | bytes 163872 | tf_op jit(solution)/shard_map/ppermute | solution.py:520
  (94 shorter events, 35.9 us)
Async XLA Ops:
  1.4 10.8 %collective-permute-start.6 = (bf16[4,2560]{1,0:T(4,128)(2,1)S(1)}, bf16[4,2560]{1,0:T(4,128)(2,1)S(1)}, u32[]{:S(2)}, u32[]{:S(2)}) collective-permute-start(bf16[4,2560]{1,0:T(4,128)(2,1)S(1)} %slice_bitcast_fusion), channel_id=1, source_target_pairs={{3,7},{7,11},{11,15},{15,19},{19,23},{23,27},{27,31},{31,35},{35,3... | collective-permute-start | bytes 61448 | tf_op jit(solution)/shard_map/ppermute | solution.py:561
  2.1 10.8 %collective-permute-start.5 = (bf16[4,2560]{1,0:T(4,128)(2,1)S(1)}, bf16[4,2560]{1,0:T(4,128)(2,1)S(1)}, u32[]{:S(2)}, u32[]{:S(2)}) collective-permute-start(bf16[4,2560]{1,0:T(4,128)(2,1)S(1)} %slice_bitcast_fusion), channel_id=1, source_target_pairs={{3,6},{7,10},{11,14},{15,18},{19,22},{23,26},{27,30},{31,34},{35,3... | collective-permute-start | bytes 61448 | tf_op jit(solution)/shard_map/ppermute | solution.py:561
  2.8 19.0 %collective-permute-start.2 = (bf16[32,2560]{1,0:T(8,128)(2,1)}, bf16[32,2560]{1,0:T(8,128)(2,1)S(1)}, u32[]{:S(2)}, u32[]{:S(2)}) collective-permute-start(bf16[32,2560]{1,0:T(8,128)(2,1)} %bitcast.15), channel_id=1, source_target_pairs={{0,3},{1,0},{2,1},{3,2},{4,7},{5,4},{6,5},{7,6},{8,11},{9,8},{10,9... | collective-permute-start | bytes 491528 | tf_op jit(solution)/shard_map/ppermute | solution.py:520
  11.5 10.3 %collective-permute-start.1 = (bf16[32,2560]{1,0:T(8,128)(2,1)}, bf16[32,2560]{1,0:T(8,128)(2,1)S(1)}, u32[]{:S(2)}, u32[]{:S(2)}) collective-permute-start(bf16[32,2560]{1,0:T(8,128)(2,1)} %bitcast.16), channel_id=1, source_target_pairs={{0,2},{1,3},{2,0},{3,1},{4,6},{5,7},{6,4},{7,5},{8,10},{9,11},{10,... | collective-permute-start | bytes 491528 | tf_op jit(solution)/shard_map/ppermute | solution.py:520
  11.5 10.3 %collective-permute-start = (bf16[32,2560]{1,0:T(8,128)(2,1)}, bf16[32,2560]{1,0:T(8,128)(2,1)S(1)}, u32[]{:S(2)}, u32[]{:S(2)}) collective-permute-start(bf16[32,2560]{1,0:T(8,128)(2,1)} %bitcast.17), channel_id=1, source_target_pairs={{0,1},{1,2},{2,3},{3,0},{4,5},{5,6},{6,7},{7,4},{8,9},{9,10},{10,1... | collective-permute-start | bytes 491528 | tf_op jit(solution)/shard_map/ppermute | solution.py:520
  12.9 8.8 %collective-permute-start.3 = (bf16[4,2560]{1,0:T(4,128)(2,1)S(1)}, bf16[4,2560]{1,0:T(4,128)(2,1)S(1)}, u32[]{:S(2)}, u32[]{:S(2)}) collective-permute-start(bf16[4,2560]{1,0:T(4,128)(2,1)S(1)} %slice_bitcast_fusion), channel_id=1, source_target_pairs={{3,4},{7,8},{11,12},{15,16},{19,20},{23,24},{27,28},{31,32},{35,36... | collective-permute-start | bytes 61448 | tf_op jit(solution)/shard_map/ppermute | solution.py:561
  50.7 14.0 %all-to-all-start.1 = ((bf16[16,8,640]{2,1,0:T(8,128)(2,1)}), bf16[16,8,640]{2,1,0:T(8,128)(2,1)S(1)}, u32[]{:S(2)}, u32[]{:S(2)}) async-start(bf16[16,8,640]{2,1,0:T(8,128)(2,1)} %shard_map.132), calls=%async_computation.1 | async-start | bytes 327680 | tf_op jit(solution)/shard_map/all_to_all | solution.py:515
  57.1 15.6 %collective-permute-start.13 = (bf16[4,320,128]{2,1,0:T(8,128)(2,1)}, bf16[4,320,128]{2,1,0:T(8,128)(2,1)S(1)}, u32[]{:S(2)}, u32[]{:S(2)}) collective-permute-start(bf16[4,320,128]{2,1,0:T(8,128)(2,1)} %get-tuple-element.104), channel_id=1, source_target_pairs={{0,4},{4,0},{1,5},{5,1},{2,6},{6,2},{3,7},{7,3},{8,12},{12,8},{9,1... | collective-permute-start | bytes 983048 | tf_op jit(solution)/shard_map/ppermute | solution.py:520
  65.9 10.4 %collective-permute-start.8 = (bf16[128,640]{1,0:T(8,128)(2,1)S(1)}, bf16[128,640]{1,0:T(8,128)(2,1)S(1)}, u32[]{:S(2)}, u32[]{:S(2)}) collective-permute-start(bf16[128,640]{1,0:T(8,128)(2,1)S(1)} %get-tuple-element.73), channel_id=1, source_target_pairs={{0,4},{4,0},{1,5},{5,1},{2,6},{6,2},{3,7},{7,3},{8,12},{12,8},{9,1... | collective-permute-start | bytes 491528 | tf_op jit(solution)/shard_map/ppermute | solution.py:520
  74.3 18.8 %collective-permute-start.14 = (bf16[2,320,128]{2,1,0:T(8,128)(2,1)S(1)}, bf16[2,320,128]{2,1,0:T(8,128)(2,1)S(1)}, u32[]{:S(2)}, u32[]{:S(2)}) collective-permute-start(bf16[2,320,128]{2,1,0:T(8,128)(2,1)S(1)} %get-tuple-element.106), channel_id=1, source_target_pairs={{0,8},{8,128},{128,136},{136,0},{1,9},{9,129},{129,137},{137,1},{2... | collective-permute-start | bytes 491528 | tf_op jit(solution)/shard_map/ppermute | solution.py:520
  79.4 6.7 %collective-permute-start.9 = (f32[8,896]{1,0:T(8,128)S(1)}, f32[8,896]{1,0:T(8,128)S(1)}, u32[]{:S(2)}, u32[]{:S(2)}) collective-permute-start(f32[8,896]{1,0:T(8,128)S(1)} %get-tuple-element.93), channel_id=1, source_target_pairs={{4,0},{8,4},{12,8},{16,12},{20,16},{24,20},{28,24},{32,28},{36,32}... | collective-permute-start | bytes 86024 | tf_op jit(solution)/shard_map/ppermute | solution.py:649
  81.6 11.6 %collective-permute-start.15 = (bf16[2,320,128]{2,1,0:T(8,128)(2,1)S(1)}, bf16[2,320,128]{2,1,0:T(8,128)(2,1)S(1)}, u32[]{:S(2)}, u32[]{:S(2)}) collective-permute-start(bf16[2,320,128]{2,1,0:T(8,128)(2,1)S(1)} %get-tuple-element.107), channel_id=1, source_target_pairs={{0,128},{8,136},{128,0},{136,8},{1,129},{9,137},{129,1},{137,9},{2... | collective-permute-start | bytes 491528 | tf_op jit(solution)/shard_map/ppermute | solution.py:520
  86.6 11.2 %collective-permute-start.31 = (bf16[128,768]{1,0:T(8,128)(2,1)S(1)}, bf16[128,768]{1,0:T(8,128)(2,1)S(1)}, u32[]{:S(2)}, u32[]{:S(2)}) collective-permute-start(bf16[128,768]{1,0:T(8,128)(2,1)S(1)} %get-tuple-element.96.refs_1_.refs_4_), channel_id=1, source_target_pairs={{0,136},{8,0},{128,8},{136,128},{1,137},{9,1},{129,9},{137,129},{2... | collective-permute-start | bytes 589832 | tf_op jit(solution)/shard_map/ppermute | solution.py:520
  90.1 8.3 %collective-permute-start.29 = (bf16[128,768]{1,0:T(8,128)(2,1)S(1)}, bf16[128,768]{1,0:T(8,128)(2,1)S(1)}, u32[]{:S(2)}, u32[]{:S(2)}) collective-permute-start(bf16[128,768]{1,0:T(8,128)(2,1)S(1)} %get-tuple-element.96.refs_1_.refs_4_), channel_id=1, source_target_pairs={{0,128},{8,136},{128,0},{136,8},{1,129},{9,137},{129,1},{137,9},{2... | collective-permute-start | bytes 589832 | tf_op jit(solution)/shard_map/ppermute | solution.py:520
  90.1 9.3 %collective-permute-start.27 = (bf16[128,768]{1,0:T(8,128)(2,1)S(1)}, bf16[128,768]{1,0:T(8,128)(2,1)S(1)}, u32[]{:S(2)}, u32[]{:S(2)}) collective-permute-start(bf16[128,768]{1,0:T(8,128)(2,1)S(1)} %get-tuple-element.96.refs_1_.refs_4_), channel_id=1, source_target_pairs={{0,8},{8,128},{128,136},{136,0},{1,9},{9,129},{129,137},{137,1},{2... | collective-permute-start | bytes 589832 | tf_op jit(solution)/shard_map/ppermute | solution.py:520
  93.3 8.6 %collective-permute-start.16 = (bf16[2,320,128]{2,1,0:T(8,128)(2,1)S(1)}, bf16[2,320,128]{2,1,0:T(8,128)(2,1)S(1)}, u32[]{:S(2)}, u32[]{:S(2)}) collective-permute-start(bf16[2,320,128]{2,1,0:T(8,128)(2,1)S(1)} %get-tuple-element.108), channel_id=1, source_target_pairs={{0,136},{8,0},{128,8},{136,128},{1,137},{9,1},{129,9},{137,129},{2... | collective-permute-start | bytes 491528 | tf_op jit(solution)/shard_map/ppermute | solution.py:520
  97.8 15.9 %collective-permute-start.32 = (bf16[128,768]{1,0:T(8,128)(2,1)S(1)}, bf16[128,768]{1,0:T(8,128)(2,1)S(1)}, u32[]{:S(2)}, u32[]{:S(2)}) collective-permute-start(bf16[128,768]{1,0:T(8,128)(2,1)S(1)} %collective-permute-done.31.refs_10_), channel_id=1, source_target_pairs={{0,4},{4,0},{1,5},{5,1},{2,6},{6,2},{3,7},{7,3},{8,12},{12,8},{9,1... | collective-permute-start | bytes 589832 | tf_op jit(solution)/shard_map/ppermute | solution.py:520
  98.4 15.4 %collective-permute-start.30 = (bf16[128,768]{1,0:T(8,128)(2,1)S(1)}, bf16[128,768]{1,0:T(8,128)(2,1)S(1)}, u32[]{:S(2)}, u32[]{:S(2)}) collective-permute-start(bf16[128,768]{1,0:T(8,128)(2,1)S(1)} %collective-permute-done.29.refs_8_), channel_id=1, source_target_pairs={{0,4},{4,0},{1,5},{5,1},{2,6},{6,2},{3,7},{7,3},{8,12},{12,8},{9,1... | collective-permute-start | bytes 589832 | tf_op jit(solution)/shard_map/ppermute | solution.py:520
  99.4 14.9 %collective-permute-start.28 = (bf16[128,768]{1,0:T(8,128)(2,1)S(1)}, bf16[128,768]{1,0:T(8,128)(2,1)S(1)}, u32[]{:S(2)}, u32[]{:S(2)}) collective-permute-start(bf16[128,768]{1,0:T(8,128)(2,1)S(1)} %collective-permute-done.27.refs_6_), channel_id=1, source_target_pairs={{0,4},{4,0},{1,5},{5,1},{2,6},{6,2},{3,7},{7,3},{8,12},{12,8},{9,1... | collective-permute-start | bytes 589832 | tf_op jit(solution)/shard_map/ppermute | solution.py:520
  108.4 7.1 %collective-permute-start.19 = (bf16[128,256]{1,0:T(8,128)(2,1)S(1)}, bf16[128,256]{1,0:T(8,128)(2,1)S(1)}, u32[]{:S(2)}, u32[]{:S(2)}) collective-permute-start(bf16[128,256]{1,0:T(8,128)(2,1)S(1)} %shard_map.144.refs_5_), channel_id=1, source_target_pairs={{0,4},{4,0},{1,5},{5,1},{2,6},{6,2},{3,7},{7,3},{8,12},{12,8},{9,1... | collective-permute-start | bytes 196616 | tf_op jit(solution)/shard_map/ppermute | solution.py:520
  117.8 23.5 %all-to-all-start.2 = ((bf16[8,40,768]{2,1,0:T(8,128)(2,1)}), bf16[8,40,768]{2,1,0:T(8,128)(2,1)}, u32[]{:S(2)}, u32[]{:S(2)}) async-start(bf16[8,40,768]{2,1,0:T(8,128)(2,1)} %copy-done.2), calls=%async_computation.2 | async-start | bytes 983040 | tf_op jit(solution)/shard_map/all_to_all | solution.py:515
  128.1 7.3 %collective-permute-start.10 = (bf16[32,2560]{1,0:T(8,128)(2,1)}, bf16[32,2560]{1,0:T(8,128)(2,1)S(1)}, u32[]{:S(2)}, u32[]{:S(2)}) collective-permute-start(bf16[32,2560]{1,0:T(8,128)(2,1)} %get-tuple-element.99), channel_id=1, source_target_pairs={{0,2},{1,3},{2,0},{3,1},{4,6},{5,7},{6,4},{7,5},{8,10},{9,11},{10,... | collective-permute-start | bytes 491528 | tf_op jit(solution)/shard_map/ppermute | solution.py:520
  128.2 11.3 %collective-permute-start.11 = (bf16[32,2560]{1,0:T(8,128)(2,1)}, bf16[32,2560]{1,0:T(8,128)(2,1)S(1)}, u32[]{:S(2)}, u32[]{:S(2)}) collective-permute-start(bf16[32,2560]{1,0:T(8,128)(2,1)} %get-tuple-element.100), channel_id=1, source_target_pairs={{0,1},{1,2},{2,3},{3,0},{4,5},{5,6},{6,7},{7,4},{8,9},{9,10},{10,1... | collective-permute-start | bytes 491528 | tf_op jit(solution)/shard_map/ppermute | solution.py:520
  129.2 10.4 %collective-permute-start.12 = (bf16[32,2560]{1,0:T(8,128)(2,1)}, bf16[32,2560]{1,0:T(8,128)(2,1)S(1)}, u32[]{:S(2)}, u32[]{:S(2)}) collective-permute-start(bf16[32,2560]{1,0:T(8,128)(2,1)} %get-tuple-element.101), channel_id=1, source_target_pairs={{0,3},{1,0},{2,1},{3,2},{4,7},{5,4},{6,5},{7,6},{8,11},{9,8},{10,9... | collective-permute-start | bytes 491528 | tf_op jit(solution)/shard_map/ppermute | solution.py:520
  (24 other events, 235.2 us)
